TPU v7x, 32 devices: a whole 2x2x4 slice. The times are simulated.
32 devices in a mesh: seq: 4 (over z), fsdp: 8 (over y, x, core).
Axes of the slice: x: 2, y: 2, z: 4, core: 2. Of those that a mesh axis runs over, the one named last changes fastest.
Arguments:
- tokens: bfloat16 [8, 1024, 1536], P('fsdp', 'seq'), may hold values from -6 to 6
- teacher: bfloat16 [8, 1024, 1536], P('fsdp', 'seq'), may hold values from -6 to 6
- valid_mask: int32 [8, 1024], P('fsdp', 'seq'), may hold values 0 or 1
- segment_ids: int32 [8, 1024], P('fsdp'), may hold values from 0 to 11, never falling along the last dimension, each value on 1 to 512 neighbouring positions
- routes: int32 [8, 1024, 6], P('fsdp', 'seq'), may hold values from 0 to 31, all different within a row; in each aligned block of 256 rows (0 to 255, 256 to 511, ..., all dimensions but the last counted through in order) at most 64 rows name the same one
- gate_weights: float32 [8, 1024, 6], P('fsdp', 'seq'), may hold values from 0.1 to 0.4
- norm1_gain: bfloat16 [1536], P(('seq', 'fsdp')), may hold values from 0.5 to 1.5
- query_weight: bfloat16 [1536, 1536], P(('seq', 'fsdp')), may hold values from -0.15625 to 0.15625
- key_weight: bfloat16 [1536, 512], P(('seq', 'fsdp')), may hold values from -0.15625 to 0.15625
- value_weight: bfloat16 [1536, 512], P(('seq', 'fsdp')), may hold values from -0.15625 to 0.15625
- output_weight: bfloat16 [1536, 1536], P(('seq', 'fsdp')), may hold values from -0.625 to 0.625
- norm2_gain: bfloat16 [1536], P(('seq', 'fsdp')), may hold values from 0.5 to 1.5
- shared_gate_weight: bfloat16 [1536, 1024], P(('seq', 'fsdp')), may hold values from -0.15625 to 0.15625
- shared_up_weight: bfloat16 [1536, 1024], P(('seq', 'fsdp')), may hold values from -0.15625 to 0.15625
- shared_down_weight: bfloat16 [1024, 1536], P(('seq', 'fsdp')), may hold values from -0.1875 to 0.1875
- expert_gate_weight: bfloat16 [32, 1536, 512], P('fsdp', 'seq'), may hold values from -0.15625 to 0.15625
- expert_up_weight: bfloat16 [32, 1536, 512], P('fsdp', 'seq'), may hold values from -0.15625 to 0.15625
- expert_down_weight: bfloat16 [32, 512, 1536], P('fsdp', 'seq'), may hold values from -0.25 to 0.25
Outputs:
- block_output: bfloat16 [8, 1024, 1536], P('fsdp', 'seq')
- grad_tokens: float32 [8, 1024, 1536], P('fsdp', 'seq')
- grad_norm1_gain: float32 [1536], P(('seq', 'fsdp'))
- grad_query_weight: float32 [1536, 1536], P(('seq', 'fsdp'))
- grad_key_weight: float32 [1536, 512], P(('seq', 'fsdp'))
- grad_value_weight: float32 [1536, 512], P(('seq', 'fsdp'))
- grad_output_weight: float32 [1536, 1536], P(('seq', 'fsdp'))
- grad_norm2_gain: float32 [1536], P(('seq', 'fsdp'))
- grad_shared_gate_weight: float32 [1536, 1024], P(('seq', 'fsdp'))
- grad_shared_up_weight: float32 [1536, 1024], P(('seq', 'fsdp'))
- grad_shared_down_weight: float32 [1024, 1536], P(('seq', 'fsdp'))
- grad_expert_gate_weight: float32 [32, 1536, 512], P('fsdp', 'seq')
- grad_expert_up_weight: float32 [32, 1536, 512], P('fsdp', 'seq')
- grad_expert_down_weight: float32 [32, 512, 1536], P('fsdp', 'seq')
Inputs may be any that keep to these rules, and one draw needn't show every extreme that they name: `segment_ids`: document numbers never fall along a sequence; a document has 1 to 512 tokens, and some document has exactly 512. `routes`: the 6 experts of a token differ; among the 256 tokens of one device no expert is named by more than 64 choices, and in some device's tokens one expert is named by exactly 64.
All inputs are finite; a program needn't handle non-finite values. No bound on the sum of `valid_mask` on one device may be relied on, other than what follows from the above.
Results may differ from a plain program's by a relative error of at most 0.015.
Values may be sent and summed in bfloat16 or wider, within the bound.
A program may use at most 256 MiB of HBM per device.

v0:
```python
import functools
import math

import jax
import jax.numpy as jnp
from jax import lax
from jax.experimental import pallas as pl
from jax.experimental.pallas import tpu as pltpu
from jax.sharding import PartitionSpec as P


HEADS = 12
KV_HEADS = 4
HEAD = 128
TOP = 6
EPSILON = 1e-05
MASKED = -1e30
PAIR = 2


BF16 = jnp.bfloat16
F32 = jnp.float32


def exchange(values, axis, bit):
    count = lax.axis_size(axis)
    return lax.ppermute(values, axis, [(i, i ^ bit) for i in range(count)])


def shift(values, axis, step):
    count = lax.axis_size(axis)
    pairs = [(i, i + step) for i in range(count) if 0 <= i + step < count]
    return lax.ppermute(values, axis, pairs)


def after(values, *others):
    return lax.optimization_barrier((values, *others))[0]


def dot(left, right, left_dim, right_dim):
    return lax.dot_general(
        left, right, (((left_dim,), (right_dim,)), ((), ())), preferred_element_type=F32
    )


def batch_dot(left, right, left_dim, right_dim):
    return lax.dot_general(
        left, right, (((left_dim,), (right_dim,)), ((0,), (0,))), preferred_element_type=F32
    )


def rms_norm(values, gain):
    factor = lax.rsqrt(jnp.mean(values * values, axis=-1, keepdims=True) + EPSILON)
    return values * factor * gain


def swiglu(gate_rows, up_rows):
    return jax.nn.silu(gate_rows) * up_rows


def swiglu_backward(gate_rows, up_rows, grad_rows):
    _, pull_back = jax.vjp(swiglu, gate_rows, up_rows)
    grad_gate, grad_up = pull_back(grad_rows)
    return (grad_gate.astype(BF16), grad_up.astype(BF16))


MESH = pl.DeviceIdType.MESH


def grant(scratch, extra):
    size = extra
    for ref in scratch:
        shape = list(ref.shape)
        shape[-2] = -(-shape[-2] // 16) * 16
        size += math.prod(shape) * jnp.dtype(ref.dtype).itemsize
    return min(size + 6 * 2**20, 66 * 10**6)


class Copies:
    def __init__(self, send_sems, recv_sems):
        self.send_sems, self.recv_sems, self.made = send_sems, recv_sems, []

    def start(self, source, target, axis, partner):
        number = len(self.made)
        copy = pltpu.make_async_remote_copy(
            src_ref=source,
            dst_ref=target,
            send_sem=self.send_sems.at[number],
            recv_sem=self.recv_sems.at[number],
            device_id={axis: partner},
            device_id_type=MESH,
        )
        copy.start()
        self.made.append(copy)
        return copy

    def finish(self):
        for copy in self.made:
            copy.wait_send()


def greet(partners):
    barrier = pltpu.get_barrier_semaphore()
    for axis, partner in partners:
        pl.semaphore_signal(barrier, inc=1, device_id={axis: partner}, device_id_type=MESH)
    pl.semaphore_wait(barrier, len(partners))


def bit_of(index, bit):
    return lax.rem(lax.div(index, bit), 2)


def flip(index, bit):
    return index + bit - 2 * bit * bit_of(index, bit)


def flip_all(index, mask):
    bit = 1
    while bit <= mask:
        if mask & bit:
            index = flip(index, bit)
        bit *= 2
    return index


def gather_dense_kernel(length, bits, count, *refs):
    shards, expert, outs, expert_full = refs[:count], refs[count], refs[count + 1 : 2 * count + 1], refs[2 * count + 1]
    send_sems, recv_sems, local_sems = refs[2 * count + 2 :]
    seq, group = lax.axis_index("seq"), lax.axis_index("fsdp")
    own = [bit_of(group, bit) for bit in bits]
    partners = [("seq", flip_all(seq, k)) for k in range(1, length)]
    partners += [("fsdp", flip(group, bit)) for bit in bits]
    greet(partners)
    copies = Copies(send_sems, recv_sems)
    far = len(bits) - 1
    half = length // 2
    side = lax.div(seq, half)
    low = [side * half, (1 - side) * half]
    orders = [list(range(far)), list(range(far))[::-1]]
    stages = far + 2
    waiting = [None] * count

    def launch(t, stage):
        if stage == 0:
            local = pltpu.make_async_copy(shards[t], outs[t].at[(seq, *own)], local_sems.at[t])
            local.start()
            made = [
                copies.start(shards[t], outs[t].at[(seq, *own)], "seq", flip_all(seq, k))
                for k in range(1, length)
            ]
            return made, local
        made = []
        for part in (0, 1):
            where = [pl.ds(low[part], half)] + list(own)
            for done in orders[part][: stage - 1]:
                where[1 + done] = slice(None)
            dim = orders[part][stage - 1] if stage <= far else far
            view = outs[t].at[tuple(where)]
            made.append(copies.start(view, view, "fsdp", flip(group, bits[dim])))
        return made, None

    def ship_expert():
        held, depth = expert.shape[0] // PAIR, expert.shape[1]
        rows = pl.ds(pl.multiple_of(seq * depth, depth), depth)
        parity = lax.rem(seq, PAIR)
        local = pltpu.make_async_copy(
            expert.at[pl.ds(parity * held, held)], expert_full.at[:, rows], local_sems.at[count]
        )
        local.start()
        made = []
        for k in range(1, length):
            other = lax.rem(parity + k, PAIR)
            made.append(
                copies.start(
                    expert.at[pl.ds(other * held, held)], expert_full.at[:, rows], "seq", flip_all(seq, k)
                )
            )
        return made, local

    for step in range(count + stages):
        if step == count:
            expert_waiting = ship_expert()
        for t in range(count):
            stage = step - t
            if 0 < stage <= stages and waiting[t]:
                made, local = waiting[t]
                for copy in made:
                    copy.wait_recv()
                if local is not None:
                    local.wait()
                waiting[t] = None
            if 0 <= stage < stages:
                waiting[t] = launch(t, stage)
    made, local = expert_waiting
    for copy in made:
        copy.wait_recv()
    local.wait()
    copies.finish()


def gather_dense(shards, expert):
    length, groups = lax.axis_size("seq"), lax.axis_size("fsdp")
    bits, bit = [], groups // 2
    while bit >= 1:
        bits.append(bit)
        bit //= 2
    count = len(shards)
    number = count * (length - 1 + 2 * len(bits)) + length - 1
    size = sum(s.size * s.dtype.itemsize for s in shards) * length * groups
    experts, depth, wide = expert.shape
    *outs, expert_full = pl.pallas_call(
        functools.partial(gather_dense_kernel, length, bits, count),
        out_shape=[
            jax.ShapeDtypeStruct((length,) + (2,) * len(bits) + s.shape, s.dtype) for s in shards
        ]
        + [jax.ShapeDtypeStruct((experts // PAIR, length * depth, wide), expert.dtype)],
        in_specs=[pl.BlockSpec(memory_space=pltpu.VMEM)] * count + [pl.BlockSpec(memory_space=pl.ANY)],
        out_specs=[pl.BlockSpec(memory_space=pl.ANY)] * (count + 1),
        scratch_shapes=[
            pltpu.SemaphoreType.DMA((number,)),
            pltpu.SemaphoreType.DMA((number,)),
            pltpu.SemaphoreType.DMA((count + 1,)),
        ],
        compiler_params=pltpu.CompilerParams(
            collective_id=0, has_side_effects=True, vmem_limit_bytes=16 * 2**20
        ),
        cost_estimate=pl.CostEstimate(flops=0, bytes_accessed=3 * size, transcendentals=0),
        name="gather_dense",
    )(*shards, expert)
    return [out.reshape(-1, out.shape[-1]) for out in outs] + [expert_full]


def scatter_dense_kernel(length, bits, count, *refs):
    grads, outs = refs[:count], refs[count : 2 * count]
    far = len(bits) - 1
    per = 3 + far
    scratch = refs[2 * count : 2 * count + per * count]
    send_sems, recv_sems, local_sems = refs[2 * count + per * count :]
    seq, group = lax.axis_index("seq"), lax.axis_index("fsdp")
    own = [bit_of(group, bit) for bit in bits]
    partners = [("seq", flip_all(seq, k)) for k in range(1, length)]
    partners += [("fsdp", flip(group, bit)) for bit in bits]
    greet(partners)
    copies = Copies(send_sems, recv_sems)
    half = length // 2
    side = lax.div(seq, half)
    low = [side * half, (1 - side) * half]
    orders = [list(range(far))[::-1], list(range(far))]
    stages = far + 2
    everything = (slice(None),) * (1 + far)

    def buffers(t):
        held = scratch[per * t : per * (t + 1)]
        return held[0], held[1], held[2 : 2 + far], held[2 + far]

    waiting = [None] * count

    def add(mine, came, lead, fixed, inner_of):
        start, size = lead
        left = [d for d in range(far) if d not in fixed]

        def body(i, carry):
            z = lax.div(i, 2 ** len(left))
            where, inner = [own[d] for d in range(far)], []
            for k, d in enumerate(left):
                where[d] = lax.rem(lax.div(i, 2 ** (len(left) - 1 - k)), 2)
                inner.append(where[d])
            place = (start + z, *where)
            total = mine[place].astype(jnp.float32) + came[inner_of(start + z, z, inner)].astype(jnp.float32)
            mine[place] = total.astype(mine.dtype)
            return carry

        lax.fori_loop(0, size * 2 ** len(left), body, 0)

    def launch(t, stage):
        mine, came_core, came_far, came_seq = buffers(t)
        if stage == 0:
            local = pltpu.make_async_copy(grads[t].at[(*everything, own[far])], mine, local_sems.at[t])
            local.start()
            sent = grads[t].at[(*everything, 1 - own[far])]
            return [copies.start(sent, came_core, "fsdp", flip(group, bits[far]))], local
        if stage <= far:
            made = []
            for part in (0, 1):
                order = orders[part]
                if stage == 1:
                    add(mine, came_core, (low[part], half), [], lambda z, at, inner: (z, *inner))
                else:
                    came = came_far[stage - 2].at[part]
                    add(mine, came, (low[part], half), order[: stage - 1], lambda z, at, inner: (at, *inner))
                dim = order[stage - 1]
                where = [slice(None)] * far
                for d in order[: stage - 1]:
                    where[d] = own[d]
                where[dim] = 1 - own[dim]
                made.append(
                    copies.start(
                        mine.at[(pl.ds(low[part], half), *where)],
                        came_far[stage - 1].at[part],
                        "fsdp",
                        flip(group, bits[dim]),
                    )
                )
            return made, None
        for part in (0, 1):
            came = came_far[far - 1].at[part]
            add(mine, came, (low[part], half), orders[part], lambda z, at, inner: (at,))
        made = []
        for k in range(1, length):
            other = flip_all(seq, k)
            made.append(copies.start(mine.at[(other, *own[:far])], came_seq.at[k - 1], "seq", other))
        return made, None

    def close(t):
        mine, _, _, came_seq = buffers(t)
        total = mine[(seq, *own[:far])].astype(jnp.float32)
        for k in range(1, length):
            total = total + came_seq[k - 1].astype(jnp.float32)
        outs[t][...] = total

    for step in range(count + stages):
        for t in range(count):
            stage = step - t
            if 0 < stage <= stages:
                made, local = waiting[t]
                for copy in made:
                    copy.wait_recv()
                if local is not None:
                    local.wait()
            if 0 <= stage < stages:
                waiting[t] = launch(t, stage)
            elif stage == stages:
                close(t)
    copies.finish()


def scatter_dense(grads, collective_id):
    length, groups = lax.axis_size("seq"), lax.axis_size("fsdp")
    bits, bit = [], groups // 2
    while bit >= 1:
        bits.append(bit)
        bit //= 2
    far = len(bits) - 1
    count = len(grads)
    number = count * (1 + 2 * far + length - 1)
    size = sum(g.size * g.dtype.itemsize for g in grads)
    scratch = []
    for g in grads:
        block = g.shape[1:]
        scratch += [pltpu.VMEM((length,) + (2,) * far + block, g.dtype)] * 2
        scratch += [
            pltpu.VMEM((2, length // 2) + (2,) * (far - 1 - s) + block, g.dtype) for s in range(far)
        ]
        scratch.append(pltpu.VMEM((length - 1,) + block, g.dtype))
    return pl.pallas_call(
        functools.partial(scatter_dense_kernel, length, bits, count),
        out_shape=[jax.ShapeDtypeStruct(g.shape[1:], jnp.float32) for g in grads],
        in_specs=[pl.BlockSpec(memory_space=pl.ANY)] * count,
        out_specs=[pl.BlockSpec(memory_space=pltpu.VMEM)] * count,
        scratch_shapes=scratch
        + [
            pltpu.SemaphoreType.DMA((number,)),
            pltpu.SemaphoreType.DMA((number,)),
            pltpu.SemaphoreType.DMA((count,)),
        ],
        compiler_params=pltpu.CompilerParams(
            collective_id=collective_id, has_side_effects=True, vmem_limit_bytes=grant(scratch, 0)
        ),
        cost_estimate=pl.CostEstimate(flops=0, bytes_accessed=3 * size, transcendentals=0),
        name="scatter_dense",
    )(*[g.reshape((length,) + (2,) * len(bits) + g.shape[1:]) for g in grads])


def row_dims():
    groups = lax.axis_size("fsdp")
    dims, bit = [("seq", 1)], groups // 2
    while bit >= 1:
        dims.append(("fsdp", bit))
        bit //= 2
    return dims


def row_places(dims):
    seq, group = lax.axis_index("seq"), lax.axis_index("fsdp")
    index = {"seq": seq, "fsdp": group}
    own = [bit_of(index[axis], bit) for axis, bit in dims]
    partner = [(axis, flip(index[axis], bit)) for axis, bit in dims]
    return own, partner


def gather_rows_kernel(dims, held, rows_ref, pick_ref, slots_ref, buffer, send_sems, recv_sems, local_sem):
    own, partner = row_places(dims)
    greet(partner)
    copies = Copies(send_sems, recv_sems)
    far = len(dims) - 1
    pieces = far
    width = rows_ref.shape[2]
    capacity = slots_ref.shape[-2]

    def view(piece, done):
        where = list(own)
        for d in done:
            where[d] = slice(None)
        return buffer.at[(piece, *where)]

    local = pltpu.make_async_copy(rows_ref, buffer.at[(slice(None), *own)], local_sem)
    local.start()
    flying = []
    for piece in range(pieces):
        first = piece
        flying.append(copies.start(rows_ref.at[piece], view(piece, []), *partner[first]))
    local.wait()

    def pick_block(piece, where):
        taken = jnp.dot(
            pick_ref[tuple(where)], buffer[(piece, *where)], preferred_element_type=jnp.float32
        ).astype(slots_ref.dtype)
        for e in range(held):
            slots_ref[(e, *where, slice(None), pl.ds(piece * width, width))] = taken[
                e * capacity : (e + 1) * capacity
            ]

    def pick_all(piece, core):
        def body(i, carry):
            where, rest = [], i
            for d in range(far):
                where.append(lax.rem(lax.div(rest, 2 ** (far - 1 - d)), 2))
            pick_block(piece, where + [core])
            return carry

        lax.fori_loop(0, 2**far, body, 0)

    for stage in range(1, far + 1):
        for piece in range(pieces):
            flying[piece].wait_recv()
            order = [(piece + k) % far for k in range(far)]
            done = order[:stage]
            ref = view(piece, done)
            flying[piece] = copies.start(ref, ref, *(partner[order[stage]] if stage < far else partner[far]))
    for piece in range(pieces):
        pick_all(piece, own[far])
    for piece in range(pieces):
        flying[piece].wait_recv()
        pick_all(piece, 1 - own[far])
    copies.finish()


def gather_rows(rows, pick_low, held, collective_id):
    dims = row_dims()
    far = len(dims) - 1
    count, feat = rows.shape
    width = feat // far
    sources = 2 ** len(dims)
    capacity = pick_low.shape[1] // held
    lead = (2,) * len(dims)
    cut = rows.reshape(count, far, width).swapaxes(0, 1)
    number = far * (far + 1)
    scratch = [pltpu.VMEM((far,) + lead + (count, width), rows.dtype)]
    slots = pl.pallas_call(
        functools.partial(gather_rows_kernel, dims, held),
        out_shape=jax.ShapeDtypeStruct((held,) + lead + (capacity, feat), rows.dtype),
        in_specs=[pl.BlockSpec(memory_space=pltpu.VMEM)] * 2,
        out_specs=pl.BlockSpec(memory_space=pltpu.VMEM),
        scratch_shapes=scratch
        + [pltpu.SemaphoreType.DMA((number,)), pltpu.SemaphoreType.DMA((number,)), pltpu.SemaphoreType.DMA],
        compiler_params=pltpu.CompilerParams(
            collective_id=collective_id,
            has_side_effects=True,
            vmem_limit_bytes=grant(scratch, 12 * 2**20),
        ),
        cost_estimate=pl.CostEstimate(
            flops=2 * sources * pick_low.shape[1] * count * feat,
            bytes_accessed=6 * sources * count * feat,
            transcendentals=0,
        ),
        name="gather_rows",
    )(cut, pick_low.reshape(lead + pick_low.shape[1:]))
    return slots.reshape(held, sources * capacity, feat)


def scatter_rows_kernel(
    dims, held, slots_ref, pick_ref, out_ref, mine, other, came_core, came_far, send_sems, recv_sems
):
    own, partner = row_places(dims)
    greet(partner)
    copies = Copies(send_sems, recv_sems)
    far = len(dims) - 1
    pieces = far
    width = out_ref.shape[2]
    capacity = slots_ref.shape[-2]
    count = out_ref.shape[1]

    def spread(piece, core, target):
        def body(i, carry):
            where = [lax.rem(lax.div(i, 2 ** (far - 1 - d)), 2) for d in range(far)]
            total = jnp.zeros((count, width), jnp.float32)
            for e in range(held):
                rows = slots_ref[(e, *where, core, slice(None), pl.ds(piece * width, width))]
                chosen = pick_ref[(*where, core, pl.ds(e * capacity, capacity))]
                total = total + lax.dot_general(
                    chosen, rows, (((0,), (0,)), ((), ())), preferred_element_type=jnp.float32
                )
            target[(piece, *where)] = total.astype(target.dtype)
            return carry

        lax.fori_loop(0, 2**far, body, 0)

    flying = []
    for piece in range(pieces):
        spread(piece, 1 - own[far], other)
        flying.append(copies.start(other.at[piece], came_core.at[piece], *partner[far]))
    for piece in range(pieces):
        spread(piece, own[far], mine)

    def add_into(piece, fixed, came_view):
        left = [d for d in range(far) if d not in fixed]

        def body(i, carry):
            where, inner = [None] * far, []
            for k, d in enumerate(left):
                where[d] = lax.rem(lax.div(i, 2 ** (len(left) - 1 - k)), 2)
                inner.append(where[d])
            for d in fixed:
                where[d] = own[d]
            total = mine[(piece, *where)].astype(jnp.float32) + came_view[tuple(inner)].astype(jnp.float32)
            mine[(piece, *where)] = total.astype(mine.dtype)
            return carry

        lax.fori_loop(0, 2 ** len(left), body, 0)

    for stage in range(far):
        for piece in range(pieces):
            order = [(piece + k) % far for k in range(far)][::-1]
            fixed = order[:stage]
            flying[piece].wait_recv()
            add_into(piece, fixed, came_core.at[piece] if stage == 0 else came_far[stage - 1].at[piece])
            dim = order[stage]
            where = [slice(None)] * far
            for d in fixed:
                where[d] = own[d]
            where[dim] = 1 - own[dim]
            flying[piece] = copies.start(
                mine.at[(piece, *where)], came_far[stage].at[piece], *partner[dim]
            )
    for piece in range(pieces):
        flying[piece].wait_recv()
        out_ref[piece] = mine[(piece, *own[:far])].astype(jnp.float32) + came_far[far - 1][piece].astype(
            jnp.float32
        )
    copies.finish()


def scatter_rows(slots, pick_low, held, collective_id):
    dims = row_dims()
    far = len(dims) - 1
    count, feat = pick_low.shape[2], slots.shape[2]
    width = feat // far
    sources = 2 ** len(dims)
    capacity = pick_low.shape[1] // held
    lead = (2,) * len(dims)
    number = far * (far + 1)

    scratch = [pltpu.VMEM((far,) + (2,) * far + (count, width), slots.dtype)] * 3
    scratch += [pltpu.VMEM((far,) + (2,) * (far - 1 - s) + (count, width), slots.dtype) for s in range(far)]

    def kernel(slots_ref, pick_ref, out_ref, mine, other, came_core, *rest):
        came_far, sems = rest[:far], rest[far:]
        scatter_rows_kernel(
            dims, held, slots_ref, pick_ref, out_ref, mine, other, came_core, came_far, *sems
        )

    out = pl.pallas_call(
        kernel,
        out_shape=jax.ShapeDtypeStruct((far, count, width), jnp.float32),
        in_specs=[pl.BlockSpec(memory_space=pltpu.VMEM)] * 2,
        out_specs=pl.BlockSpec(memory_space=pltpu.VMEM),
        scratch_shapes=scratch + [pltpu.SemaphoreType.DMA((number,)), pltpu.SemaphoreType.DMA((number,))],
        compiler_params=pltpu.CompilerParams(
            collective_id=collective_id,
            has_side_effects=True,
            vmem_limit_bytes=grant(scratch, 4 * 2**20),
        ),
        cost_estimate=pl.CostEstimate(
            flops=2 * sources * pick_low.shape[1] * count * feat,
            bytes_accessed=6 * sources * count * feat,
            transcendentals=0,
        ),
        name="scatter_rows",
    )(slots.reshape((held,) + lead + (capacity, feat)), pick_low.reshape(lead + pick_low.shape[1:]))
    return out.swapaxes(0, 1).reshape(count, feat)


def block(
    tokens,
    teacher,
    valid_mask,
    segment_ids,
    routes,
    gate_weights,
    norm1_gain,
    query_weight,
    key_weight,
    value_weight,
    output_weight,
    norm2_gain,
    shared_gate_weight,
    shared_up_weight,
    shared_down_weight,
    expert_gate_weight,
    expert_up_weight,
    expert_down_weight,
):
    length, groups = lax.axis_size("seq"), lax.axis_size("fsdp")
    seq_index, group_index = lax.axis_index("seq"), lax.axis_index("fsdp")
    devices = length * groups
    tok_rows = tokens.shape[1]
    seq_len = segment_ids.shape[1]
    head_group = HEADS // KV_HEADS
    score_scale = 1.0 / math.sqrt(HEAD)
    key_width = KV_HEADS * HEAD
    query_width = HEADS * HEAD
    shared_width = shared_gate_weight.shape[1]

    lanes = 128
    gains = jnp.pad(jnp.stack([norm1_gain, norm2_gain], axis=1), ((0, 0), (0, lanes - 2)))
    qkv_full, output_full, gate_up_full, down_full, expert_gate_full = gather_dense(
        [
            jnp.concatenate([query_weight, key_weight, value_weight, gains], axis=1),
            output_weight,
            jnp.concatenate([shared_gate_weight, shared_up_weight], axis=1),
            shared_down_weight,
        ],
        expert_gate_weight,
    )

    def weight_grad(rows, grad_rows):
        grad = dot(rows, grad_rows, 0, 0).astype(BF16)
        return grad.reshape(devices, -1, grad.shape[1])

    qkv_width = query_width + 2 * key_width
    gain_plain = qkv_full[:, qkv_width : qkv_width + 2].T.astype(F32)
    qkv_full = qkv_full[:, :qkv_width]
    gain_one, gain_two = gain_plain[0], gain_plain[1]

    meta = jnp.concatenate([routes[0].T.astype(F32), gate_weights[0].T], axis=0)
    meta = after(meta, qkv_full)[None]
    for axis, bit in row_dims()[::-1]:
        came = exchange(meta, axis, bit)
        high = lax.rem(lax.div(lax.axis_index(axis), bit), 2) == 1
        meta = jnp.where(high, jnp.concatenate([came, meta]), jnp.concatenate([meta, came]))

    num_local = expert_gate_weight.shape[0]
    num_held = num_local // PAIR
    side = seq_index % PAIR

    def share(weight, k):
        return lax.dynamic_slice_in_dim(weight, (side ^ (k % PAIR)) * num_held, num_held, axis=0)

    def collect_start(weight, wait):
        sent = after(weight, *wait)
        return [exchange(share(sent, k), "seq", k) for k in range(1, length)]

    def collect_done(weight, came):
        part = weight.shape[1]
        full = jnp.zeros((num_held, length * part, weight.shape[2]), weight.dtype)
        for k, block in enumerate([share(weight, 0)] + came):
            full = lax.dynamic_update_slice(full, block, (0, (seq_index ^ k) * part, 0))
        return full

    x_float = tokens[0].astype(F32)
    normed_one = rms_norm(x_float, gain_one).astype(BF16)
    qkv_rows = dot(normed_one, qkv_full, 1, 0).astype(BF16)
    query_rows = qkv_rows[:, :query_width]
    key_value = [qkv_rows[:, query_width:]]
    longest = seq_len // 2
    back = min(length - 1, -(-(longest - 1) // tok_rows))
    for _ in range(back):
        key_value.insert(0, shift(key_value[0], "seq", 1))
    key_value_all = jnp.concatenate(key_value, axis=0)
    up_came = collect_start(expert_up_weight, [key_value_all])
    window = (back + 1) * tok_rows
    seg_padded = jnp.concatenate([jnp.full((back * tok_rows,), -1, jnp.int32), segment_ids[0]])
    seg_keys = lax.dynamic_slice_in_dim(seg_padded, seq_index * tok_rows, window)
    seg_here = seg_keys[back * tok_rows :]
    positions = back * tok_rows + jnp.arange(tok_rows, dtype=jnp.int32)
    key_positions = jnp.arange(window, dtype=jnp.int32)
    allowed = (key_positions[None, :] <= positions[:, None]) & (seg_keys[None, :] == seg_here[:, None])
    query_heads = query_rows.reshape(tok_rows, KV_HEADS, head_group, HEAD)
    key_heads = key_value_all[:, :key_width].reshape(window, KV_HEADS, HEAD)
    value_heads = key_value_all[:, key_width:].reshape(window, KV_HEADS, HEAD)

    def all_scores():
        raw_scores = jnp.einsum(
            "thgd,jhd->hgtj", query_heads, key_heads, preferred_element_type=F32
        )
        return jnp.where(allowed[None, None], raw_scores * score_scale, MASKED)

    scores = all_scores()
    log_total = jax.nn.logsumexp(scores, axis=-1, keepdims=True)
    prob_low = jnp.exp(scores - log_total).astype(BF16)
    attended = (
        jnp.einsum("hgtj,jhd->thgd", prob_low, value_heads, preferred_element_type=F32)
        .reshape(tok_rows, query_width)
        .astype(BF16)
    )
    mixed_rows = x_float + dot(attended, output_full, 1, 0)
    normed_two = rms_norm(mixed_rows, gain_two).astype(BF16)

    experts_all = num_local * groups
    capacity = tok_rows * TOP * 4 // (3 * experts_all)
    route_all, gate_all = meta[:, :TOP], meta[:, TOP:]
    held_ids = group_index * num_local + side * num_held + jnp.arange(num_held, dtype=jnp.int32)
    named = route_all[:, None] == held_ids.astype(F32)[None, :, None, None]
    has = jnp.any(named, axis=2)
    gate_of = jnp.sum(jnp.where(named, gate_all[:, None], 0.0), axis=2)
    token_order = jnp.arange(tok_rows, dtype=jnp.int32)
    earlier = (token_order[:, None] < token_order[None, :]).astype(BF16)
    before = lax.dot_general(
        has.astype(BF16), earlier, (((2,), (0,)), ((), ())), preferred_element_type=F32
    )
    slot_number = jnp.arange(capacity, dtype=F32)
    chosen = has[:, :, None] & (before[:, :, None] == slot_number[None, None, :, None])
    gate_slots = jnp.sum(jnp.where(chosen, gate_of[:, :, None], 0.0), axis=3)
    sources = PAIR * groups
    chosen_low = chosen.astype(BF16).reshape(sources, num_held * capacity, tok_rows)
    gate_canonical = jnp.moveaxis(gate_slots, 0, 1).reshape(num_held, sources * capacity, 1)
    down_came = collect_start(expert_down_weight, [normed_two])
    slot_rows = gather_rows(normed_two, chosen_low, num_held, 1)

    gate_up = dot(normed_two, gate_up_full, 1, 0)
    shared_gate, shared_up = gate_up[:, :shared_width], gate_up[:, shared_width:]
    shared_hidden = swiglu(shared_gate, shared_up).astype(BF16)
    shared_out = dot(shared_hidden, down_full, 1, 0)
    expert_gate_rows = batch_dot(slot_rows, expert_gate_full, 2, 1)
    up_came = [after(came, shared_out) for came in up_came]
    expert_up_full = collect_done(expert_up_weight, up_came)
    expert_up_rows = batch_dot(slot_rows, expert_up_full, 2, 1)
    expert_hidden = swiglu(expert_gate_rows, expert_up_rows).astype(BF16)
    expert_down_full = collect_done(
        expert_down_weight, [after(came, expert_hidden) for came in down_came]
    )
    expert_output = (gate_canonical * batch_dot(expert_hidden, expert_down_full, 2, 1)).astype(BF16)
    routed = scatter_rows(expert_output, chosen_low, num_held, 2)

    output = mixed_rows + shared_out + routed
    block_output = output.astype(BF16)
    valid_rows = valid_mask[0].astype(F32)[:, None]
    grad_out = valid_rows * (output - teacher[0].astype(F32))
    grad_low = grad_out.astype(BF16)

    grad_slots = gather_rows(grad_low, chosen_low, num_held, 3)
    grad_slots = (gate_canonical * grad_slots.astype(F32)).astype(BF16)

    def expert_grad(left, right, wait):
        grad = after(batch_dot(left, right, 1, 1).astype(BF16), *wait)
        rows = grad.shape[1] // length
        own = [None] * length
        for k in range(length):
            slab = lax.dynamic_slice_in_dim(grad, (seq_index ^ k) * rows, rows, axis=1)
            own[k] = exchange(slab, "seq", k) if k else slab
        return own

    def expert_sum(own, wait):
        own = [after(part, *wait).astype(F32) for part in own]
        same = sum(own[k] for k in range(0, length, PAIR))
        crossed = sum(own[k] for k in range(1, length, PAIR))
        return jnp.concatenate(
            [jnp.where(side == 0, same, crossed), jnp.where(side == 0, crossed, same)], axis=0
        )

    expert_down_own = expert_grad(expert_hidden, grad_slots, [])
    grad_hidden = batch_dot(grad_slots, expert_down_full, 2, 2)
    grad_gate_rows, grad_up_rows = swiglu_backward(expert_gate_rows, expert_up_rows, grad_hidden)
    grad_input = (
        batch_dot(grad_gate_rows, expert_gate_full, 2, 2) + batch_dot(grad_up_rows, expert_up_full, 2, 2)
    ).astype(BF16)
    grad_routed = scatter_rows(grad_input, chosen_low, num_held, 4)
    expert_gate_own = expert_grad(slot_rows, grad_gate_rows, [grad_routed])
    expert_up_own = expert_grad(slot_rows, grad_up_rows, [grad_routed])

    grad_shidden = dot(grad_low, down_full, 1, 1)
    grad_sgate_rows, grad_sup_rows = swiglu_backward(shared_gate, shared_up, grad_shidden)
    grad_gate_up = jnp.concatenate([grad_sgate_rows, grad_sup_rows], axis=1)
    grad_normed_two = dot(grad_gate_up, gate_up_full, 1, 1) + grad_routed
    _, pull_two = jax.vjp(rms_norm, mixed_rows, gain_two)
    grad_mixed_norm, grad_gain_two = pull_two(grad_normed_two)
    grad_mixed = grad_out + grad_mixed_norm
    grad_mixed_low = grad_mixed.astype(BF16)

    grad_attended = dot(grad_mixed_low, output_full, 1, 1).astype(BF16)
    grad_att_heads = grad_attended.reshape(tok_rows, KV_HEADS, head_group, HEAD)
    prob_full = jnp.exp(all_scores() - log_total)
    prob_back = prob_full.astype(BF16)
    grad_prob = jnp.einsum(
        "thgd,jhd->hgtj", grad_att_heads, value_heads, preferred_element_type=F32
    )
    grad_values = jnp.einsum(
        "hgtj,thgd->jhd", prob_back, grad_att_heads, preferred_element_type=F32
    ).reshape(window, key_width)
    row_delta = jnp.sum(prob_full * grad_prob, axis=-1, keepdims=True)
    grad_scores = (prob_full * (grad_prob - row_delta)).astype(BF16)
    grad_query = (
        (
            jnp.einsum("hgtj,jhd->thgd", grad_scores, key_heads, preferred_element_type=F32)
            * score_scale
        )
        .reshape(tok_rows, query_width)
        .astype(BF16)
    )
    grad_keys = (
        jnp.einsum("hgtj,thgd->jhd", grad_scores, query_heads, preferred_element_type=F32)
        * score_scale
    ).reshape(window, key_width)
    grad_key_value = jnp.concatenate([grad_keys, grad_values], axis=1)
    total = grad_key_value[:tok_rows]
    for step in range(1, back + 1):
        came = shift(total.astype(BF16), "seq", -1)
        total = came.astype(F32) + grad_key_value[step * tok_rows : (step + 1) * tok_rows]
    grad_qkv = jnp.concatenate([grad_query, total.astype(BF16)], axis=1)
    grad_normed_one = dot(grad_qkv, qkv_full, 1, 1)
    _, pull_one = jax.vjp(rms_norm, x_float, gain_one)
    grad_x_norm, grad_gain_one = pull_one(grad_normed_one)
    grad_tokens = grad_mixed + grad_x_norm

    gain_grads = jnp.stack([grad_gain_one, grad_gain_two]).reshape(2, devices, -1).swapaxes(0, 1)
    gain_rows = gain_grads.shape[2]
    gain_grads = jnp.pad(gain_grads, ((0, 0), (0, 6), (0, lanes - gain_rows)))
    grad_gate_up_block, grad_qkv_block, grad_output_block, grad_down_block, grad_gain_block = scatter_dense(
        [
            weight_grad(normed_two, grad_gate_up),
            weight_grad(normed_one, grad_qkv),
            weight_grad(attended, grad_mixed_low),
            weight_grad(shared_hidden, grad_low),
            gain_grads,
        ],
        5,
    )
    last = [grad_gain_block]
    grad_expert_down = expert_sum(expert_down_own, last)
    grad_expert_gate = expert_sum(expert_gate_own, last)
    grad_expert_up = expert_sum(expert_up_own, last)
    return (
        block_output[None],
        grad_tokens[None],
        grad_gain_block[0, :gain_rows],
        grad_qkv_block[:, :query_width],
        grad_qkv_block[:, query_width : query_width + key_width],
        grad_qkv_block[:, query_width + key_width :],
        grad_output_block,
        grad_gain_block[1, :gain_rows],
        grad_gate_up_block[:, :shared_width],
        grad_gate_up_block[:, shared_width:],
        grad_down_block,
        grad_expert_gate,
        grad_expert_up,
        grad_expert_down,
    )


def solution(mesh):
    rows = P("fsdp", "seq", None)
    dense = P(("seq", "fsdp"), None)
    gain = P(("seq", "fsdp"))
    return jax.shard_map(
        block,
        mesh=mesh,
        in_specs=(
            rows, rows, P("fsdp", "seq"), P("fsdp", None), rows, rows,
            gain, dense, dense, dense, dense, gain, dense, dense, dense, rows, rows, rows,
        ),
        out_specs=(
            rows, rows, gain, dense, dense, dense, dense, gain, dense, dense, dense, rows, rows, rows,
        ),
        check_vma=False,
    )
```

profile of v0, /device:TPU:0, one launch (start us, length us, event | category | flops | bytes accessed | tf_op | source)
XLA Modules:
  0.0 1048.0 jit_solution(16399143548189088781)
XLA Ops:
  10.0 131.0 %gather_dense.1 = (bf16[4,2,2,2,48,2688]{5,4,3,2,1,0:T(8,128)(2,1)S(1)}, bf16[4,2,2,2,48,1536]{5,4,3,2,1,0:T(8,128)(2,1)S(1)}, bf16[4,2,2,2,48,2048]{5,4,3,2,1,0...) custom-call(bf16[48,2688]{1,0:T(8,128)(2,1)S(1)} %fusion.50.refs_0_, ...), custom_call_target="tpu_custom_call" | custom-call | bytes 67239936 | tf_op jit(solution)/shard_map/gather_dense/pallas_call | solution.py:211
  141.1 2.1 copy-done.2
  144.8 2.7 copy-done.11
  149.2 3.3 copy-done.10
  152.9 5.5 convolution_convert_fusion.3
  160.3 17.2 %collective-permute-start = (bf16[256,1024]{1,0:T(8,128)(2,1)}, bf16[256,1024]{1,0:T(8,128)(2,1)}, u32[]{:S(2)}, u32[]{:S(2)}) collective-permute-start(bf16[256,1024]{1,0:T(8,128)(2,1)} %slice.96), channel_id=1, source_target_pairs={{0,8},{8,16},{16,24},{1,9},{9,17},{17,25},{2,10},{10,18},{18,26},{... | collective-permute-start | bytes 1572872 | tf_op jit(solution)/shard_map/ppermute | solution.py:33
  179.5 2.2 dynamic-slice_dynamic-update-slice_fusion
  181.7 3.6 collective-permute-start.3
  187.3 2.1 collective-permute-start.4
  192.7 4.9 collective-permute-done.5
  198.0 2.7 collective-permute-start.1
  202.4 4.6 collective-permute-done.1
  209.7 2.1 collective-permute-start.8
  214.4 2.0 copy.176
  216.4 2.7 reshape.228
  219.1 2.6 fusion.5
  225.4 2.3 convolution_convert_fusion.9
  231.8 2.6 constant_dynamic-slice_fusion.10
  234.4 2.8 collective-permute-start.11
  240.2 4.7 fusion.74
  245.3 2.1 fusion.75
  247.5 105.7 %gather_rows.2 = bf16[2,2,2,2,2,64,1536]{6,5,4,3,2,1,0:T(8,128)(2,1)S(1)} custom-call(bf16[3,256,512]{2,1,0:T(8,128)(2,1)S(1)} %bitcast.179, bf16[2,2,2,2,128,256]{5,4,3,2,1,0:T(8,128)(2,1)S(1)} %and_convert_fusion.pick_ref), custom_call_target="tpu_custom_call" | custom-call | flops 1610612736 | bytes 37748736 | tf_op jit(solution)/shard_map/gather_rows/pallas_call | solution.py:459
  353.2 3.4 fusion.76
  356.7 2.7 constant_dynamic-update-slice_fusion.5
  359.4 2.1 constant_dynamic-update-slice_fusion.4
  361.4 2.1 constant_dynamic-update-slice_fusion.3
  363.5 7.1 multiply_convert_fusion.2
  370.6 18.5 %collective-permute-done.10 = bf16[2,128,1536]{2,1,0:T(8,128)(2,1)S(1)} collective-permute-done((bf16[2,128,1536]{2,1,0:T(8,128)(2,1)S(1)}, bf16[2,128,1536]{2,1,0:T(8,128)(2,1)S(1)}, u32[]{:S(2)}, u32[]{:S(2)}) %collective-permute-start.10) | collective-permute-done | bytes 786464 | tf_op jit(solution)/shard_map/ppermute | solution.py:27
  389.1 2.1 constant_dynamic-update-slice_fusion.2
  392.1 2.1 constant_dynamic-update-slice_fusion
  394.1 5.5 multiply_convert_fusion
  399.7 63.8 %scatter_rows.2 = f32[3,256,512]{2,1,0:T(8,128)S(1)} custom-call(bf16[2,2,2,2,2,64,1536]{6,5,4,3,2,1,0:T(8,128)(2,1)S(1)} %bitcast.168, bf16[2,2,2,2,128,256]{5,4,3,2,1,0:T(8,128)(2,1)S(1)} %and_convert_fusion.pick_ref), custom_call_target="tpu_custom_call" | custom-call | flops 1610612736 | bytes 37748736 | tf_op jit(solution)/shard_map/scatter_rows/pallas_call | solution.py:572
  465.1 3.1 copy.155
  468.2 4.0 fusion.38
  473.1 2.3 fusion.29
  476.8 3.8 convolution_convert_fusion.4
  480.9 54.7 %gather_rows.3 = bf16[2,2,2,2,2,64,1536]{6,5,4,3,2,1,0:T(8,128)(2,1)S(1)} custom-call(bf16[3,256,512]{2,1,0:T(8,128)(2,1)S(1)} %bitcast.180, bf16[2,2,2,2,128,256]{5,4,3,2,1,0:T(8,128)(2,1)S(1)} %and_convert_fusion.pick_ref), custom_call_target="tpu_custom_call" | custom-call | flops 1610612736 | bytes 37748736 | tf_op jit(solution)/shard_map/gather_rows/pallas_call | solution.py:459
  536.8 6.8 convolution_convert_fusion.5
  543.6 9.5 multiply_convert_fusion.1
  553.2 6.6 convolution_convert_fusion.7
  559.9 6.4 fusion.77
  566.3 5.3 convolution_convert_fusion.6
  571.6 9.6 add_convert_fusion
  581.2 63.9 %scatter_rows.3 = f32[3,256,512]{2,1,0:T(8,128)S(1)} custom-call(bf16[2,2,2,2,2,64,1536]{6,5,4,3,2,1,0:T(8,128)(2,1)S(1)} %bitcast.160, bf16[2,2,2,2,128,256]{5,4,3,2,1,0:T(8,128)(2,1)S(1)} %and_convert_fusion.pick_ref), custom_call_target="tpu_custom_call" | custom-call | flops 1610612736 | bytes 37748736 | tf_op jit(solution)/shard_map/scatter_rows/pallas_call | solution.py:572
  646.7 3.2 copy.159
  649.9 5.7 multiply_reduce_fusion
  661.0 7.7 fusion.54
  668.8 5.5 fusion.1
  674.2 11.0 %fusion.3 = bf16[4,3,256,768]{2,3,1,0:T(8,128)(2,1)} fusion(f32[4,768,256,3]{2,1,3,0:T(8,128)} %get-tuple-element.134, f32[4,768,256,3]{2,1,3,0:T(8,128)} %copy-done.15, f32[4,3,256]{2,1,0:T(4,128)S(1)} %get-tuple-element.133, f32[4,3,256]{2,1,0:T(4,128)S(1)} %log_add_fusion, pred[256,768]{0,1:T(8,128)(4,1)S(1)} %copy-done.32), kind=kLoop, calls=%fused_computation.9 | loop fusion | flops 14155776 | bytes 23814144 | tf_op jit(solution)/shard_map/convert_element_type | solution.py:801
  685.3 4.2 multiply_convert_fusion.3
  699.1 2.7 collective-permute-start.18
  701.8 4.5 convolution_convert_fusion.1
  706.3 35.5 %collective-permute-done.12 = bf16[256,1024]{0,1:T(8,128)(2,1)S(1)} collective-permute-done((bf16[256,1024]{0,1:T(8,128)(2,1)S(1)}, bf16[256,1024]{0,1:T(8,128)(2,1)S(1)}, u32[]{:S(2)}, u32[]{:S(2)}) %collective-permute-start.12) | collective-permute-done | bytes 524320 | tf_op jit(solution)/shard_map/ppermute | solution.py:33
  746.2 2.6 collective-permute-start.15
  748.9 5.0 convolution_convert_fusion.2
  754.0 16.0 %collective-permute-done.13 = bf16[256,1024]{0,1:T(8,128)(2,1)} collective-permute-done((bf16[256,1024]{0,1:T(8,128)(2,1)}, bf16[256,1024]{0,1:T(8,128)(2,1)}, u32[]{:S(2)}, u32[]{:S(2)}) %collective-permute-start.13) | collective-permute-done | bytes 524320 | tf_op jit(solution)/shard_map/ppermute | solution.py:33
  774.1 2.9 collective-permute-start.19
  777.1 6.7 fusion.14
  783.9 7.1 convolution_convert_fusion
  791.0 48.7 %collective-permute-done.19 = bf16[2,384,512]{2,1,0:T(8,128)(2,1)} collective-permute-done((bf16[2,384,512]{2,1,0:T(8,128)(2,1)}, bf16[2,384,512]{2,1,0:T(8,128)(2,1)}, u32[]{:S(2)}, u32[]{:S(2)}) %collective-permute-start.19) | collective-permute-done | bytes 786464 | tf_op jit(solution)/shard_map/ppermute | solution.py:27
  839.9 2.3 copy-done
  842.2 188.7 %scatter_dense.1 = (f32[48,2048]{1,0:T(8,128)S(1)}, f32[48,2560]{1,0:T(8,128)S(1)}, f32[48,1536]{1,0:T(8,128)S(1)}, f32[32,1536]{1,0:T(8,128)S(1)}, f32[8,128]{1,0:T(8,128)S(1)}) custom-call(bf16[4,2,2,2,48,2048]{5,4,3,2,1,0:T(8,128)(2,1)S(1)} %bitcast.158, bf16[4,2,2,2,48,2560]{5,4,3,2,1,0:T(8,128)(2,1)} %bitcast.189, ...), custom_call_target="tpu_custom_call" | custom-call | bytes 66453504 | tf_op jit(solution)/shard_map/scatter_dense/pallas_call | solution.py:355
  1035.3 3.4 fusion.22
  1038.6 2.0 pad_maximum_fusion
  (293 shorter events, 83.4 us)
Async XLA Ops:
  0.6 152.2 %copy-start.20 = (bf16[1,256,1536]{2,1,0:T(8,128)(2,1)S(1)}, bf16[1,256,1536]{2,1,0:T(8,128)(2,1)}, u32[]{:S(2)}) copy-start(bf16[1,256,1536]{2,1,0:T(8,128)(2,1)} %param.18) | copy-start | bytes 2359300
  2.1 179.5 %collective-permute-start.2 = (f32[1,12,256]{2,1,0:T(8,128)S(1)}, f32[1,12,256]{2,1,0:T(8,128)S(1)}, u32[]{:S(2)}, u32[]{:S(2)}) collective-permute-start(f32[1,12,256]{2,1,0:T(8,128)S(1)} %bitcast.213), channel_id=1, source_target_pairs={{0,1},{1,0},{2,3},{3,2},{4,5},{5,4},{6,7},{7,6},{8,9},{9,8},{10,11... | collective-permute-start | bytes 36872 | tf_op jit(solution)/shard_map/ppermute | solution.py:27
  4.0 145.2 %copy-start.67 = (f32[256]{0:T(256)}, f32[256]{0:T(256)S(1)}, u32[]{:S(2)}) copy-start(f32[256]{0:T(256)S(1)} %fusion.18) | copy-start | bytes 3076
  4.1 154.3 %copy-start.65 = (f32[256]{0:T(256)}, f32[256]{0:T(256)S(1)}, u32[]{:S(2)}) copy-start(f32[256]{0:T(256)S(1)} %fusion.58) | copy-start | bytes 3076
  152.9 24.7 %copy-start.69 = (s32[1,1024]{1,0:T(1,128)S(1)}, s32[1,1024]{1,0:T(1,128)}, u32[]{:S(2)}) copy-start(s32[1,1024]{1,0:T(1,128)} %param.21) | copy-start | bytes 12292
  160.3 37.7 %collective-permute-start = (bf16[256,1024]{1,0:T(8,128)(2,1)}, bf16[256,1024]{1,0:T(8,128)(2,1)}, u32[]{:S(2)}, u32[]{:S(2)}) collective-permute-start(bf16[256,1024]{1,0:T(8,128)(2,1)} %slice.96), channel_id=1, source_target_pairs={{0,8},{8,16},{16,24},{1,9},{9,17},{17,25},{2,10},{10,18},{18,26},{... | collective-permute-start | bytes 1572872 | tf_op jit(solution)/shard_map/ppermute | solution.py:33
  179.5 11.7 %copy-start.39 = (bf16[4,384,512]{2,1,0:T(8,128)(2,1)S(1)}, bf16[4,384,512]{2,1,0:T(8,128)(2,1)}, u32[]{:S(2)}) copy-start(bf16[4,384,512]{2,1,0:T(8,128)(2,1)} %param.34) | copy-start | bytes 4718596
  181.7 5.5 collective-permute-start.3
  187.3 5.3 collective-permute-start.4
  192.5 26.6 %copy-start.25 = (bf16[256,1536]{0,1:T(8,128)(2,1)}, bf16[256,1536]{0,1:T(8,128)(2,1)S(1)}, u32[]{:S(2)}) copy-start(bf16[256,1536]{0,1:T(8,128)(2,1)S(1)} %copy.140) | copy-start | bytes 2359300
  192.6 5.0 collective-permute-start.5
  198.0 8.9 collective-permute-start.1
  201.9 6.6 copy-start.40
  209.7 146.9 %collective-permute-start.8 = (bf16[2,384,512]{2,1,0:T(8,128)(2,1)}, bf16[2,384,512]{2,1,0:T(8,128)(2,1)}, u32[]{:S(2)}, u32[]{:S(2)}) collective-permute-start(bf16[2,384,512]{2,1,0:T(8,128)(2,1)} %get-tuple-element.115), channel_id=1, source_target_pairs={{0,24},{8,16},{16,8},{24,0},{1,25},{9,17},{17,9},{25,1},{2,26},{10... | collective-permute-start | bytes 2359304 | tf_op jit(solution)/shard_map/ppermute | solution.py:27
  211.7 145.0 %collective-permute-start.6 = (bf16[2,384,512]{2,1,0:T(8,128)(2,1)}, bf16[2,384,512]{2,1,0:T(8,128)(2,1)}, u32[]{:S(2)}, u32[]{:S(2)}) collective-permute-start(bf16[2,384,512]{2,1,0:T(8,128)(2,1)} %get-tuple-element.115), channel_id=1, source_target_pairs={{0,8},{8,0},{16,24},{24,16},{1,9},{9,1},{17,25},{25,17},{2,10},{10... | collective-permute-start | bytes 2359304 | tf_op jit(solution)/shard_map/ppermute | solution.py:27
  221.8 5.9 slice-start.2
  230.6 9.6 copy-start.33
  234.4 136.2 %collective-permute-start.11 = (bf16[2,128,1536]{2,1,0:T(8,128)(2,1)}, bf16[2,128,1536]{2,1,0:T(8,128)(2,1)}, u32[]{:S(2)}, u32[]{:S(2)}) collective-permute-start(bf16[2,128,1536]{2,1,0:T(8,128)(2,1)} %get-tuple-element.113), channel_id=1, source_target_pairs={{0,24},{8,16},{16,8},{24,0},{1,25},{9,17},{17,9},{25,1},{2,26},{10... | collective-permute-start | bytes 2359304 | tf_op jit(solution)/shard_map/ppermute | solution.py:27
  237.2 151.9 %collective-permute-start.9 = (bf16[2,128,1536]{2,1,0:T(8,128)(2,1)}, bf16[2,128,1536]{2,1,0:T(8,128)(2,1)}, u32[]{:S(2)}, u32[]{:S(2)}) collective-permute-start(bf16[2,128,1536]{2,1,0:T(8,128)(2,1)} %get-tuple-element.113), channel_id=1, source_target_pairs={{0,8},{8,0},{16,24},{24,16},{1,9},{9,1},{17,25},{25,17},{2,10},{10... | collective-permute-start | bytes 2359304 | tf_op jit(solution)/shard_map/ppermute | solution.py:27
  237.2 119.5 %collective-permute-start.7 = (bf16[2,384,512]{2,1,0:T(8,128)(2,1)}, bf16[2,384,512]{2,1,0:T(8,128)(2,1)}, u32[]{:S(2)}, u32[]{:S(2)}) collective-permute-start(bf16[2,384,512]{2,1,0:T(8,128)(2,1)} %get-tuple-element.114), channel_id=1, source_target_pairs={{0,16},{8,24},{16,0},{24,8},{1,17},{9,25},{17,1},{25,9},{2,18},{10... | collective-permute-start | bytes 2359304 | tf_op jit(solution)/shard_map/ppermute | solution.py:27
  245.3 107.8 %copy-start.36 = (bf16[256,1024]{1,0:T(8,128)(2,1)}, bf16[256,1024]{1,0:T(8,128)(2,1)S(1)}, u32[]{:S(2)}) copy-start(bf16[256,1024]{1,0:T(8,128)(2,1)S(1)} %multiply_convert_fusion.6) | copy-start | bytes 1572868
  247.5 105.7 %copy-start.13 = (bf16[2,1536,512]{2,1,0:T(8,128)(2,1)S(1)}, bf16[2,1536,512]{2,1,0:T(8,128)(2,1)}, u32[]{:S(2)}) copy-start(bf16[2,1536,512]{2,1,0:T(8,128)(2,1)} %copy-done.12) | copy-start | bytes 9437188
  353.1 10.3 copy-start.3
  356.6 14.0 %copy-start.72 = (f32[2,1024,512]{2,1,0:T(8,128)}, f32[2,1024,512]{2,1,0:T(8,128)S(1)}, u32[]{:S(2)}) copy-start(f32[2,1024,512]{2,1,0:T(8,128)S(1)} %fusion.76) | copy-start | bytes 12582916
  356.6 32.5 %collective-permute-start.10 = (bf16[2,128,1536]{2,1,0:T(8,128)(2,1)S(1)}, bf16[2,128,1536]{2,1,0:T(8,128)(2,1)S(1)}, u32[]{:S(2)}, u32[]{:S(2)}) collective-permute-start(bf16[2,128,1536]{2,1,0:T(8,128)(2,1)S(1)} %copy-done.58), channel_id=1, source_target_pairs={{0,16},{8,24},{16,0},{24,8},{1,17},{9,25},{17,1},{25,9},{2,18},{10... | collective-permute-start | bytes 2359304 | tf_op jit(solution)/shard_map/ppermute | solution.py:27
  370.6 29.1 %copy-start.73 = (bf16[2,1024,512]{2,1,0:T(8,128)(2,1)}, bf16[2,1024,512]{2,1,0:T(8,128)(2,1)S(1)}, u32[]{:S(2)}) copy-start(bf16[2,1024,512]{2,1,0:T(8,128)(2,1)S(1)} %get-tuple-element.130) | copy-start | bytes 6291460
  536.8 16.4 %slice-start.6 = ((s8[6291456]{0:T(1024)(128)(4,1)}), s8[4194304]{0:T(1024)(128)(4,1)S(1)}, s32[]{:S(2)}) async-start(s8[6291456]{0:T(1024)(128)(4,1)} %bitcast.171), calls=%async_computation.6 | async-start | bytes 8388608
  543.6 9.6 slice-start.7
  553.2 6.6 copy-start.14
  553.2 6.6 copy-start.71
  559.9 6.4 copy-start.53
  645.1 13.3 %slice-start.4 = ((s8[4718592]{0:T(1024)(128)(4,1)}), s8[524288]{0:T(1024)(128)(4,1)S(1)}, s32[]{:S(2)}) async-start(s8[4718592]{0:T(1024)(128)(4,1)} %bitcast.165), calls=%async_computation.4 | async-start | bytes 1048576
  649.9 8.4 slice-start.5
  658.3 10.4 slice-start.8
  660.9 7.8 slice-start.9
  661.0 7.8 slice-start.10
  661.0 7.8 copy-start.42
  661.0 7.8 copy-start.43
  674.2 11.0 %copy-start.28 = (bf16[768,4,128,1]{0,2,3,1:T(8,128)(2,1)S(1)}, bf16[768,4,128,1]{0,2,3,1:T(8,128)(2,1)}, u32[]{:S(2)}) copy-start(bf16[768,4,128,1]{0,2,3,1:T(8,128)(2,1)} %copy-done.27) | copy-start | bytes 2359300
  693.1 79.9 %collective-permute-start.21 = (bf16[2,128,1536]{2,1,0:T(8,128)(2,1)}, bf16[2,128,1536]{2,1,0:T(8,128)(2,1)}, u32[]{:S(2)}, u32[]{:S(2)}) collective-permute-start(bf16[2,128,1536]{2,1,0:T(8,128)(2,1)} %get-tuple-element.92), channel_id=1, source_target_pairs={{0,8},{8,0},{16,24},{24,16},{1,9},{9,1},{17,25},{25,17},{2,10},{10... | collective-permute-start | bytes 2359304 | tf_op jit(solution)/shard_map/ppermute | solution.py:27
  694.9 79.2 %collective-permute-start.20 = (bf16[2,128,1536]{2,1,0:T(8,128)(2,1)}, bf16[2,128,1536]{2,1,0:T(8,128)(2,1)}, u32[]{:S(2)}, u32[]{:S(2)}) collective-permute-start(bf16[2,128,1536]{2,1,0:T(8,128)(2,1)} %get-tuple-element.94), channel_id=1, source_target_pairs={{0,16},{8,24},{16,0},{24,8},{1,17},{9,25},{17,1},{25,9},{2,18},{10... | collective-permute-start | bytes 2359304 | tf_op jit(solution)/shard_map/ppermute | solution.py:27
  695.9 45.9 %collective-permute-start.12 = (bf16[256,1024]{0,1:T(8,128)(2,1)S(1)}, bf16[256,1024]{0,1:T(8,128)(2,1)S(1)}, u32[]{:S(2)}, u32[]{:S(2)}) collective-permute-start(bf16[256,1024]{0,1:T(8,128)(2,1)S(1)} %fusion.34), channel_id=1, source_target_pairs={{8,0},{16,8},{24,16},{9,1},{17,9},{25,17},{10,2},{18,10},{26,18},{... | collective-permute-start | bytes 1572872 | tf_op jit(solution)/shard_map/ppermute | solution.py:33
  699.1 77.9 %collective-permute-start.18 = (bf16[2,384,512]{2,1,0:T(8,128)(2,1)}, bf16[2,384,512]{2,1,0:T(8,128)(2,1)}, u32[]{:S(2)}, u32[]{:S(2)}) collective-permute-start(bf16[2,384,512]{2,1,0:T(8,128)(2,1)} %get-tuple-element.98), channel_id=1, source_target_pairs={{0,8},{8,0},{16,24},{24,16},{1,9},{9,1},{17,25},{25,17},{2,10},{10... | collective-permute-start | bytes 2359304 | tf_op jit(solution)/shard_map/ppermute | solution.py:27
  706.3 38.1 %copy-start.45 = (bf16[2,1536,512]{2,1,0:T(8,128)(2,1)S(1)}, bf16[2,1536,512]{2,1,0:T(8,128)(2,1)}, u32[]{:S(2)}) copy-start(bf16[2,1536,512]{2,1,0:T(8,128)(2,1)} %convolution_convert_fusion.7) | copy-start | bytes 9437188
  742.8 6.1 copy-start.30
  742.8 27.2 %collective-permute-start.13 = (bf16[256,1024]{0,1:T(8,128)(2,1)}, bf16[256,1024]{0,1:T(8,128)(2,1)}, u32[]{:S(2)}, u32[]{:S(2)}) collective-permute-start(bf16[256,1024]{0,1:T(8,128)(2,1)} %fusion.32), channel_id=1, source_target_pairs={{8,0},{16,8},{24,16},{9,1},{17,9},{25,17},{10,2},{18,10},{26,18},{... | collective-permute-start | bytes 1572872 | tf_op jit(solution)/shard_map/ppermute | solution.py:33
  746.2 284.7 %collective-permute-start.15 = (bf16[2,384,512]{2,1,0:T(8,128)(2,1)}, bf16[2,384,512]{2,1,0:T(8,128)(2,1)}, u32[]{:S(2)}, u32[]{:S(2)}) collective-permute-start(bf16[2,384,512]{2,1,0:T(8,128)(2,1)} %get-tuple-element.104), channel_id=1, source_target_pairs={{0,8},{8,0},{16,24},{24,16},{1,9},{9,1},{17,25},{25,17},{2,10},{10... | collective-permute-start | bytes 2359304 | tf_op jit(solution)/shard_map/ppermute | solution.py:27
  748.9 22.9 %copy-start.22 = (f32[4,128,768,1]{2,1,3,0:T(8,128)S(1)}, f32[4,128,768,1]{2,1,3,0:T(8,128)}, u32[]{:S(2)}) copy-start(f32[4,128,768,1]{2,1,3,0:T(8,128)} %fusion.54) | copy-start | bytes 4718596
  754.0 23.1 %copy-start.44 = (bf16[4,128,3,256]{3,1,2,0:T(8,128)(2,1)S(1)}, bf16[4,128,3,256]{3,1,2,0:T(8,128)(2,1)}, u32[]{:S(2)}) copy-start(bf16[4,128,3,256]{3,1,2,0:T(8,128)(2,1)} %multiply_convert_fusion.3) | copy-start | bytes 2359300
  754.0 23.1 %copy-start.64 = (f32[1536]{0:T(1024)S(1)}, f32[1536]{0:T(1024)}, u32[]{:S(2)}) copy-start(f32[1536]{0:T(1024)} %copy-done.63) | copy-start | bytes 18436
  754.0 23.1 %copy-start.66 = (f32[256]{0:T(256)S(1)}, f32[256]{0:T(256)}, u32[]{:S(2)}) copy-start(f32[256]{0:T(256)} %copy-done.65) | copy-start | bytes 3076
  770.0 260.9 %collective-permute-start.16 = (bf16[2,384,512]{2,1,0:T(8,128)(2,1)}, bf16[2,384,512]{2,1,0:T(8,128)(2,1)}, u32[]{:S(2)}, u32[]{:S(2)}) collective-permute-start(bf16[2,384,512]{2,1,0:T(8,128)(2,1)} %get-tuple-element.105), channel_id=1, source_target_pairs={{0,24},{8,16},{16,8},{24,0},{1,25},{9,17},{17,9},{25,1},{2,26},{10... | collective-permute-start | bytes 2359304 | tf_op jit(solution)/shard_map/ppermute | solution.py:27
  773.0 10.9 %copy-start.56 = (bf16[256,1024]{0,1:T(8,128)(2,1)}, bf16[256,1024]{0,1:T(8,128)(2,1)S(1)}, u32[]{:S(2)}) copy-start(bf16[256,1024]{0,1:T(8,128)(2,1)S(1)} %fusion.36) | copy-start | bytes 1572868
  773.0 258.0 %collective-permute-start.14 = (bf16[2,384,512]{2,1,0:T(8,128)(2,1)}, bf16[2,384,512]{2,1,0:T(8,128)(2,1)}, u32[]{:S(2)}, u32[]{:S(2)}) collective-permute-start(bf16[2,384,512]{2,1,0:T(8,128)(2,1)} %get-tuple-element.106), channel_id=1, source_target_pairs={{0,16},{8,24},{16,0},{24,8},{1,17},{9,25},{17,1},{25,9},{2,18},{10... | collective-permute-start | bytes 2359304 | tf_op jit(solution)/shard_map/ppermute | solution.py:27
  774.1 65.7 %collective-permute-start.19 = (bf16[2,384,512]{2,1,0:T(8,128)(2,1)}, bf16[2,384,512]{2,1,0:T(8,128)(2,1)}, u32[]{:S(2)}, u32[]{:S(2)}) collective-permute-start(bf16[2,384,512]{2,1,0:T(8,128)(2,1)} %get-tuple-element.99), channel_id=1, source_target_pairs={{0,24},{8,16},{16,8},{24,0},{1,25},{9,17},{17,9},{25,1},{2,26},{10... | collective-permute-start | bytes 2359304 | tf_op jit(solution)/shard_map/ppermute | solution.py:27
  777.0 253.9 %collective-permute-start.17 = (bf16[2,384,512]{2,1,0:T(8,128)(2,1)}, bf16[2,384,512]{2,1,0:T(8,128)(2,1)}, u32[]{:S(2)}, u32[]{:S(2)}) collective-permute-start(bf16[2,384,512]{2,1,0:T(8,128)(2,1)} %get-tuple-element.100), channel_id=1, source_target_pairs={{0,16},{8,24},{16,0},{24,8},{1,17},{9,25},{17,1},{25,9},{2,18},{10... | collective-permute-start | bytes 2359304 | tf_op jit(solution)/shard_map/ppermute | solution.py:27
  783.8 56.0 %slice-start = ((s8[6291456]{0:T(1024)(128)(4,1)}), s8[2097152]{0:T(1024)(128)(4,1)S(1)}, s32[]{:S(2)}) async-start(s8[6291456]{0:T(1024)(128)(4,1)} %bitcast.156), calls=%async_computation | async-start | bytes 4194304
  783.9 55.8 %copy-start.59 = (bf16[2,128,1536]{2,1,0:T(8,128)(2,1)S(1)}, bf16[2,128,1536]{2,1,0:T(8,128)(2,1)}, u32[]{:S(2)}) copy-start(bf16[2,128,1536]{2,1,0:T(8,128)(2,1)} %get-tuple-element.93) | copy-start | bytes 2359300
  783.9 55.9 %slice-start.1 = ((s8[6291456]{0:T(1024)(128)(4,1)}), s8[4194304]{0:T(1024)(128)(4,1)S(1)}, s32[]{:S(2)}) async-start(s8[6291456]{0:T(1024)(128)(4,1)} %bitcast.156), calls=%async_computation.1 | async-start | bytes 8388608
  783.9 55.9 %copy-start.1 = (bf16[1024,1536]{1,0:T(8,128)(2,1)S(1)}, bf16[1024,1536]{1,0:T(8,128)(2,1)}, u32[]{:S(2)}) copy-start(bf16[1024,1536]{1,0:T(8,128)(2,1)} %convolution_convert_fusion.4) | copy-start | bytes 9437188
  839.8 193.1 %collective-permute-start.22 = (bf16[2,128,1536]{2,1,0:T(8,128)(2,1)S(1)}, bf16[2,128,1536]{2,1,0:T(8,128)(2,1)S(1)}, u32[]{:S(2)}, u32[]{:S(2)}) collective-permute-start(bf16[2,128,1536]{2,1,0:T(8,128)(2,1)S(1)} %copy-done.59), channel_id=1, source_target_pairs={{0,24},{8,16},{16,8},{24,0},{1,25},{9,17},{17,9},{25,1},{2,26},{10... | collective-permute-start | bytes 2359304 | tf_op jit(solution)/shard_map/ppermute | solution.py:27
  842.2 189.5 %copy-start.68 = (f32[256]{0:T(256)S(1)}, f32[256]{0:T(256)}, u32[]{:S(2)}) copy-start(f32[256]{0:T(256)} %copy-done.67) | copy-start | bytes 3076
  842.2 191.5 %copy-start.24 = (f32[256,1536]{1,0:T(8,128)S(1)}, f32[256,1536]{1,0:T(8,128)}, u32[]{:S(2)}) copy-start(f32[256,1536]{1,0:T(8,128)} %copy-done.23) | copy-start | bytes 4718596
  842.2 191.5 %copy-start.57 = (f32[256,1536]{1,0:T(8,128)S(1)}, f32[256,1536]{1,0:T(8,128)}, u32[]{:S(2)}) copy-start(f32[256,1536]{1,0:T(8,128)} %get-tuple-element.135) | copy-start | bytes 4718596
  (45 other events, 147.4 us)
where the time goes:
time: 1050 us
  Pallas kernels  608 us (58%)
  matrix products  135 us (13%)
  waiting for transfers between devices  129 us (12%)
  local copies, waits for them, and re-layouts  80.2 us (8%)
  starting transfers between devices  50.4 us (5%)
  other arithmetic  43.6 us (4%)
    pallas_call x1, Pallas kernels, scatter_dense(): pl.pallas_call(functools.partial(scatter_dense_kernel, length, bits, coun...  189 us
    pallas_call x2, Pallas kernels, gather_rows(): pl.pallas_call(functools.partial(gather_rows_kernel, dims, held), out_sha...  160 us
    pallas_call x1, Pallas kernels, gather_dense(): pl.pallas_call(functools.partial(gather_dense_kernel, length, bits, count...  131 us
    pallas_call x2, Pallas kernels, scatter_rows(): pl.pallas_call(kernel, out_shape=jax.ShapeDtypeStruct((far, count, width)...  128 us
    ppermute x19, waiting for transfers between devices, exchange(): return lax.ppermute(values, axis, [(i, i ^ bit) for i in range(count)])  73.2 us
    dot_general x9, matrix products, batch_dot(): lax.dot_general(left, right, (((left_dim,), (right_dim,)), ((0,), (0,))),...  60.3 us
    ppermute x4, waiting for transfers between devices, shift(): return lax.ppermute(values, axis, pairs)  56.1 us
    dot_general x12, matrix products, dot(): lax.dot_general(left, right, (((left_dim,), (right_dim,)), ((), ())), pre...  50.4 us
  transfers between devices with their start and end apart: 23, of which 7 were waited for; matrix products, arithmetic and copies ran while one was open for 9% of the time, Pallas kernels for 41%

commit v1 on v0

--- a/solution.py
+++ b/solution.py
@@ -222,7 +222,7 @@
             pltpu.SemaphoreType.DMA((count + 1,)),
         ],
         compiler_params=pltpu.CompilerParams(
-            collective_id=0, has_side_effects=True, vmem_limit_bytes=16 * 2**20
+            collective_id=0, has_side_effects=True, vmem_limit_bytes=60 * 2**20
         ),
         cost_estimate=pl.CostEstimate(flops=0, bytes_accessed=3 * size, transcendentals=0),
         name="gather_dense",
@@ -623,9 +623,12 @@
 
     lanes = 128
     gains = jnp.pad(jnp.stack([norm1_gain, norm2_gain], axis=1), ((0, 0), (0, lanes - 2)))
-    qkv_full, output_full, gate_up_full, down_full, expert_gate_full = gather_dense(
+    meta = jnp.concatenate([routes[0].T.astype(F32), gate_weights[0].T], axis=0)
+    meta = jnp.pad(meta, ((0, 16 - 2 * TOP), (0, 0)))
+    qkv_full, meta, output_full, gate_up_full, down_full, expert_gate_full = gather_dense(
         [
             jnp.concatenate([query_weight, key_weight, value_weight, gains], axis=1),
+            meta,
             output_weight,
             jnp.concatenate([shared_gate_weight, shared_up_weight], axis=1),
             shared_down_weight,
@@ -641,13 +644,6 @@
     gain_plain = qkv_full[:, qkv_width : qkv_width + 2].T.astype(F32)
     qkv_full = qkv_full[:, :qkv_width]
     gain_one, gain_two = gain_plain[0], gain_plain[1]
-
-    meta = jnp.concatenate([routes[0].T.astype(F32), gate_weights[0].T], axis=0)
-    meta = after(meta, qkv_full)[None]
-    for axis, bit in row_dims()[::-1]:
-        came = exchange(meta, axis, bit)
-        high = lax.rem(lax.div(lax.axis_index(axis), bit), 2) == 1
-        meta = jnp.where(high, jnp.concatenate([came, meta]), jnp.concatenate([meta, came]))
 
     num_local = expert_gate_weight.shape[0]
     num_held = num_local // PAIR
@@ -708,7 +704,10 @@
 
     experts_all = num_local * groups
     capacity = tok_rows * TOP * 4 // (3 * experts_all)
-    route_all, gate_all = meta[:, :TOP], meta[:, TOP:]
+    meta = lax.dynamic_slice_in_dim(
+        meta.reshape(length, groups, 16, tok_rows), seq_index // PAIR * PAIR, PAIR, axis=0
+    ).reshape(PAIR * groups, 16, tok_rows)
+    route_all, gate_all = meta[:, :TOP], meta[:, TOP : 2 * TOP]
     held_ids = group_index * num_local + side * num_held + jnp.arange(num_held, dtype=jnp.int32)
     named = route_all[:, None] == held_ids.astype(F32)[None, :, None, None]
     has = jnp.any(named, axis=2)
@@ -776,7 +775,6 @@
     ).astype(BF16)
     grad_routed = scatter_rows(grad_input, chosen_low, num_held, 4)
     expert_gate_own = expert_grad(slot_rows, grad_gate_rows, [grad_routed])
-    expert_up_own = expert_grad(slot_rows, grad_up_rows, [grad_routed])
 
     grad_shidden = dot(grad_low, down_full, 1, 1)
     grad_sgate_rows, grad_sup_rows = swiglu_backward(shared_gate, shared_up, grad_shidden)
@@ -817,6 +815,7 @@
         came = shift(total.astype(BF16), "seq", -1)
         total = came.astype(F32) + grad_key_value[step * tok_rows : (step + 1) * tok_rows]
     grad_qkv = jnp.concatenate([grad_query, total.astype(BF16)], axis=1)
+    expert_up_own = expert_grad(slot_rows, grad_up_rows, [total])
     grad_normed_one = dot(grad_qkv, qkv_full, 1, 1)
     _, pull_one = jax.vjp(rms_norm, x_float, gain_one)
     grad_x_norm, grad_gain_one = pull_one(grad_normed_one)
@@ -825,16 +824,15 @@
     gain_grads = jnp.stack([grad_gain_one, grad_gain_two]).reshape(2, devices, -1).swapaxes(0, 1)
     gain_rows = gain_grads.shape[2]
     gain_grads = jnp.pad(gain_grads, ((0, 0), (0, 6), (0, lanes - gain_rows)))
-    grad_gate_up_block, grad_qkv_block, grad_output_block, grad_down_block, grad_gain_block = scatter_dense(
-        [
-            weight_grad(normed_two, grad_gate_up),
-            weight_grad(normed_one, grad_qkv),
-            weight_grad(attended, grad_mixed_low),
-            weight_grad(shared_hidden, grad_low),
-            gain_grads,
-        ],
-        5,
-    )
+    dense_grads = [
+        weight_grad(normed_two, grad_gate_up),
+        weight_grad(normed_one, grad_qkv),
+        weight_grad(attended, grad_mixed_low),
+        weight_grad(shared_hidden, grad_low),
+        gain_grads,
+    ]
+    sums = scatter_dense(dense_grads, 5)
+    grad_gate_up_block, grad_qkv_block, grad_output_block, grad_down_block, grad_gain_block = sums
     last = [grad_gain_block]
     grad_expert_down = expert_sum(expert_down_own, last)
     grad_expert_gate = expert_sum(expert_gate_own, last)

time: 1050 us -> 1020 us (0.971)
  local copies, waits for them, and re-layouts: 80.2 us -> 57.9 us
  Pallas kernels: 608 us -> 591 us
    pallas_call x1, Pallas kernels: 189 us -> 158 us  [scatter_dense(): pl.pallas_call(functools.partial(scatter_dense_kernel, length, bits, coun...]
    pallas_call x1, Pallas kernels: 131 us -> 143 us  [gather_dense(): pl.pallas_call(functools.partial(gather_dense_kernel, length, bits, count...]
    unnamed x174 -> x164, local copies, waits for them, and re-layouts: 25.7 us -> 16.2 us
    ppermute x19 -> x15, waiting for transfers between devices: 73.2 us -> 79.8 us  [exchange(): return lax.ppermute(values, axis, [(i, i ^ bit) for i in range(count)])]
    ppermute x19 -> x15, starting transfers between devices: 27.4 us -> 22.7 us  [exchange(): return lax.ppermute(values, axis, [(i, i ^ bit) for i in range(count)])]
  transfers between devices with their start and end apart: 23 -> 19, of which waited for: 7 -> 7; matrix products, arithmetic and copies ran while one was open for 9% -> 8% of each run, Pallas kernels for 41% -> 26%
where the time goes in v1:
time: 1020 us; the launch traced here: 1010 us
  Pallas kernels  591 us (58%)
  matrix products  132 us (13%)
  waiting for transfers between devices  130 us (13%)
  local copies, waits for them, and re-layouts  57.9 us (6%)
  starting transfers between devices  49.6 us (5%)
  other arithmetic  45.7 us (4%)
    pallas_call x2, Pallas kernels, gather_rows(): pl.pallas_call(functools.partial(gather_rows_kernel, dims, held), out_sha...  162 us
    pallas_call x1, Pallas kernels, scatter_dense(): pl.pallas_call(functools.partial(scatter_dense_kernel, length, bits, coun...  158 us
    pallas_call x1, Pallas kernels, gather_dense(): pl.pallas_call(functools.partial(gather_dense_kernel, length, bits, count...  143 us
    pallas_call x2, Pallas kernels, scatter_rows(): pl.pallas_call(kernel, out_shape=jax.ShapeDtypeStruct((far, count, width)...  128 us
    ppermute x15, waiting for transfers between devices, exchange(): return lax.ppermute(values, axis, [(i, i ^ bit) for i in range(count)])  79.8 us
    dot_general x9, matrix products, batch_dot(): lax.dot_general(left, right, (((left_dim,), (right_dim,)), ((0,), (0,))),...  56.5 us
    dot_general x12, matrix products, dot(): lax.dot_general(left, right, (((left_dim,), (right_dim,)), ((), ())), pre...  51.7 us
    ppermute x4, waiting for transfers between devices, shift(): return lax.ppermute(values, axis, pairs)  50.5 us
  transfers between devices with their start and end apart: 19, of which 7 were waited for; matrix products, arithmetic and copies ran while one was open for 8% of the time, Pallas kernels for 26%

profile of v1, /device:TPU:0, one launch (start us, length us, event | category | flops | bytes accessed | tf_op | source)
XLA Modules:
  0.0 1008.7 jit_solution(3285420922913060545)
XLA Ops:
  8.2 142.8 %gather_dense.1 = (bf16[4,2,2,2,48,2688]{5,4,3,2,1,0:T(8,128)(2,1)}, f32[4,2,2,2,16,256]{5,4,3,2,1,0:T(8,128)}, bf16[4,2,2,2,48,1536]{5,4,3,2,1,0:T(8,128)(2,1)}...) custom-call(bf16[48,2688]{1,0:T(8,128)(2,1)} %fusion.55.refs_0_, ...), custom_call_target="tpu_custom_call" | custom-call | bytes 68812800 | tf_op jit(solution)/shard_map/gather_dense/pallas_call | solution.py:211
  152.5 5.6 fusion.14
  158.2 19.1 %collective-permute-start = (bf16[256,1024]{1,0:T(8,128)(2,1)S(1)}, bf16[256,1024]{1,0:T(8,128)(2,1)}, u32[]{:S(2)}, u32[]{:S(2)}) collective-permute-start(bf16[256,1024]{1,0:T(8,128)(2,1)S(1)} %slice.96), channel_id=1, source_target_pairs={{0,8},{8,16},{16,24},{1,9},{9,17},{17,25},{2,10},{10,18},{18,26},{... | collective-permute-start | bytes 1572872 | tf_op jit(solution)/shard_map/ppermute | solution.py:33
  181.1 5.8 collective-permute-done
  186.9 4.5 collective-permute-start.1
  193.2 8.1 collective-permute-done.1
  203.7 2.1 collective-permute-start.4
  208.7 2.0 copy.206
  210.7 2.7 reshape.231
  213.4 2.6 fusion.9
  216.2 1.9 exponential_reduce_fusion
  218.1 2.8 copy-done.4
  220.9 2.3 convolution_convert_fusion.8
  227.3 2.6 constant_dynamic-slice_fusion.10
  229.9 2.4 collective-permute-start.7
  232.2 2.0 collective-permute-start.3
  235.7 4.7 fusion.77
  240.8 2.1 fusion.78
  242.9 108.7 %gather_rows.2 = bf16[2,2,2,2,2,64,1536]{6,5,4,3,2,1,0:T(8,128)(2,1)S(1)} custom-call(bf16[3,256,512]{2,1,0:T(8,128)(2,1)S(1)} %bitcast.170, bf16[2,2,2,2,128,256]{5,4,3,2,1,0:T(8,128)(2,1)S(1)} %and_convert_fusion.pick_ref), custom_call_target="tpu_custom_call" | custom-call | flops 1610612736 | bytes 37748736 | tf_op jit(solution)/shard_map/gather_rows/pallas_call | solution.py:459
  351.6 3.4 fusion.79
  360.2 5.3 multiply_convert_fusion.2
  365.5 24.1 %collective-permute-done.6 = bf16[2,128,1536]{2,1,0:T(8,128)(2,1)S(1)} collective-permute-done((bf16[2,128,1536]{2,1,0:T(8,128)(2,1)S(1)}, bf16[2,128,1536]{2,1,0:T(8,128)(2,1)S(1)}, u32[]{:S(2)}, u32[]{:S(2)}) %collective-permute-start.6) | collective-permute-done | bytes 786464 | tf_op jit(solution)/shard_map/ppermute | solution.py:27
  392.1 3.6 multiply_convert_fusion
  395.8 62.5 %scatter_rows.2 = f32[3,256,512]{2,1,0:T(8,128)S(1)} custom-call(bf16[2,2,2,2,2,64,1536]{6,5,4,3,2,1,0:T(8,128)(2,1)S(1)} %bitcast.161, bf16[2,2,2,2,128,256]{5,4,3,2,1,0:T(8,128)(2,1)S(1)} %and_convert_fusion.pick_ref), custom_call_target="tpu_custom_call" | custom-call | flops 1610612736 | bytes 37748736 | tf_op jit(solution)/shard_map/scatter_rows/pallas_call | solution.py:572
  459.9 3.1 copy.185
  463.0 4.0 fusion.44
  467.9 2.3 fusion.36
  471.6 3.8 convolution_convert_fusion.3
  475.7 53.7 %gather_rows.3 = bf16[2,2,2,2,2,64,1536]{6,5,4,3,2,1,0:T(8,128)(2,1)S(1)} custom-call(bf16[3,256,512]{2,1,0:T(8,128)(2,1)S(1)} %bitcast.171, bf16[2,2,2,2,128,256]{5,4,3,2,1,0:T(8,128)(2,1)S(1)} %and_convert_fusion.pick_ref), custom_call_target="tpu_custom_call" | custom-call | flops 1610612736 | bytes 37748736 | tf_op jit(solution)/shard_map/gather_rows/pallas_call | solution.py:459
  530.7 7.0 convolution_convert_fusion.4
  537.8 9.5 multiply_convert_fusion.1
  547.3 6.6 convolution_convert_fusion.6
  553.9 6.5 fusion.80
  560.4 4.9 convolution_convert_fusion.5
  565.3 9.6 add_convert_fusion
  574.9 65.2 %scatter_rows.3 = f32[3,256,512]{2,1,0:T(8,128)S(1)} custom-call(bf16[2,2,2,2,2,64,1536]{6,5,4,3,2,1,0:T(8,128)(2,1)S(1)} %bitcast.159, bf16[2,2,2,2,128,256]{5,4,3,2,1,0:T(8,128)(2,1)S(1)} %and_convert_fusion.pick_ref), custom_call_target="tpu_custom_call" | custom-call | flops 1610612736 | bytes 37748736 | tf_op jit(solution)/shard_map/scatter_rows/pallas_call | solution.py:572
  641.7 3.2 copy.189
  644.9 5.8 multiply_reduce_fusion
  653.4 3.8 convolution_convert_fusion.7
  658.5 7.7 fusion.59
  666.3 5.4 fusion.1
  671.6 11.1 %fusion.3 = bf16[4,3,256,768]{2,3,1,0:T(8,128)(2,1)} fusion(f32[4,768,256,3]{2,1,3,0:T(8,128)} %get-tuple-element.134, f32[4,768,256,3]{2,1,3,0:T(8,128)} %copy-done.4, f32[4,3,256]{2,1,0:T(4,128)S(1)} %get-tuple-element.133, f32[4,3,256]{2,1,0:T(4,128)S(1)} %log_add_fusion, pred[256,768]{0,1:T(8,128)(4,1)S(1)} %copy-done.26), kind=kLoop, calls=%fused_computation.9 | loop fusion | flops 14155776 | bytes 23814144 | tf_op jit(solution)/shard_map/convert_element_type | solution.py:799
  682.8 4.2 multiply_convert_fusion.3
  692.2 2.5 collective-permute-start.17
  694.6 2.8 collective-permute-start.16
  697.4 4.5 convolution_convert_fusion.1
  702.0 19.6 %collective-permute-done.8 = bf16[256,1024]{0,1:T(8,128)(2,1)S(1)} collective-permute-done((bf16[256,1024]{0,1:T(8,128)(2,1)S(1)}, bf16[256,1024]{0,1:T(8,128)(2,1)S(1)}, u32[]{:S(2)}, u32[]{:S(2)}) %collective-permute-start.8) | collective-permute-done | bytes 524320 | tf_op jit(solution)/shard_map/ppermute | solution.py:33
  724.1 1.7 constant_dynamic-slice_fusion.7
  725.9 2.6 collective-permute-start.11
  728.6 5.0 convolution_convert_fusion.2
  733.7 17.0 %collective-permute-done.9 = bf16[256,1024]{0,1:T(8,128)(2,1)} collective-permute-done((bf16[256,1024]{0,1:T(8,128)(2,1)}, bf16[256,1024]{0,1:T(8,128)(2,1)}, u32[]{:S(2)}, u32[]{:S(2)}) %collective-permute-start.9) | collective-permute-done | bytes 524320 | tf_op jit(solution)/shard_map/ppermute | solution.py:33
  750.7 2.8 collective-permute-start.10
  754.7 6.8 fusion.21
  762.6 5.6 convolution_convert_fusion
  768.4 2.8 copy-done
  771.2 2.3 copy-done.1
  773.5 157.8 %scatter_dense.1 = (f32[48,2048]{1,0:T(8,128)S(1)}, f32[48,2560]{1,0:T(8,128)S(1)}, f32[48,1536]{1,0:T(8,128)S(1)}, f32[32,1536]{1,0:T(8,128)S(1)}, f32[8,128]{1,0:T(8,128)S(1)}) custom-call(bf16[4,2,2,2,48,2048]{5,4,3,2,1,0:T(8,128)(2,1)S(1)} %bitcast.157, bf16[4,2,2,2,48,2560]{5,4,3,2,1,0:T(8,128)(2,1)} %bitcast.175, ...), custom_call_target="tpu_custom_call" | custom-call | bytes 66453504 | tf_op jit(solution)/shard_map/scatter_dense/pallas_call | solution.py:355
  937.9 2.1 fusion.33
  940.0 1.9 pad_maximum_fusion.2
  944.8 24.1 %collective-permute-done.15 = bf16[2,384,512]{2,1,0:T(8,128)(2,1)S(1)} collective-permute-done((bf16[2,384,512]{2,1,0:T(8,128)(2,1)S(1)}, bf16[2,384,512]{2,1,0:T(8,128)(2,1)S(1)}, u32[]{:S(2)}, u32[]{:S(2)}) %collective-permute-start.15) | collective-permute-done | bytes 786464 | tf_op jit(solution)/shard_map/ppermute | solution.py:27
  968.9 31.6 %collective-permute-done.13 = bf16[2,384,512]{2,1,0:T(8,128)(2,1)S(1)} collective-permute-done((bf16[2,384,512]{2,1,0:T(8,128)(2,1)S(1)}, bf16[2,384,512]{2,1,0:T(8,128)(2,1)S(1)}, u32[]{:S(2)}, u32[]{:S(2)}) %collective-permute-start.13) | collective-permute-done | bytes 786464 | tf_op jit(solution)/shard_map/ppermute | solution.py:27
  1000.5 2.7 fusion.29
  1003.1 2.0 pad_maximum_fusion
  1005.1 2.0 pad_maximum_fusion.1
  (269 shorter events, 64.9 us)
Async XLA Ops:
  0.6 151.8 %copy-start.9 = (bf16[1,256,1536]{2,1,0:T(8,128)(2,1)S(1)}, bf16[1,256,1536]{2,1,0:T(8,128)(2,1)}, u32[]{:S(2)}) copy-start(bf16[1,256,1536]{2,1,0:T(8,128)(2,1)} %param.18) | copy-start | bytes 2359300
  2.1 149.0 %copy-start.64 = (f32[256]{0:T(256)}, f32[256]{0:T(256)S(1)}, u32[]{:S(2)}) copy-start(f32[256]{0:T(256)S(1)} %fusion.25) | copy-start | bytes 3076
  2.1 155.9 %copy-start.62 = (f32[256]{0:T(256)}, f32[256]{0:T(256)S(1)}, u32[]{:S(2)}) copy-start(f32[256]{0:T(256)S(1)} %fusion.63) | copy-start | bytes 3076
  152.5 24.8 %copy-start.59 = (f32[4,2,2,2,16,256]{5,4,3,2,1,0:T(8,128)S(1)}, f32[4,2,2,2,16,256]{5,4,3,2,1,0:T(8,128)}, u32[]{:S(2)}) copy-start(f32[4,2,2,2,16,256]{5,4,3,2,1,0:T(8,128)} %get-tuple-element.51) | copy-start | bytes 1572868
  158.1 20.3 %copy-start.66 = (s32[1,1024]{1,0:T(1,128)S(1)}, s32[1,1024]{1,0:T(1,128)}, u32[]{:S(2)}) copy-start(s32[1,1024]{1,0:T(1,128)} %param.21) | copy-start | bytes 12292
  158.1 20.5 %copy-start.67 = (s32[1,256]{1,0:T(1,128)S(1)}, s32[1,256]{1,0:T(1,128)}, u32[]{:S(2)}) copy-start(s32[1,256]{1,0:T(1,128)} %param.20) | copy-start | bytes 3076
  158.2 21.2 %copy-start.53 = (bf16[256,1024]{1,0:T(8,128)(2,1)}, bf16[256,1024]{1,0:T(8,128)(2,1)S(1)}, u32[]{:S(2)}) copy-start(bf16[256,1024]{1,0:T(8,128)(2,1)S(1)} %slice.96) | copy-start | bytes 1572868
  158.2 28.7 %collective-permute-start = (bf16[256,1024]{1,0:T(8,128)(2,1)S(1)}, bf16[256,1024]{1,0:T(8,128)(2,1)}, u32[]{:S(2)}, u32[]{:S(2)}) collective-permute-start(bf16[256,1024]{1,0:T(8,128)(2,1)S(1)} %slice.96), channel_id=1, source_target_pairs={{0,8},{8,16},{16,24},{1,9},{9,17},{17,25},{2,10},{10,18},{18,26},{... | collective-permute-start | bytes 1572872 | tf_op jit(solution)/shard_map/ppermute | solution.py:33
  179.0 34.4 %copy-start.19 = (bf16[256,1536]{0,1:T(8,128)(2,1)}, bf16[256,1536]{0,1:T(8,128)(2,1)S(1)}, u32[]{:S(2)}) copy-start(bf16[256,1536]{0,1:T(8,128)(2,1)S(1)} %copy.171) | copy-start | bytes 2359300
  180.7 12.0 %copy-start.16 = (bf16[2,1536,512]{2,1,0:T(8,128)(2,1)}, bf16[2,1536,512]{2,1,0:T(8,128)(2,1)S(1)}, u32[]{:S(2)}) copy-start(bf16[2,1536,512]{2,1,0:T(8,128)(2,1)S(1)} %dynamic-slice_dynamic-update-slice_fusion.1) | copy-start | bytes 9437188
  181.0 12.1 %copy-start.44 = (bf16[2,512,1536]{2,1,0:T(8,128)(2,1)}, bf16[2,512,1536]{2,1,0:T(8,128)(2,1)S(1)}, u32[]{:S(2)}) copy-start(bf16[2,512,1536]{2,1,0:T(8,128)(2,1)S(1)} %dynamic-slice_dynamic-update-slice_fusion) | copy-start | bytes 9437188
  186.9 14.4 %collective-permute-start.1 = (bf16[256,1024]{1,0:T(8,128)(2,1)}, bf16[256,1024]{1,0:T(8,128)(2,1)S(1)}, u32[]{:S(2)}, u32[]{:S(2)}) collective-permute-start(bf16[256,1024]{1,0:T(8,128)(2,1)} %collective-permute-done), channel_id=1, source_target_pairs={{0,8},{8,16},{16,24},{1,9},{9,17},{17,25},{2,10},{10,18},{18,26},{... | collective-permute-start | bytes 1572872 | tf_op jit(solution)/shard_map/ppermute | solution.py:33
  192.3 8.9 copy-start.54
  192.6 9.8 copy-start.33
  203.7 151.4 %collective-permute-start.4 = (bf16[2,384,512]{2,1,0:T(8,128)(2,1)}, bf16[2,384,512]{2,1,0:T(8,128)(2,1)}, u32[]{:S(2)}, u32[]{:S(2)}) collective-permute-start(bf16[2,384,512]{2,1,0:T(8,128)(2,1)} %get-tuple-element.115), channel_id=1, source_target_pairs={{0,24},{8,16},{16,8},{24,0},{1,25},{9,17},{17,9},{25,1},{2,26},{10... | collective-permute-start | bytes 2359304 | tf_op jit(solution)/shard_map/ppermute | solution.py:27
  205.8 149.4 %collective-permute-start.2 = (bf16[2,384,512]{2,1,0:T(8,128)(2,1)}, bf16[2,384,512]{2,1,0:T(8,128)(2,1)}, u32[]{:S(2)}, u32[]{:S(2)}) collective-permute-start(bf16[2,384,512]{2,1,0:T(8,128)(2,1)} %get-tuple-element.115), channel_id=1, source_target_pairs={{0,8},{8,0},{16,24},{24,16},{1,9},{9,1},{17,25},{25,17},{2,10},{10... | collective-permute-start | bytes 2359304 | tf_op jit(solution)/shard_map/ppermute | solution.py:27
  216.2 7.1 slice-start.5
  226.1 9.6 copy-start.27
  229.9 135.6 %collective-permute-start.7 = (bf16[2,128,1536]{2,1,0:T(8,128)(2,1)}, bf16[2,128,1536]{2,1,0:T(8,128)(2,1)}, u32[]{:S(2)}, u32[]{:S(2)}) collective-permute-start(bf16[2,128,1536]{2,1,0:T(8,128)(2,1)} %get-tuple-element.113), channel_id=1, source_target_pairs={{0,24},{8,16},{16,8},{24,0},{1,25},{9,17},{17,9},{25,1},{2,26},{10... | collective-permute-start | bytes 2359304 | tf_op jit(solution)/shard_map/ppermute | solution.py:27
  232.2 157.4 %collective-permute-start.5 = (bf16[2,128,1536]{2,1,0:T(8,128)(2,1)}, bf16[2,128,1536]{2,1,0:T(8,128)(2,1)}, u32[]{:S(2)}, u32[]{:S(2)}) collective-permute-start(bf16[2,128,1536]{2,1,0:T(8,128)(2,1)} %get-tuple-element.113), channel_id=1, source_target_pairs={{0,8},{8,0},{16,24},{24,16},{1,9},{9,1},{17,25},{25,17},{2,10},{10... | collective-permute-start | bytes 2359304 | tf_op jit(solution)/shard_map/ppermute | solution.py:27
  232.2 122.9 %collective-permute-start.3 = (bf16[2,384,512]{2,1,0:T(8,128)(2,1)}, bf16[2,384,512]{2,1,0:T(8,128)(2,1)}, u32[]{:S(2)}, u32[]{:S(2)}) collective-permute-start(bf16[2,384,512]{2,1,0:T(8,128)(2,1)} %get-tuple-element.114), channel_id=1, source_target_pairs={{0,16},{8,24},{16,0},{24,8},{1,17},{9,25},{17,1},{25,9},{2,18},{10... | collective-permute-start | bytes 2359304 | tf_op jit(solution)/shard_map/ppermute | solution.py:27
  240.8 110.8 %copy-start.30 = (bf16[256,1024]{1,0:T(8,128)(2,1)}, bf16[256,1024]{1,0:T(8,128)(2,1)S(1)}, u32[]{:S(2)}) copy-start(bf16[256,1024]{1,0:T(8,128)(2,1)S(1)} %multiply_convert_fusion.6) | copy-start | bytes 1572868
  242.9 108.7 %copy-start.68 = (bf16[2,1536,512]{2,1,0:T(8,128)(2,1)S(1)}, bf16[2,1536,512]{2,1,0:T(8,128)(2,1)}, u32[]{:S(2)}) copy-start(bf16[2,1536,512]{2,1,0:T(8,128)(2,1)} %get-tuple-element.52) | copy-start | bytes 9437188
  351.6 8.5 copy-start.3
  355.1 10.4 %copy-start.71 = (f32[2,1024,512]{2,1,0:T(8,128)}, f32[2,1024,512]{2,1,0:T(8,128)S(1)}, u32[]{:S(2)}) copy-start(f32[2,1024,512]{2,1,0:T(8,128)S(1)} %fusion.79) | copy-start | bytes 12582916
  355.1 34.5 %collective-permute-start.6 = (bf16[2,128,1536]{2,1,0:T(8,128)(2,1)S(1)}, bf16[2,128,1536]{2,1,0:T(8,128)(2,1)S(1)}, u32[]{:S(2)}, u32[]{:S(2)}) collective-permute-start(bf16[2,128,1536]{2,1,0:T(8,128)(2,1)S(1)} %copy-done.56), channel_id=1, source_target_pairs={{0,16},{8,24},{16,0},{24,8},{1,17},{9,25},{17,1},{25,9},{2,18},{10... | collective-permute-start | bytes 2359304 | tf_op jit(solution)/shard_map/ppermute | solution.py:27
  360.1 29.5 %copy-start.45 = (bf16[2,512,1536]{2,1,0:T(8,128)(2,1)S(1)}, bf16[2,512,1536]{2,1,0:T(8,128)(2,1)}, u32[]{:S(2)}) copy-start(bf16[2,512,1536]{2,1,0:T(8,128)(2,1)} %copy-done.44) | copy-start | bytes 9437188
  365.5 30.3 %copy-start.72 = (bf16[2,1024,512]{2,1,0:T(8,128)(2,1)}, bf16[2,1024,512]{2,1,0:T(8,128)(2,1)S(1)}, u32[]{:S(2)}) copy-start(bf16[2,1024,512]{2,1,0:T(8,128)(2,1)S(1)} %get-tuple-element.130) | copy-start | bytes 6291460
  530.7 16.5 %slice-start = ((s8[6291456]{0:T(1024)(128)(4,1)}), s8[4194304]{0:T(1024)(128)(4,1)S(1)}, s32[]{:S(2)}) async-start(s8[6291456]{0:T(1024)(128)(4,1)} %bitcast.164), calls=%async_computation | async-start | bytes 8388608
  537.8 9.5 slice-start.1
  547.3 6.6 copy-start.69
  547.3 6.6 copy-start.70
  553.9 6.5 copy-start.50
  653.4 12.8 %slice-start.2 = ((s8[9437184]{0:T(1024)(128)(4,1)}), s8[1048576]{0:T(1024)(128)(4,1)S(1)}, s32[]{:S(2)}) async-start(s8[9437184]{0:T(1024)(128)(4,1)} %bitcast.173), calls=%async_computation.2 | async-start | bytes 2097152
  658.5 7.8 slice-start.3
  658.5 7.8 slice-start.4
  658.5 7.8 copy-start.36
  658.5 7.8 copy-start.37
  671.6 11.1 %copy-start.22 = (bf16[768,4,128,1]{0,2,3,1:T(8,128)(2,1)S(1)}, bf16[768,4,128,1]{0,2,3,1:T(8,128)(2,1)}, u32[]{:S(2)}) copy-start(bf16[768,4,128,1]{0,2,3,1:T(8,128)(2,1)} %copy-done.21) | copy-start | bytes 2359300
  688.7 8.8 copy-start.28
  688.7 8.7 copy-start.57
  688.7 8.7 copy-start.58
  688.7 32.8 %collective-permute-start.8 = (bf16[256,1024]{0,1:T(8,128)(2,1)S(1)}, bf16[256,1024]{0,1:T(8,128)(2,1)S(1)}, u32[]{:S(2)}, u32[]{:S(2)}) collective-permute-start(bf16[256,1024]{0,1:T(8,128)(2,1)S(1)} %fusion.41), channel_id=1, source_target_pairs={{8,0},{16,8},{24,16},{9,1},{17,9},{25,17},{10,2},{18,10},{26,18},{... | collective-permute-start | bytes 1572872 | tf_op jit(solution)/shard_map/ppermute | solution.py:33
  692.2 69.3 %collective-permute-start.17 = (bf16[2,128,1536]{2,1,0:T(8,128)(2,1)}, bf16[2,128,1536]{2,1,0:T(8,128)(2,1)}, u32[]{:S(2)}, u32[]{:S(2)}) collective-permute-start(bf16[2,128,1536]{2,1,0:T(8,128)(2,1)} %get-tuple-element.92), channel_id=1, source_target_pairs={{0,8},{8,0},{16,24},{24,16},{1,9},{9,1},{17,25},{25,17},{2,10},{10... | collective-permute-start | bytes 2359304 | tf_op jit(solution)/shard_map/ppermute | solution.py:27
  694.6 237.0 %collective-permute-start.16 = (bf16[2,128,1536]{2,1,0:T(8,128)(2,1)}, bf16[2,128,1536]{2,1,0:T(8,128)(2,1)}, u32[]{:S(2)}, u32[]{:S(2)}) collective-permute-start(bf16[2,128,1536]{2,1,0:T(8,128)(2,1)} %get-tuple-element.94), channel_id=1, source_target_pairs={{0,16},{8,24},{16,0},{24,8},{1,17},{9,25},{17,1},{25,9},{2,18},{10... | collective-permute-start | bytes 2359304 | tf_op jit(solution)/shard_map/ppermute | solution.py:27
  702.0 22.2 %copy-start.42 = (bf16[2,1536,512]{2,1,0:T(8,128)(2,1)S(1)}, bf16[2,1536,512]{2,1,0:T(8,128)(2,1)}, u32[]{:S(2)}) copy-start(bf16[2,1536,512]{2,1,0:T(8,128)(2,1)} %convolution_convert_fusion.6) | copy-start | bytes 9437188
  722.5 6.1 copy-start.24
  722.5 28.2 %collective-permute-start.9 = (bf16[256,1024]{0,1:T(8,128)(2,1)}, bf16[256,1024]{0,1:T(8,128)(2,1)}, u32[]{:S(2)}, u32[]{:S(2)}) collective-permute-start(bf16[256,1024]{0,1:T(8,128)(2,1)} %fusion.39), channel_id=1, source_target_pairs={{8,0},{16,8},{24,16},{9,1},{17,9},{25,17},{10,2},{18,10},{26,18},{... | collective-permute-start | bytes 1572872 | tf_op jit(solution)/shard_map/ppermute | solution.py:33
  725.9 207.7 %collective-permute-start.11 = (bf16[2,384,512]{2,1,0:T(8,128)(2,1)}, bf16[2,384,512]{2,1,0:T(8,128)(2,1)}, u32[]{:S(2)}, u32[]{:S(2)}) collective-permute-start(bf16[2,384,512]{2,1,0:T(8,128)(2,1)} %get-tuple-element.104), channel_id=1, source_target_pairs={{0,8},{8,0},{16,24},{24,16},{1,9},{9,1},{17,25},{25,17},{2,10},{10... | collective-permute-start | bytes 2359304 | tf_op jit(solution)/shard_map/ppermute | solution.py:27
  728.5 203.8 %collective-permute-start.12 = (bf16[2,384,512]{2,1,0:T(8,128)(2,1)}, bf16[2,384,512]{2,1,0:T(8,128)(2,1)}, u32[]{:S(2)}, u32[]{:S(2)}) collective-permute-start(bf16[2,384,512]{2,1,0:T(8,128)(2,1)} %get-tuple-element.105), channel_id=1, source_target_pairs={{0,24},{8,16},{16,8},{24,0},{1,25},{9,17},{17,9},{25,1},{2,26},{10... | collective-permute-start | bytes 2359304 | tf_op jit(solution)/shard_map/ppermute | solution.py:27
  728.6 24.9 %copy-start.13 = (f32[4,128,768,1]{2,1,3,0:T(8,128)S(1)}, f32[4,128,768,1]{2,1,3,0:T(8,128)}, u32[]{:S(2)}) copy-start(f32[4,128,768,1]{2,1,3,0:T(8,128)} %fusion.59) | copy-start | bytes 4718596
  733.7 21.0 %copy-start.38 = (bf16[4,128,3,256]{3,1,2,0:T(8,128)(2,1)S(1)}, bf16[4,128,3,256]{3,1,2,0:T(8,128)(2,1)}, u32[]{:S(2)}) copy-start(bf16[4,128,3,256]{3,1,2,0:T(8,128)(2,1)} %multiply_convert_fusion.3) | copy-start | bytes 2359300
  733.7 21.0 %copy-start.61 = (f32[1536]{0:T(1024)S(1)}, f32[1536]{0:T(1024)}, u32[]{:S(2)}) copy-start(f32[1536]{0:T(1024)} %copy-done.60) | copy-start | bytes 18436
  733.7 21.0 %copy-start.63 = (f32[256]{0:T(256)S(1)}, f32[256]{0:T(256)}, u32[]{:S(2)}) copy-start(f32[256]{0:T(256)} %copy-done.62) | copy-start | bytes 3076
  750.7 184.5 %collective-permute-start.10 = (bf16[2,384,512]{2,1,0:T(8,128)(2,1)}, bf16[2,384,512]{2,1,0:T(8,128)(2,1)}, u32[]{:S(2)}, u32[]{:S(2)}) collective-permute-start(bf16[2,384,512]{2,1,0:T(8,128)(2,1)} %get-tuple-element.106), channel_id=1, source_target_pairs={{0,16},{8,24},{16,0},{24,8},{1,17},{9,25},{17,1},{25,9},{2,18},{10... | collective-permute-start | bytes 2359304 | tf_op jit(solution)/shard_map/ppermute | solution.py:27
  754.7 7.9 copy-start.10
  761.5 6.9 copy-start.2
  761.5 175.6 %collective-permute-start.18 = (bf16[2,128,1536]{2,1,0:T(8,128)(2,1)}, bf16[2,128,1536]{2,1,0:T(8,128)(2,1)}, u32[]{:S(2)}, u32[]{:S(2)}) collective-permute-start(bf16[2,128,1536]{2,1,0:T(8,128)(2,1)} %get-tuple-element.93), channel_id=1, source_target_pairs={{0,24},{8,16},{16,8},{24,0},{1,25},{9,17},{17,9},{25,1},{2,26},{10... | collective-permute-start | bytes 2359304 | tf_op jit(solution)/shard_map/ppermute | solution.py:27
  773.5 157.9 %copy-start.41 = (bf16[2,1536,512]{2,1,0:T(8,128)(2,1)S(1)}, bf16[2,1536,512]{2,1,0:T(8,128)(2,1)}, u32[]{:S(2)}) copy-start(bf16[2,1536,512]{2,1,0:T(8,128)(2,1)} %convolution_convert_fusion.5) | copy-start | bytes 9437188
  931.4 6.5 copy-start.48
  931.6 37.3 %collective-permute-start.14 = (bf16[2,384,512]{2,1,0:T(8,128)(2,1)S(1)}, bf16[2,384,512]{2,1,0:T(8,128)(2,1)S(1)}, u32[]{:S(2)}, u32[]{:S(2)}) collective-permute-start(bf16[2,384,512]{2,1,0:T(8,128)(2,1)S(1)} %get-tuple-element.98), channel_id=1, source_target_pairs={{0,8},{8,0},{16,24},{24,16},{1,9},{9,1},{17,25},{25,17},{2,10},{10... | collective-permute-start | bytes 2359304 | tf_op jit(solution)/shard_map/ppermute | solution.py:27
  932.3 36.6 %collective-permute-start.15 = (bf16[2,384,512]{2,1,0:T(8,128)(2,1)S(1)}, bf16[2,384,512]{2,1,0:T(8,128)(2,1)S(1)}, u32[]{:S(2)}, u32[]{:S(2)}) collective-permute-start(bf16[2,384,512]{2,1,0:T(8,128)(2,1)S(1)} %get-tuple-element.99), channel_id=1, source_target_pairs={{0,24},{8,16},{16,8},{24,0},{1,25},{9,17},{17,9},{25,1},{2,26},{10... | collective-permute-start | bytes 2359304 | tf_op jit(solution)/shard_map/ppermute | solution.py:27
  933.6 66.9 %collective-permute-start.13 = (bf16[2,384,512]{2,1,0:T(8,128)(2,1)S(1)}, bf16[2,384,512]{2,1,0:T(8,128)(2,1)S(1)}, u32[]{:S(2)}, u32[]{:S(2)}) collective-permute-start(bf16[2,384,512]{2,1,0:T(8,128)(2,1)S(1)} %get-tuple-element.100), channel_id=1, source_target_pairs={{0,16},{8,24},{16,0},{24,8},{1,17},{9,25},{17,1},{25,9},{2,18},{10... | collective-permute-start | bytes 2359304 | tf_op jit(solution)/shard_map/ppermute | solution.py:27
  941.9 58.6 %copy-start.47 = (bf16[2,384,512]{2,1,0:T(8,128)(2,1)S(1)}, bf16[2,384,512]{2,1,0:T(8,128)(2,1)}, u32[]{:S(2)}) copy-start(bf16[2,384,512]{2,1,0:T(8,128)(2,1)} %get-tuple-element.67) | copy-start | bytes 2359300
  (35 other events, 119.9 us)

commit v2 on v1

--- a/solution.py
+++ b/solution.py
@@ -123,9 +123,17 @@
     return index
 
 
-def gather_dense_kernel(length, bits, count, *refs):
-    shards, expert, outs, expert_full = refs[:count], refs[count], refs[count + 1 : 2 * count + 1], refs[2 * count + 1]
-    send_sems, recv_sems, local_sems = refs[2 * count + 2 :]
+def gather_dense_kernel(length, bits, count, back, *refs):
+    extra = 0 if back is None else 1
+    shards, expert = refs[:count], refs[count]
+    outs, expert_full = refs[count + 1 + extra : 2 * count + 1 + extra], refs[2 * count + 1 + extra]
+    if back is None:
+        send_sems, recv_sems, local_sems = refs[2 * count + 2 :]
+        places = list(outs)
+    else:
+        tokens = refs[count + 1]
+        normed_ref, query_ref, window_ref, held, send_sems, recv_sems, local_sems, key_sems = refs[2 * count + 3 :]
+        places = [held] + list(outs[1:])
     seq, group = lax.axis_index("seq"), lax.axis_index("fsdp")
     own = [bit_of(group, bit) for bit in bits]
     partners = [("seq", flip_all(seq, k)) for k in range(1, length)]
@@ -142,10 +150,10 @@
 
     def launch(t, stage):
         if stage == 0:
-            local = pltpu.make_async_copy(shards[t], outs[t].at[(seq, *own)], local_sems.at[t])
+            local = pltpu.make_async_copy(shards[t], places[t].at[(seq, *own)], local_sems.at[t])
             local.start()
             made = [
-                copies.start(shards[t], outs[t].at[(seq, *own)], "seq", flip_all(seq, k))
+                copies.start(shards[t], places[t].at[(seq, *own)], "seq", flip_all(seq, k))
                 for k in range(1, length)
             ]
             return made, local
@@ -155,7 +163,7 @@
             for done in orders[part][: stage - 1]:
                 where[1 + done] = slice(None)
             dim = orders[part][stage - 1] if stage <= far else far
-            view = outs[t].at[tuple(where)]
+            view = places[t].at[tuple(where)]
             made.append(copies.start(view, view, "fsdp", flip(group, bits[dim])))
         return made, None
 
@@ -177,6 +185,48 @@
             )
         return made, local
 
+    def project():
+        rows, width = normed_ref.shape
+        query_width = query_ref.shape[1]
+        key_width = window_ref.shape[1]
+
+        def columns(start, size):
+            return held[(slice(None),) * (2 + far) + (slice(None), pl.ds(start, size))].reshape(width, size)
+
+        gain = columns(query_width + key_width, 128).astype(jnp.float32).T[0:1]
+        values = tokens[...].astype(jnp.float32)
+        factor = lax.rsqrt(jnp.mean(values * values, axis=-1, keepdims=True) + EPSILON)
+        normed_ref[...] = (values * factor * gain).astype(normed_ref.dtype)
+        here = pl.ds(back * rows, rows)
+        for start in range(0, key_width, 512):
+            tile = jnp.dot(
+                normed_ref[...], columns(query_width + start, 512), preferred_element_type=jnp.float32
+            )
+            window_ref[here, pl.ds(start, 512)] = tile.astype(window_ref.dtype)
+        sent = []
+        for j in range(1, back + 1):
+            copy = pltpu.make_async_remote_copy(
+                src_ref=window_ref.at[here],
+                dst_ref=window_ref.at[pl.ds((back - j) * rows, rows)],
+                send_sem=key_sems.at[0, j - 1],
+                recv_sem=key_sems.at[1, j - 1],
+                device_id={"seq": lax.rem(seq + j, length)},
+                device_id_type=MESH,
+            )
+            pl.when(seq + j < length)(copy.start)
+            sent.append(copy)
+
+            @pl.when(seq < j)
+            def _(j=j):
+                window_ref[pl.ds((back - j) * rows, rows)] = jnp.zeros((rows, key_width), window_ref.dtype)
+
+        for start in range(0, query_width, 512):
+            tile = jnp.dot(normed_ref[...], columns(start, 512), preferred_element_type=jnp.float32)
+            query_ref[:, pl.ds(start, 512)] = tile.astype(query_ref.dtype)
+        kept = pltpu.make_async_copy(held, outs[0], local_sems.at[0])
+        kept.start()
+        return sent, kept
+
     for step in range(count + stages):
         if step == count:
             expert_waiting = ship_expert()
@@ -191,14 +241,21 @@
                 waiting[t] = None
             if 0 <= stage < stages:
                 waiting[t] = launch(t, stage)
+        if step == stages and back is not None:
+            sent, kept = project()
     made, local = expert_waiting
     for copy in made:
         copy.wait_recv()
     local.wait()
     copies.finish()
-
-
-def gather_dense(shards, expert):
+    if back is not None:
+        for j, copy in enumerate(sent, 1):
+            pl.when(seq >= j)(copy.wait_recv)
+            pl.when(seq + j < length)(copy.wait_send)
+        kept.wait()
+
+
+def gather_dense(shards, expert, tokens, back, key_width):
     length, groups = lax.axis_size("seq"), lax.axis_size("fsdp")
     bits, bit = [], groups // 2
     while bit >= 1:
@@ -208,26 +265,47 @@
     number = count * (length - 1 + 2 * len(bits)) + length - 1
     size = sum(s.size * s.dtype.itemsize for s in shards) * length * groups
     experts, depth, wide = expert.shape
-    *outs, expert_full = pl.pallas_call(
-        functools.partial(gather_dense_kernel, length, bits, count),
+    lead = (length,) + (2,) * len(bits)
+    rows, width = tokens.shape
+    fused = shards[0].shape[0] % 16 == 0
+    extra_in, extra_out, extra_scratch, key_scratch = [], [], [], []
+    if fused:
+        query_width = shards[0].shape[1] - key_width - 128
+        extra_in = [tokens]
+        extra_out = [
+            jax.ShapeDtypeStruct((rows, width), tokens.dtype),
+            jax.ShapeDtypeStruct((rows, query_width), tokens.dtype),
+            jax.ShapeDtypeStruct(((back + 1) * rows, key_width), tokens.dtype),
+        ]
+        extra_scratch = [pltpu.VMEM(lead + shards[0].shape, shards[0].dtype)]
+        key_scratch = [pltpu.SemaphoreType.DMA((2, back))]
+    results = pl.pallas_call(
+        functools.partial(gather_dense_kernel, length, bits, count, back if fused else None),
         out_shape=[
             jax.ShapeDtypeStruct((length,) + (2,) * len(bits) + s.shape, s.dtype) for s in shards
         ]
-        + [jax.ShapeDtypeStruct((experts // PAIR, length * depth, wide), expert.dtype)],
-        in_specs=[pl.BlockSpec(memory_space=pltpu.VMEM)] * count + [pl.BlockSpec(memory_space=pl.ANY)],
-        out_specs=[pl.BlockSpec(memory_space=pl.ANY)] * (count + 1),
-        scratch_shapes=[
+        + [jax.ShapeDtypeStruct((experts // PAIR, length * depth, wide), expert.dtype)]
+        + extra_out,
+        in_specs=[pl.BlockSpec(memory_space=pltpu.VMEM)] * count
+        + [pl.BlockSpec(memory_space=pl.ANY)]
+        + [pl.BlockSpec(memory_space=pltpu.VMEM)] * len(extra_in),
+        out_specs=[pl.BlockSpec(memory_space=pl.ANY)] * (count + 1)
+        + [pl.BlockSpec(memory_space=pltpu.VMEM)] * len(extra_out),
+        scratch_shapes=extra_scratch
+        + [
             pltpu.SemaphoreType.DMA((number,)),
             pltpu.SemaphoreType.DMA((number,)),
             pltpu.SemaphoreType.DMA((count + 1,)),
-        ],
+        ]
+        + key_scratch,
         compiler_params=pltpu.CompilerParams(
             collective_id=0, has_side_effects=True, vmem_limit_bytes=60 * 2**20
         ),
         cost_estimate=pl.CostEstimate(flops=0, bytes_accessed=3 * size, transcendentals=0),
         name="gather_dense",
-    )(*shards, expert)
-    return [out.reshape(-1, out.shape[-1]) for out in outs] + [expert_full]
+    )(*shards, expert, *extra_in)
+    outs = [out.reshape(-1, out.shape[-1]) for out in results[:count]] + [results[count]]
+    return outs + (list(results[count + 1 :]) if fused else [None] * 3)
 
 
 def scatter_dense_kernel(length, bits, count, *refs):
@@ -388,13 +466,19 @@
     return own, partner
 
 
-def gather_rows_kernel(dims, held, rows_ref, pick_ref, slots_ref, buffer, send_sems, recv_sems, local_sem):
+def row_orders(far, light):
+    if light:
+        return [[0] + [1 + (i + k) % (far - 1) for k in range(far - 1)] for i in range(far - 1)]
+    return [[(i + k) % far for k in range(far)] for i in range(far)]
+
+
+def gather_rows_kernel(dims, orders, held, rows_ref, pick_ref, slots_ref, buffer, send_sems, recv_sems, local_sem):
     own, partner = row_places(dims)
     greet(partner)
     copies = Copies(send_sems, recv_sems)
     far = len(dims) - 1
-    pieces = far
-    width = rows_ref.shape[2]
+    pieces = len(orders)
+    width = rows_ref.shape[1] // pieces
     capacity = slots_ref.shape[-2]
 
     def view(piece, done):
@@ -403,13 +487,14 @@
             where[d] = slice(None)
         return buffer.at[(piece, *where)]
 
-    local = pltpu.make_async_copy(rows_ref, buffer.at[(slice(None), *own)], local_sem)
-    local.start()
-    flying = []
+    flying, local = [], []
     for piece in range(pieces):
-        first = piece
-        flying.append(copies.start(rows_ref.at[piece], view(piece, []), *partner[first]))
-    local.wait()
+        cut = rows_ref.at[:, pl.ds(piece * width, width)]
+        flying.append(copies.start(cut, view(piece, []), *partner[orders[piece][0]]))
+        local.append(pltpu.make_async_copy(cut, view(piece, []), local_sem.at[piece]))
+        local[piece].start()
+    for copy in local:
+        copy.wait()
 
     def pick_block(piece, where):
         taken = jnp.dot(
@@ -433,7 +518,7 @@
     for stage in range(1, far + 1):
         for piece in range(pieces):
             flying[piece].wait_recv()
-            order = [(piece + k) % far for k in range(far)]
+            order = orders[piece]
             done = order[:stage]
             ref = view(piece, done)
             flying[piece] = copies.start(ref, ref, *(partner[order[stage]] if stage < far else partner[far]))
@@ -445,24 +530,24 @@
     copies.finish()
 
 
-def gather_rows(rows, pick_low, held, collective_id):
+def gather_rows(rows, pick_low, held, collective_id, light):
     dims = row_dims()
     far = len(dims) - 1
+    orders = row_orders(far, light)
     count, feat = rows.shape
-    width = feat // far
+    width = feat // len(orders)
     sources = 2 ** len(dims)
     capacity = pick_low.shape[1] // held
     lead = (2,) * len(dims)
-    cut = rows.reshape(count, far, width).swapaxes(0, 1)
-    number = far * (far + 1)
-    scratch = [pltpu.VMEM((far,) + lead + (count, width), rows.dtype)]
+    number = len(orders) * (far + 1)
+    scratch = [pltpu.VMEM((len(orders),) + lead + (count, width), rows.dtype)]
     slots = pl.pallas_call(
-        functools.partial(gather_rows_kernel, dims, held),
+        functools.partial(gather_rows_kernel, dims, orders, held),
         out_shape=jax.ShapeDtypeStruct((held,) + lead + (capacity, feat), rows.dtype),
         in_specs=[pl.BlockSpec(memory_space=pltpu.VMEM)] * 2,
         out_specs=pl.BlockSpec(memory_space=pltpu.VMEM),
         scratch_shapes=scratch
-        + [pltpu.SemaphoreType.DMA((number,)), pltpu.SemaphoreType.DMA((number,)), pltpu.SemaphoreType.DMA],
+        + [pltpu.SemaphoreType.DMA((n,)) for n in (number, number, len(orders))],
         compiler_params=pltpu.CompilerParams(
             collective_id=collective_id,
             has_side_effects=True,
@@ -474,21 +559,21 @@
             transcendentals=0,
         ),
         name="gather_rows",
-    )(cut, pick_low.reshape(lead + pick_low.shape[1:]))
+    )(rows, pick_low.reshape(lead + pick_low.shape[1:]))
     return slots.reshape(held, sources * capacity, feat)
 
 
 def scatter_rows_kernel(
-    dims, held, slots_ref, pick_ref, out_ref, mine, other, came_core, came_far, send_sems, recv_sems
+    dims, orders, held, slots_ref, pick_ref, out_ref, mine, other, came_core, came_far, send_sems, recv_sems
 ):
     own, partner = row_places(dims)
     greet(partner)
     copies = Copies(send_sems, recv_sems)
     far = len(dims) - 1
-    pieces = far
-    width = out_ref.shape[2]
+    pieces = len(orders)
+    width = out_ref.shape[1] // pieces
     capacity = slots_ref.shape[-2]
-    count = out_ref.shape[1]
+    count = out_ref.shape[0]
 
     def spread(piece, core, target):
         def body(i, carry):
@@ -530,7 +615,7 @@
 
     for stage in range(far):
         for piece in range(pieces):
-            order = [(piece + k) % far for k in range(far)][::-1]
+            order = orders[piece][::-1]
             fixed = order[:stage]
             flying[piece].wait_recv()
             add_into(piece, fixed, came_core.at[piece] if stage == 0 else came_far[stage - 1].at[piece])
@@ -544,34 +629,35 @@
             )
     for piece in range(pieces):
         flying[piece].wait_recv()
-        out_ref[piece] = mine[(piece, *own[:far])].astype(jnp.float32) + came_far[far - 1][piece].astype(
+        out_ref[:, pl.ds(piece * width, width)] = mine[(piece, *own[:far])].astype(jnp.float32) + came_far[far - 1][piece].astype(
             jnp.float32
         )
     copies.finish()
 
 
-def scatter_rows(slots, pick_low, held, collective_id):
+def scatter_rows(slots, pick_low, held, collective_id, light):
     dims = row_dims()
     far = len(dims) - 1
+    orders = row_orders(far, light)
     count, feat = pick_low.shape[2], slots.shape[2]
-    width = feat // far
+    width = feat // len(orders)
     sources = 2 ** len(dims)
     capacity = pick_low.shape[1] // held
     lead = (2,) * len(dims)
-    number = far * (far + 1)
-
-    scratch = [pltpu.VMEM((far,) + (2,) * far + (count, width), slots.dtype)] * 3
-    scratch += [pltpu.VMEM((far,) + (2,) * (far - 1 - s) + (count, width), slots.dtype) for s in range(far)]
+    number = len(orders) * (far + 1)
+
+    scratch = [pltpu.VMEM((len(orders),) + (2,) * far + (count, width), slots.dtype)] * 3
+    scratch += [pltpu.VMEM((len(orders),) + (2,) * (far - 1 - s) + (count, width), slots.dtype) for s in range(far)]
 
     def kernel(slots_ref, pick_ref, out_ref, mine, other, came_core, *rest):
         came_far, sems = rest[:far], rest[far:]
         scatter_rows_kernel(
-            dims, held, slots_ref, pick_ref, out_ref, mine, other, came_core, came_far, *sems
+            dims, orders, held, slots_ref, pick_ref, out_ref, mine, other, came_core, came_far, *sems
         )
 
-    out = pl.pallas_call(
+    return pl.pallas_call(
         kernel,
-        out_shape=jax.ShapeDtypeStruct((far, count, width), jnp.float32),
+        out_shape=jax.ShapeDtypeStruct((count, feat), jnp.float32),
         in_specs=[pl.BlockSpec(memory_space=pltpu.VMEM)] * 2,
         out_specs=pl.BlockSpec(memory_space=pltpu.VMEM),
         scratch_shapes=scratch + [pltpu.SemaphoreType.DMA((number,)), pltpu.SemaphoreType.DMA((number,))],
@@ -587,7 +673,130 @@
         ),
         name="scatter_rows",
     )(slots.reshape((held,) + lead + (capacity, feat)), pick_low.reshape(lead + pick_low.shape[1:]))
-    return out.swapaxes(0, 1).reshape(count, feat)
+
+
+def allowed_keys(seg_rows_ref, seg_keys_ref, back_rows):
+    shape = (seg_rows_ref.shape[0], seg_keys_ref.shape[1])
+    row = lax.broadcasted_iota(jnp.int32, shape, 0) + back_rows
+    key = lax.broadcasted_iota(jnp.int32, shape, 1)
+    return (key <= row) & (seg_rows_ref[...] == seg_keys_ref[...])
+
+
+def attend_kernel(scale, back_rows, query, key, value, seg_rows, seg_keys, out, log_total):
+    allowed = allowed_keys(seg_rows, seg_keys, back_rows)
+    keys, values = key[...], value[...]
+    lane = lax.broadcasted_iota(jnp.int32, (query.shape[0], 128), 1)
+    logs = jnp.zeros((query.shape[0], 128), jnp.float32)
+    for j in range(query.shape[1] // HEAD):
+        columns = slice(j * HEAD, (j + 1) * HEAD)
+        scores = lax.dot_general(
+            query[:, columns], keys, (((1,), (1,)), ((), ())), preferred_element_type=jnp.float32
+        )
+        scores = jnp.where(allowed, scores * scale, MASKED)
+        top = jnp.max(scores, axis=1, keepdims=True)
+        weights = jnp.exp(scores - top)
+        total = jnp.sum(weights, axis=1, keepdims=True)
+        prob = (weights * (1.0 / total)).astype(jnp.bfloat16)
+        out[:, columns] = jnp.dot(prob, values, preferred_element_type=jnp.float32).astype(out.dtype)
+        logs = jnp.where(lane == j, top + jnp.log(total), logs)
+    log_total[...] = logs
+
+
+def attend_back_kernel(
+    scale, back_rows, query, key, value, seg_rows, seg_keys, log_total, grad, grad_query, grad_key_value
+):
+    allowed = allowed_keys(seg_rows, seg_keys, back_rows)
+    keys, values = key[...], value[...]
+    grad_keys = jnp.zeros(keys.shape, jnp.float32)
+    grad_values = jnp.zeros(values.shape, jnp.float32)
+    for j in range(query.shape[1] // HEAD):
+        columns = slice(j * HEAD, (j + 1) * HEAD)
+        rows, grad_rows = query[:, columns], grad[:, columns]
+        scores = lax.dot_general(
+            rows, keys, (((1,), (1,)), ((), ())), preferred_element_type=jnp.float32
+        )
+        scores = jnp.where(allowed, scores * scale, MASKED)
+        prob = jnp.exp(scores - log_total[:, j : j + 1])
+        grad_prob = lax.dot_general(
+            grad_rows, values, (((1,), (1,)), ((), ())), preferred_element_type=jnp.float32
+        )
+        delta = jnp.sum(prob * grad_prob, axis=1, keepdims=True)
+        grad_scores = (prob * (grad_prob - delta)).astype(jnp.bfloat16)
+        grad_query[:, columns] = (
+            jnp.dot(grad_scores, keys, preferred_element_type=jnp.float32) * scale
+        ).astype(grad_query.dtype)
+        grad_keys = grad_keys + lax.dot_general(
+            grad_scores, rows, (((0,), (0,)), ((), ())), preferred_element_type=jnp.float32
+        )
+        grad_values = grad_values + lax.dot_general(
+            prob.astype(jnp.bfloat16), grad_rows, (((0,), (0,)), ((), ())), preferred_element_type=jnp.float32
+        )
+    grad_key_value[0] = grad_keys * scale
+    grad_key_value[1] = grad_values
+
+
+def attend_specs(tok_rows, window, group_width):
+    return [
+        pl.BlockSpec((tok_rows, group_width), lambda g: (0, g)),
+        pl.BlockSpec((window, HEAD), lambda g: (0, g)),
+        pl.BlockSpec((window, HEAD), lambda g: (0, KV_HEADS + g)),
+        pl.BlockSpec((tok_rows, 1), lambda g: (0, 0)),
+        pl.BlockSpec((1, window), lambda g: (0, 0)),
+    ]
+
+
+def attend(query, key_value, seg_rows, seg_keys, scale):
+    tok_rows, window = query.shape[0], key_value.shape[0]
+    group_width = query.shape[1] // KV_HEADS
+    return pl.pallas_call(
+        functools.partial(attend_kernel, scale, window - tok_rows),
+        grid=(KV_HEADS,),
+        in_specs=attend_specs(tok_rows, window, group_width),
+        out_specs=[
+            pl.BlockSpec((tok_rows, group_width), lambda g: (0, g)),
+            pl.BlockSpec((None, tok_rows, 128), lambda g: (g, 0, 0)),
+        ],
+        out_shape=[
+            jax.ShapeDtypeStruct(query.shape, query.dtype),
+            jax.ShapeDtypeStruct((KV_HEADS, tok_rows, 128), jnp.float32),
+        ],
+        compiler_params=pltpu.CompilerParams(vmem_limit_bytes=32 * 2**20),
+        cost_estimate=pl.CostEstimate(
+            flops=4 * HEADS * tok_rows * window * HEAD,
+            bytes_accessed=8 * query.size,
+            transcendentals=HEADS * tok_rows * window,
+        ),
+        name="attend",
+    )(query, key_value, key_value, seg_rows, seg_keys)
+
+
+def attend_back(query, key_value, seg_rows, seg_keys, log_total, grad, scale):
+    tok_rows, window = query.shape[0], key_value.shape[0]
+    group_width = query.shape[1] // KV_HEADS
+    return pl.pallas_call(
+        functools.partial(attend_back_kernel, scale, window - tok_rows),
+        grid=(KV_HEADS,),
+        in_specs=attend_specs(tok_rows, window, group_width)
+        + [
+            pl.BlockSpec((None, tok_rows, 128), lambda g: (g, 0, 0)),
+            pl.BlockSpec((tok_rows, group_width), lambda g: (0, g)),
+        ],
+        out_specs=[
+            pl.BlockSpec((tok_rows, group_width), lambda g: (0, g)),
+            pl.BlockSpec((2, window, HEAD), lambda g: (0, 0, g)),
+        ],
+        out_shape=[
+            jax.ShapeDtypeStruct(query.shape, query.dtype),
+            jax.ShapeDtypeStruct((2, window, KV_HEADS * HEAD), jnp.float32),
+        ],
+        compiler_params=pltpu.CompilerParams(vmem_limit_bytes=32 * 2**20),
+        cost_estimate=pl.CostEstimate(
+            flops=10 * HEADS * tok_rows * window * HEAD,
+            bytes_accessed=16 * query.size,
+            transcendentals=HEADS * tok_rows * window,
+        ),
+        name="attend_back",
+    )(query, key_value, key_value, seg_rows, seg_keys, log_total, grad)
 
 
 def block(
@@ -615,7 +824,6 @@
     devices = length * groups
     tok_rows = tokens.shape[1]
     seq_len = segment_ids.shape[1]
-    head_group = HEADS // KV_HEADS
     score_scale = 1.0 / math.sqrt(HEAD)
     key_width = KV_HEADS * HEAD
     query_width = HEADS * HEAD
@@ -625,7 +833,9 @@
     gains = jnp.pad(jnp.stack([norm1_gain, norm2_gain], axis=1), ((0, 0), (0, lanes - 2)))
     meta = jnp.concatenate([routes[0].T.astype(F32), gate_weights[0].T], axis=0)
     meta = jnp.pad(meta, ((0, 16 - 2 * TOP), (0, 0)))
-    qkv_full, meta, output_full, gate_up_full, down_full, expert_gate_full = gather_dense(
+    longest = seq_len // 2
+    back = min(length - 1, -(-(longest - 1) // tok_rows))
+    gathered = gather_dense(
         [
             jnp.concatenate([query_weight, key_weight, value_weight, gains], axis=1),
             meta,
@@ -634,7 +844,12 @@
             shared_down_weight,
         ],
         expert_gate_weight,
+        tokens[0],
+        back,
+        2 * key_width,
     )
+    qkv_full, meta, output_full, gate_up_full, down_full, expert_gate_full = gathered[:6]
+    normed_one, query_rows, key_value_all = gathered[6:]
 
     def weight_grad(rows, grad_rows):
         grad = dot(rows, grad_rows, 0, 0).astype(BF16)
@@ -664,41 +879,21 @@
         return full
 
     x_float = tokens[0].astype(F32)
-    normed_one = rms_norm(x_float, gain_one).astype(BF16)
-    qkv_rows = dot(normed_one, qkv_full, 1, 0).astype(BF16)
-    query_rows = qkv_rows[:, :query_width]
-    key_value = [qkv_rows[:, query_width:]]
-    longest = seq_len // 2
-    back = min(length - 1, -(-(longest - 1) // tok_rows))
-    for _ in range(back):
-        key_value.insert(0, shift(key_value[0], "seq", 1))
-    key_value_all = jnp.concatenate(key_value, axis=0)
+    if normed_one is None:
+        normed_one = rms_norm(x_float, gain_one).astype(BF16)
+        qkv_rows = dot(normed_one, qkv_full, 1, 0).astype(BF16)
+        query_rows = qkv_rows[:, :query_width]
+        key_value = [qkv_rows[:, query_width:]]
+        for _ in range(back):
+            key_value.insert(0, shift(key_value[0], "seq", 1))
+        key_value_all = jnp.concatenate(key_value, axis=0)
     up_came = collect_start(expert_up_weight, [key_value_all])
     window = (back + 1) * tok_rows
     seg_padded = jnp.concatenate([jnp.full((back * tok_rows,), -1, jnp.int32), segment_ids[0]])
     seg_keys = lax.dynamic_slice_in_dim(seg_padded, seq_index * tok_rows, window)
     seg_here = seg_keys[back * tok_rows :]
-    positions = back * tok_rows + jnp.arange(tok_rows, dtype=jnp.int32)
-    key_positions = jnp.arange(window, dtype=jnp.int32)
-    allowed = (key_positions[None, :] <= positions[:, None]) & (seg_keys[None, :] == seg_here[:, None])
-    query_heads = query_rows.reshape(tok_rows, KV_HEADS, head_group, HEAD)
-    key_heads = key_value_all[:, :key_width].reshape(window, KV_HEADS, HEAD)
-    value_heads = key_value_all[:, key_width:].reshape(window, KV_HEADS, HEAD)
-
-    def all_scores():
-        raw_scores = jnp.einsum(
-            "thgd,jhd->hgtj", query_heads, key_heads, preferred_element_type=F32
-        )
-        return jnp.where(allowed[None, None], raw_scores * score_scale, MASKED)
-
-    scores = all_scores()
-    log_total = jax.nn.logsumexp(scores, axis=-1, keepdims=True)
-    prob_low = jnp.exp(scores - log_total).astype(BF16)
-    attended = (
-        jnp.einsum("hgtj,jhd->thgd", prob_low, value_heads, preferred_element_type=F32)
-        .reshape(tok_rows, query_width)
-        .astype(BF16)
-    )
+    seg_rows, seg_line = seg_here[:, None], seg_keys[None, :]
+    attended, log_total = attend(query_rows, key_value_all, seg_rows, seg_line, score_scale)
     mixed_rows = x_float + dot(attended, output_full, 1, 0)
     normed_two = rms_norm(mixed_rows, gain_two).astype(BF16)
 
@@ -724,7 +919,7 @@
     chosen_low = chosen.astype(BF16).reshape(sources, num_held * capacity, tok_rows)
     gate_canonical = jnp.moveaxis(gate_slots, 0, 1).reshape(num_held, sources * capacity, 1)
     down_came = collect_start(expert_down_weight, [normed_two])
-    slot_rows = gather_rows(normed_two, chosen_low, num_held, 1)
+    slot_rows = gather_rows(normed_two, chosen_low, num_held, 1, False)
 
     gate_up = dot(normed_two, gate_up_full, 1, 0)
     shared_gate, shared_up = gate_up[:, :shared_width], gate_up[:, shared_width:]
@@ -739,7 +934,7 @@
         expert_down_weight, [after(came, expert_hidden) for came in down_came]
     )
     expert_output = (gate_canonical * batch_dot(expert_hidden, expert_down_full, 2, 1)).astype(BF16)
-    routed = scatter_rows(expert_output, chosen_low, num_held, 2)
+    routed = scatter_rows(expert_output, chosen_low, num_held, 2, False)
 
     output = mixed_rows + shared_out + routed
     block_output = output.astype(BF16)
@@ -747,7 +942,7 @@
     grad_out = valid_rows * (output - teacher[0].astype(F32))
     grad_low = grad_out.astype(BF16)
 
-    grad_slots = gather_rows(grad_low, chosen_low, num_held, 3)
+    grad_slots = gather_rows(grad_low, chosen_low, num_held, 3, False)
     grad_slots = (gate_canonical * grad_slots.astype(F32)).astype(BF16)
 
     def expert_grad(left, right, wait):
@@ -760,22 +955,20 @@
         return own
 
     def expert_sum(own, wait):
-        own = [after(part, *wait).astype(F32) for part in own]
-        same = sum(own[k] for k in range(0, length, PAIR))
-        crossed = sum(own[k] for k in range(1, length, PAIR))
-        return jnp.concatenate(
-            [jnp.where(side == 0, same, crossed), jnp.where(side == 0, crossed, same)], axis=0
-        )
+        own = [after(part, *wait) for part in own]
+        same = sum(own[k].astype(F32) for k in range(0, length, PAIR))
+        crossed = sum(own[k].astype(F32) for k in range(1, length, PAIR))
+        first = (jnp.arange(PAIR) == side)[:, None, None, None]
+        return jnp.where(first, same[None], crossed[None]).reshape(num_local, *same.shape[1:])
 
     expert_down_own = expert_grad(expert_hidden, grad_slots, [])
     grad_hidden = batch_dot(grad_slots, expert_down_full, 2, 2)
     grad_gate_rows, grad_up_rows = swiglu_backward(expert_gate_rows, expert_up_rows, grad_hidden)
+    expert_gate_own = expert_grad(slot_rows, grad_gate_rows, [])
     grad_input = (
         batch_dot(grad_gate_rows, expert_gate_full, 2, 2) + batch_dot(grad_up_rows, expert_up_full, 2, 2)
     ).astype(BF16)
-    grad_routed = scatter_rows(grad_input, chosen_low, num_held, 4)
-    expert_gate_own = expert_grad(slot_rows, grad_gate_rows, [grad_routed])
-
+    grad_routed = scatter_rows(grad_input, chosen_low, num_held, 4, True)
     grad_shidden = dot(grad_low, down_full, 1, 1)
     grad_sgate_rows, grad_sup_rows = swiglu_backward(shared_gate, shared_up, grad_shidden)
     grad_gate_up = jnp.concatenate([grad_sgate_rows, grad_sup_rows], axis=1)
@@ -786,30 +979,10 @@
     grad_mixed_low = grad_mixed.astype(BF16)
 
     grad_attended = dot(grad_mixed_low, output_full, 1, 1).astype(BF16)
-    grad_att_heads = grad_attended.reshape(tok_rows, KV_HEADS, head_group, HEAD)
-    prob_full = jnp.exp(all_scores() - log_total)
-    prob_back = prob_full.astype(BF16)
-    grad_prob = jnp.einsum(
-        "thgd,jhd->hgtj", grad_att_heads, value_heads, preferred_element_type=F32
+    grad_query, grad_key_value = attend_back(
+        query_rows, key_value_all, seg_rows, seg_line, log_total, grad_attended, score_scale
     )
-    grad_values = jnp.einsum(
-        "hgtj,thgd->jhd", prob_back, grad_att_heads, preferred_element_type=F32
-    ).reshape(window, key_width)
-    row_delta = jnp.sum(prob_full * grad_prob, axis=-1, keepdims=True)
-    grad_scores = (prob_full * (grad_prob - row_delta)).astype(BF16)
-    grad_query = (
-        (
-            jnp.einsum("hgtj,jhd->thgd", grad_scores, key_heads, preferred_element_type=F32)
-            * score_scale
-        )
-        .reshape(tok_rows, query_width)
-        .astype(BF16)
-    )
-    grad_keys = (
-        jnp.einsum("hgtj,thgd->jhd", grad_scores, query_heads, preferred_element_type=F32)
-        * score_scale
-    ).reshape(window, key_width)
-    grad_key_value = jnp.concatenate([grad_keys, grad_values], axis=1)
+    grad_key_value = jnp.concatenate([grad_key_value[0], grad_key_value[1]], axis=1)
     total = grad_key_value[:tok_rows]
     for step in range(1, back + 1):
         came = shift(total.astype(BF16), "seq", -1)

time: 1020 us -> 1010 us (level)
  Pallas kernels: 591 us -> 622 us
  matrix products: 132 us -> 108 us
  starting transfers between devices: 49.6 us -> 71.3 us
  other arithmetic: 45.7 us -> 30.3 us
  local copies, waits for them, and re-layouts: 57.9 us -> 44.9 us
    ppermute x15, starting transfers between devices: 22.7 us -> 68.5 us  [exchange(): return lax.ppermute(values, axis, [(i, i ^ bit) for i in range(count)])]
    pallas_call x4 -> x6, Pallas kernels: 290 us -> 323 us  [the longest x2 153 us: gather_rows(): pl.pallas_call(functools.partial(gather_rows_kernel, dims, orders, held),...]
    ppermute x4 -> x2, starting transfers between devices: 26.8 us -> 2.85 us  [shift(): return lax.ppermute(values, axis, pairs)]
    dot_general x6 -> x0, matrix products: 23.9 us -> none  [the longest x1 7.75 us: block(): jnp.einsum('hgtj,thgd->jhd', prob_back, grad_att_heads, preferred_element...]
    pallas_call x1, Pallas kernels: 158 us -> 141 us  [scatter_dense(): pl.pallas_call(functools.partial(scatter_dense_kernel, length, bits, coun...]
    pallas_call x1, Pallas kernels: 143 us -> 159 us  [gather_dense(): pl.pallas_call(functools.partial(gather_dense_kernel, length, bits, count...]
    reshape x7 -> x0, local copies, waits for them, and re-layouts: 13.8 us -> none  [the longest x2 6.31 us: scatter_rows(): return out.swapaxes(0, 1).reshape(count, feat)]
    ppermute x15, waiting for transfers between devices: 79.8 us -> 66 us  [exchange(): return lax.ppermute(values, axis, [(i, i ^ bit) for i in range(count)])]
  transfers between devices with their start and end apart: 19 -> 17, of which waited for: 7 -> 6; matrix products, arithmetic and copies ran while one was open for 8% -> 8% of each run, Pallas kernels for 26% -> 25%
where the time goes in v2:
time: 1010 us; the launch traced here: 999 us
  Pallas kernels  622 us (62%)
  waiting for transfers between devices  121 us (12%)
  matrix products  108 us (11%)
  starting transfers between devices  71.3 us (7%)
  local copies, waits for them, and re-layouts  44.9 us (4%)
  other arithmetic  30.3 us (3%)
    pallas_call x1, Pallas kernels, gather_dense(): pl.pallas_call(functools.partial(gather_dense_kernel, length, bits, count...  159 us
    pallas_call x2, Pallas kernels, gather_rows(): pl.pallas_call(functools.partial(gather_rows_kernel, dims, orders, held),...  153 us
    pallas_call x2, Pallas kernels, scatter_rows(): pl.pallas_call(kernel, out_shape=jax.ShapeDtypeStruct((count, feat), jnp....  150 us
    pallas_call x1, Pallas kernels, scatter_dense(): pl.pallas_call(functools.partial(scatter_dense_kernel, length, bits, coun...  141 us
    ppermute x15, starting transfers between devices, exchange(): return lax.ppermute(values, axis, [(i, i ^ bit) for i in range(count)])  68.5 us
    ppermute x15, waiting for transfers between devices, exchange(): return lax.ppermute(values, axis, [(i, i ^ bit) for i in range(count)])  66 us
    dot_general x9, matrix products, batch_dot(): lax.dot_general(left, right, (((left_dim,), (right_dim,)), ((0,), (0,))),...  60.3 us
    ppermute x2, waiting for transfers between devices, shift(): return lax.ppermute(values, axis, pairs)  54.5 us
  transfers between devices with their start and end apart: 17, of which 6 were waited for; matrix products, arithmetic and copies ran while one was open for 8% of the time, Pallas kernels for 25%

profile of v2, /device:TPU:0, one launch (start us, length us, event | category | flops | bytes accessed | tf_op | source)
XLA Modules:
  0.0 999.0 jit_solution(14662171376634464195)
XLA Ops:
  3.5 1.6 pad_maximum_fusion.7.refs_3_
  5.1 1.7 fusion.33.refs_0_
  6.8 159.0 %gather_dense.1 = (bf16[4,2,2,2,48,2688]{5,4,3,2,1,0:T(8,128)(2,1)}, f32[4,2,2,2,16,256]{5,4,3,2,1,0:T(8,128)}, bf16[4,2,2,2,48,1536]{5,4,3,2,1,0:T(8,128)(2,1)}...) custom-call(bf16[48,2688]{1,0:T(8,128)(2,1)} %fusion.33.refs_0_, ...), custom_call_target="tpu_custom_call" | custom-call | bytes 68812800 | tf_op jit(solution)/shard_map/gather_dense/pallas_call | solution.py:282
  165.8 2.8 constant_dynamic-slice_fusion.13
  168.6 22.6 %collective-permute-start.2 = (bf16[2,384,512]{2,1,0:T(8,128)(2,1)}, bf16[2,384,512]{2,1,0:T(8,128)(2,1)}, u32[]{:S(2)}, u32[]{:S(2)}) collective-permute-start(bf16[2,384,512]{2,1,0:T(8,128)(2,1)} %get-tuple-element.123), channel_id=1, source_target_pairs={{0,24},{8,16},{16,8},{24,0},{1,25},{9,17},{17,9},{25,1},{2,26},{10... | collective-permute-start | bytes 2359304 | tf_op jit(solution)/shard_map/ppermute | solution.py:27
  191.2 29.6 %collective-permute-start = (bf16[2,384,512]{2,1,0:T(8,128)(2,1)}, bf16[2,384,512]{2,1,0:T(8,128)(2,1)}, u32[]{:S(2)}, u32[]{:S(2)}) collective-permute-start(bf16[2,384,512]{2,1,0:T(8,128)(2,1)} %get-tuple-element.123), channel_id=1, source_target_pairs={{0,8},{8,0},{16,24},{24,16},{1,9},{9,1},{17,25},{25,17},{2,10},{10... | collective-permute-start | bytes 2359304 | tf_op jit(solution)/shard_map/ppermute | solution.py:27
  223.0 8.1 attend.1
  231.1 4.0 multiply_reduce_fusion.2
  235.4 1.7 copy-done.26
  239.3 3.5 collective-permute-start.1
  248.3 4.6 fusion.45
  255.1 97.1 %gather_rows.2 = bf16[2,2,2,2,2,64,1536]{6,5,4,3,2,1,0:T(8,128)(2,1)S(1)} custom-call(bf16[256,1536]{1,0:T(8,128)(2,1)S(1)} %multiply_convert_fusion.3.rows_ref, bf16[2,2,2,2,128,256]{5,4,3,2,1,0:T(8,128)(2,1)S(1)} %and_convert_fusion.pick_ref), custom_call_target="tpu_custom_call" | custom-call | flops 1610612736 | bytes 37748736 | tf_op jit(solution)/shard_map/gather_rows/pallas_call | solution.py:544
  352.2 2.6 copy-done.3
  356.4 1.9 broadcast_in_dim.155
  359.3 3.0 fusion.46
  362.3 3.4 fusion.47
  365.9 1.8 constant_dynamic-update-slice_fusion.5
  370.1 5.3 multiply_convert_fusion.2
  375.4 25.5 %collective-permute-done.4 = bf16[2,128,1536]{2,1,0:T(8,128)(2,1)S(1)} collective-permute-done((bf16[2,128,1536]{2,1,0:T(8,128)(2,1)S(1)}, bf16[2,128,1536]{2,1,0:T(8,128)(2,1)S(1)}, u32[]{:S(2)}, u32[]{:S(2)}) %collective-permute-start.4) | collective-permute-done | bytes 786464 | tf_op jit(solution)/shard_map/ppermute | solution.py:27
  400.9 2.1 constant_dynamic-update-slice_fusion.2
  403.9 2.1 constant_dynamic-update-slice_fusion
  406.0 5.9 multiply_convert_fusion
  412.0 61.2 %scatter_rows.2 = f32[256,1536]{1,0:T(8,128)S(1)} custom-call(bf16[2,2,2,2,2,64,1536]{6,5,4,3,2,1,0:T(8,128)(2,1)S(1)} %bitcast.112, bf16[2,2,2,2,128,256]{5,4,3,2,1,0:T(8,128)(2,1)S(1)} %and_convert_fusion.pick_ref), custom_call_target="tpu_custom_call" | custom-call | flops 1610612736 | bytes 37748736 | tf_op jit(solution)/shard_map/scatter_rows/pallas_call | solution.py:658
  473.2 1.8 fusion.26
  476.3 2.3 fusion.18
  478.6 2.7 convolution_convert_fusion.3
  481.3 56.1 %gather_rows.3 = bf16[2,2,2,2,2,64,1536]{6,5,4,3,2,1,0:T(8,128)(2,1)S(1)} custom-call(bf16[256,1536]{1,0:T(8,128)(2,1)S(1)} %get-tuple-element.98.rows_ref, bf16[2,2,2,2,128,256]{5,4,3,2,1,0:T(8,128)(2,1)S(1)} %and_convert_fusion.pick_ref), custom_call_target="tpu_custom_call" | custom-call | flops 1610612736 | bytes 37748736 | tf_op jit(solution)/shard_map/gather_rows/pallas_call | solution.py:544
  537.4 3.9 fusion
  541.2 8.5 convolution_convert_fusion.4
  549.8 11.1 %multiply_convert_fusion.1 = (bf16[2,1024,512]{2,1,0:T(8,128)(2,1)S(1)}, bf16[2,1024,512]{2,1,0:T(8,128)(2,1)S(1)}) fusion(f32[2,1024,512]{2,1,0:T(8,128)} %copy-done.62, f32[2,1024,512]{2,1,0:T(8,128)} %get-tuple-element.137, bf16[2,1024,1536]{2,1,0:T(8,128)(2,1)} %fusion, bf16[2,512,1536]{2,1,0:T(8,128)(2,1)} %constant_dynamic-update-slice_fusion), kind=kOutput, calls=%fused_computation.13 | convolution fusion | flops 3235905536 | bytes 22020096 | tf_op jit(solution)/shard_map/dot_general | solution.py:47
  560.9 4.9 convolution_convert_fusion.6
  565.8 6.4 fusion.48
  572.3 5.0 convolution_convert_fusion.5
  577.3 9.6 add_convert_fusion
  587.0 88.6 %scatter_rows.3 = f32[256,1536]{1,0:T(8,128)S(1)} custom-call(bf16[2,2,2,2,2,64,1536]{6,5,4,3,2,1,0:T(8,128)(2,1)S(1)} %bitcast.110, bf16[2,2,2,2,128,256]{5,4,3,2,1,0:T(8,128)(2,1)S(1)} %and_convert_fusion.pick_ref), custom_call_target="tpu_custom_call" | custom-call | flops 1610612736 | bytes 37748736 | tf_op jit(solution)/shard_map/scatter_rows/pallas_call | solution.py:658
  675.7 5.8 multiply_reduce_fusion
  681.6 1.5 fusion.8
  683.1 1.5 convolution_convert_fusion.7.grad
  685.2 11.6 %attend_back.1 = (bf16[256,1536]{1,0:T(8,128)(2,1)S(1)}, f32[2,768,512]{2,1,0:T(8,128)S(1)}) custom-call(bf16[256,1536]{1,0:T(8,128)(2,1)S(1)} %copy-done.7, bf16[768,1024]{1,0:T(8,128)(2,1)S(1)} %copy-done.6, bf16[768,1024]{1,0:T(8,128)(2,1)S(1)} %copy-done.6, s32[256,1]{1,0:T(8,128)S(1)} %copy.86.seg_rows, s32[1,768]{1,0:T(1,128)S(1)} %broadcast_in_dim.149.seg_keys, ...), custom_call_target="tpu_custom_call" | custom-call | flops 3019898880 | bytes 6291456 | tf_op jit(solution)/shard_map/attend_back/pallas_call | solution.py:776
  697.3 1.6 collective-permute-start.6
  700.2 1.8 constant_dynamic-slice_fusion.1
  703.3 1.9 collective-permute-start.14
  705.2 4.5 convolution_convert_fusion.1
  709.8 21.1 %collective-permute-done.6 = bf16[256,1024]{1,0:T(8,128)(2,1)S(1)} collective-permute-done((bf16[256,1024]{1,0:T(8,128)(2,1)S(1)}, bf16[256,1024]{1,0:T(8,128)(2,1)S(1)}, u32[]{:S(2)}, u32[]{:S(2)}) %collective-permute-start.6) | collective-permute-done | bytes 524320 | tf_op jit(solution)/shard_map/ppermute | solution.py:33
  732.3 1.7 constant_dynamic-slice_fusion.9
  734.1 2.6 collective-permute-start.9
  736.8 5.2 convolution_convert_fusion.2
  742.1 33.4 %collective-permute-done.7 = bf16[256,1024]{1,0:T(8,128)(2,1)S(1)} collective-permute-done((bf16[256,1024]{1,0:T(8,128)(2,1)S(1)}, bf16[256,1024]{1,0:T(8,128)(2,1)S(1)}, u32[]{:S(2)}, u32[]{:S(2)}) %collective-permute-start.7) | collective-permute-done | bytes 524320 | tf_op jit(solution)/shard_map/ppermute | solution.py:33
  775.7 6.7 fusion.14
  782.4 1.4 collective-permute-start.16
  783.8 6.7 convolution_convert_fusion
  790.7 2.8 copy-done
  793.5 2.3 copy-done.1
  795.8 140.7 %scatter_dense.1 = (f32[48,2048]{1,0:T(8,128)S(1)}, f32[48,2560]{1,0:T(8,128)S(1)}, f32[48,1536]{1,0:T(8,128)S(1)}, f32[32,1536]{1,0:T(8,128)S(1)}, f32[8,128]{1,0:T(8,128)S(1)}) custom-call(bf16[4,2,2,2,48,2048]{5,4,3,2,1,0:T(8,128)(2,1)S(1)} %bitcast.108, bf16[4,2,2,2,48,2560]{5,4,3,2,1,0:T(8,128)(2,1)} %bitcast.120, ...), custom_call_target="tpu_custom_call" | custom-call | bytes 66453504 | tf_op jit(solution)/shard_map/scatter_dense/pallas_call | solution.py:433
  936.8 1.6 collective-permute-start.13
  938.4 2.9 collective-permute-start.11
  944.0 1.8 convert_add_fusion.1
  945.8 2.1 bitcast_select_fusion
  947.9 2.2 convert_add_fusion.5
  950.7 1.6 fusion.10
  952.3 6.9 collective-permute-done.13
  959.2 7.4 collective-permute-done.12
  966.5 26.3 %collective-permute-done.11 = bf16[2,384,512]{2,1,0:T(8,128)(2,1)S(1)} collective-permute-done((bf16[2,384,512]{2,1,0:T(8,128)(2,1)S(1)}, bf16[2,384,512]{2,1,0:T(8,128)(2,1)S(1)}, u32[]{:S(2)}, u32[]{:S(2)}) %collective-permute-start.11) | collective-permute-done | bytes 786464 | tf_op jit(solution)/shard_map/ppermute | solution.py:27
  993.3 4.0 bitcast_select_fusion.1
  (218 shorter events, 33.3 us)
Async XLA Ops:
  6.8 214.0 %copy-start.56 = (s32[1,1024]{1,0:T(1,128)S(1)}, s32[1,1024]{1,0:T(1,128)}, u32[]{:S(2)}) copy-start(s32[1,1024]{1,0:T(1,128)} %param.21) | copy-start | bytes 12292
  165.8 57.2 %copy-start.5 = (bf16[768,1024]{1,0:T(8,128)(2,1)S(1)}, bf16[768,1024]{1,0:T(8,128)(2,1)}, u32[]{:S(2)}) copy-start(bf16[768,1024]{1,0:T(8,128)(2,1)} %get-tuple-element.54.key.value) | copy-start | bytes 4718596
  165.8 57.2 %copy-start.7 = (bf16[256,1536]{1,0:T(8,128)(2,1)S(1)}, bf16[256,1536]{1,0:T(8,128)(2,1)}, u32[]{:S(2)}) copy-start(bf16[256,1536]{1,0:T(8,128)(2,1)} %get-tuple-element.53.query) | copy-start | bytes 2359300
  168.6 197.2 %collective-permute-start.2 = (bf16[2,384,512]{2,1,0:T(8,128)(2,1)}, bf16[2,384,512]{2,1,0:T(8,128)(2,1)}, u32[]{:S(2)}, u32[]{:S(2)}) collective-permute-start(bf16[2,384,512]{2,1,0:T(8,128)(2,1)} %get-tuple-element.123), channel_id=1, source_target_pairs={{0,24},{8,16},{16,8},{24,0},{1,25},{9,17},{17,9},{25,1},{2,26},{10... | collective-permute-start | bytes 2359304 | tf_op jit(solution)/shard_map/ppermute | solution.py:27
  191.2 174.6 %collective-permute-start = (bf16[2,384,512]{2,1,0:T(8,128)(2,1)}, bf16[2,384,512]{2,1,0:T(8,128)(2,1)}, u32[]{:S(2)}, u32[]{:S(2)}) collective-permute-start(bf16[2,384,512]{2,1,0:T(8,128)(2,1)} %get-tuple-element.123), channel_id=1, source_target_pairs={{0,8},{8,0},{16,24},{24,16},{1,9},{9,1},{17,25},{25,17},{2,10},{10... | collective-permute-start | bytes 2359304 | tf_op jit(solution)/shard_map/ppermute | solution.py:27
  222.4 8.7 copy-start.20
  231.1 4.0 copy-start.8
  235.1 3.3 copy-start.14
  235.1 3.3 copy-start.54
  235.2 7.7 copy-start.21
  237.1 8.6 copy-start.58
  238.4 137.1 %collective-permute-start.5 = (bf16[2,128,1536]{2,1,0:T(8,128)(2,1)}, bf16[2,128,1536]{2,1,0:T(8,128)(2,1)}, u32[]{:S(2)}, u32[]{:S(2)}) collective-permute-start(bf16[2,128,1536]{2,1,0:T(8,128)(2,1)} %get-tuple-element.121), channel_id=1, source_target_pairs={{0,24},{8,16},{16,8},{24,0},{1,25},{9,17},{17,9},{25,1},{2,26},{10... | collective-permute-start | bytes 2359304 | tf_op jit(solution)/shard_map/ppermute | solution.py:27
  239.3 161.6 %collective-permute-start.3 = (bf16[2,128,1536]{2,1,0:T(8,128)(2,1)}, bf16[2,128,1536]{2,1,0:T(8,128)(2,1)}, u32[]{:S(2)}, u32[]{:S(2)}) collective-permute-start(bf16[2,128,1536]{2,1,0:T(8,128)(2,1)} %get-tuple-element.121), channel_id=1, source_target_pairs={{0,8},{8,0},{16,24},{24,16},{1,9},{9,1},{17,25},{25,17},{2,10},{10... | collective-permute-start | bytes 2359304 | tf_op jit(solution)/shard_map/ppermute | solution.py:27
  239.3 126.5 %collective-permute-start.1 = (bf16[2,384,512]{2,1,0:T(8,128)(2,1)}, bf16[2,384,512]{2,1,0:T(8,128)(2,1)}, u32[]{:S(2)}, u32[]{:S(2)}) collective-permute-start(bf16[2,384,512]{2,1,0:T(8,128)(2,1)} %get-tuple-element.122), channel_id=1, source_target_pairs={{0,16},{8,24},{16,0},{24,8},{1,17},{9,25},{17,1},{25,9},{2,18},{10... | collective-permute-start | bytes 2359304 | tf_op jit(solution)/shard_map/ppermute | solution.py:27
  354.8 7.4 slice-start
  355.0 3.3 copy-start.27
  356.4 5.8 slice-start.1
  362.3 3.4 copy-start.43
  365.7 9.7 copy-start.62
  365.8 35.2 %collective-permute-start.4 = (bf16[2,128,1536]{2,1,0:T(8,128)(2,1)S(1)}, bf16[2,128,1536]{2,1,0:T(8,128)(2,1)S(1)}, u32[]{:S(2)}, u32[]{:S(2)}) collective-permute-start(bf16[2,128,1536]{2,1,0:T(8,128)(2,1)S(1)} %copy-done.43), channel_id=1, source_target_pairs={{0,16},{8,24},{16,0},{24,8},{1,17},{9,25},{17,1},{25,9},{2,18},{10... | collective-permute-start | bytes 2359304 | tf_op jit(solution)/shard_map/ppermute | solution.py:27
  370.1 5.4 copy-start.19
  375.4 36.5 %copy-start.63 = (bf16[2,1024,512]{2,1,0:T(8,128)(2,1)}, bf16[2,1024,512]{2,1,0:T(8,128)(2,1)S(1)}, u32[]{:S(2)}) copy-start(bf16[2,1024,512]{2,1,0:T(8,128)(2,1)S(1)} %get-tuple-element.136) | copy-start | bytes 6291460
  375.4 30.6 %copy-start.47 = (f32[2,1024]{1,0:T(2,128)S(1)}, f32[2,1024]{1,0:T(2,128)}, u32[]{:S(2)}) copy-start(f32[2,1024]{1,0:T(2,128)} %mul.265) | copy-start | bytes 24580
  411.9 61.3 %copy-start.15 = (f32[256,1536]{1,0:T(8,128)S(1)}, f32[256,1536]{1,0:T(8,128)}, u32[]{:S(2)}) copy-start(f32[256,1536]{1,0:T(8,128)} %copy-done.14) | copy-start | bytes 4718596
  411.9 61.3 %copy-start.34 = (bf16[1,256,1536]{2,1,0:T(8,128)(2,1)S(1)}, bf16[1,256,1536]{2,1,0:T(8,128)(2,1)}, u32[]{:S(2)}) copy-start(bf16[1,256,1536]{2,1,0:T(8,128)(2,1)} %param.19) | copy-start | bytes 2359300
  412.0 61.3 %copy-start.50 = (f32[1,256]{1,0:T(1,128)S(1)}, f32[1,256]{1,0:T(1,128)}, u32[]{:S(2)}) copy-start(f32[1,256]{1,0:T(1,128)} %convert_element_type.184) | copy-start | bytes 3076
  560.9 11.4 %copy-start.36 = (bf16[2,1024,512]{2,1,0:T(8,128)(2,1)}, bf16[2,1024,512]{2,1,0:T(8,128)(2,1)S(1)}, u32[]{:S(2)}) copy-start(bf16[2,1024,512]{2,1,0:T(8,128)(2,1)S(1)} %get-tuple-element.100) | copy-start | bytes 6291460
  560.9 5.0 copy-start.61
  586.9 88.7 %copy-start.16 = (f32[256,1536]{1,0:T(8,128)S(1)}, f32[256,1536]{1,0:T(8,128)}, u32[]{:S(2)}) copy-start(f32[256,1536]{1,0:T(8,128)} %copy-done.14) | copy-start | bytes 4718596
  587.0 88.6 %copy-start.44 = (bf16[256,1024]{1,0:T(8,128)(2,1)S(1)}, bf16[256,1024]{1,0:T(8,128)(2,1)}, u32[]{:S(2)}) copy-start(bf16[256,1024]{1,0:T(8,128)(2,1)} %get-tuple-element.116) | copy-start | bytes 1572868
  587.0 88.6 %copy-start.45 = (bf16[256,1024]{1,0:T(8,128)(2,1)S(1)}, bf16[256,1024]{1,0:T(8,128)(2,1)}, u32[]{:S(2)}) copy-start(bf16[256,1024]{1,0:T(8,128)(2,1)} %get-tuple-element.117) | copy-start | bytes 1572868
  587.0 88.6 %copy-start.49 = (f32[256]{0:T(256)S(1)}, f32[256]{0:T(256)}, u32[]{:S(2)}) copy-start(f32[256]{0:T(256)} %copy-done.48) | copy-start | bytes 3076
  587.0 96.1 %slice-start.2 = ((s8[4718592]{0:T(1024)(128)(4,1)}), s8[4194304]{0:T(1024)(128)(4,1)S(1)}, s32[]{:S(2)}) async-start(s8[4718592]{0:T(1024)(128)(4,1)} %bitcast.140), calls=%async_computation.2 | async-start | bytes 8388608
  675.6 5.9 copy-start.55
  675.7 5.9 copy-start.25
  675.7 5.9 copy-start.35
  675.7 5.9 copy-start.51
  675.7 7.4 slice-start.3
  696.8 78.8 %copy-start.4 = (bf16[256,1536]{1,0:T(8,128)(2,1)}, bf16[256,1536]{1,0:T(8,128)(2,1)S(1)}, u32[]{:S(2)}) copy-start(bf16[256,1536]{1,0:T(8,128)(2,1)S(1)} %get-tuple-element.71) | copy-start | bytes 2359300
  697.2 33.7 %copy-start.10 = (f32[768,512]{1,0:T(8,128)}, f32[768,512]{1,0:T(8,128)S(1)}, u32[]{:S(2)}) copy-start(f32[768,512]{1,0:T(8,128)S(1)} %get-tuple-element.114) | copy-start | bytes 4718596
  697.2 33.7 %copy-start.12 = (f32[768,512]{1,0:T(8,128)}, f32[768,512]{1,0:T(8,128)S(1)}, u32[]{:S(2)}) copy-start(f32[768,512]{1,0:T(8,128)S(1)} %get-tuple-element.115) | copy-start | bytes 4718596
  697.3 33.6 %collective-permute-start.6 = (bf16[256,1024]{1,0:T(8,128)(2,1)S(1)}, bf16[256,1024]{1,0:T(8,128)(2,1)S(1)}, u32[]{:S(2)}, u32[]{:S(2)}) collective-permute-start(bf16[256,1024]{1,0:T(8,128)(2,1)S(1)} %fusion.23), channel_id=1, source_target_pairs={{8,0},{16,8},{24,16},{9,1},{17,9},{25,17},{10,2},{18,10},{26,18},{... | collective-permute-start | bytes 1572872 | tf_op jit(solution)/shard_map/ppermute | solution.py:33
  702.0 80.4 %collective-permute-start.15 = (bf16[2,128,1536]{2,1,0:T(8,128)(2,1)}, bf16[2,128,1536]{2,1,0:T(8,128)(2,1)S(1)}, u32[]{:S(2)}, u32[]{:S(2)}) collective-permute-start(bf16[2,128,1536]{2,1,0:T(8,128)(2,1)} %get-tuple-element.104), channel_id=1, source_target_pairs={{0,8},{8,0},{16,24},{24,16},{1,9},{9,1},{17,25},{25,17},{2,10},{10... | collective-permute-start | bytes 2359304 | tf_op jit(solution)/shard_map/ppermute | solution.py:27
  703.3 233.5 %collective-permute-start.14 = (bf16[2,128,1536]{2,1,0:T(8,128)(2,1)}, bf16[2,128,1536]{2,1,0:T(8,128)(2,1)}, u32[]{:S(2)}, u32[]{:S(2)}) collective-permute-start(bf16[2,128,1536]{2,1,0:T(8,128)(2,1)} %get-tuple-element.105), channel_id=1, source_target_pairs={{0,16},{8,24},{16,0},{24,8},{1,17},{9,25},{17,1},{25,9},{2,18},{10... | collective-permute-start | bytes 2359304 | tf_op jit(solution)/shard_map/ppermute | solution.py:27
  709.7 22.6 %copy-start.30 = (bf16[2,1536,512]{2,1,0:T(8,128)(2,1)S(1)}, bf16[2,1536,512]{2,1,0:T(8,128)(2,1)}, u32[]{:S(2)}) copy-start(bf16[2,1536,512]{2,1,0:T(8,128)(2,1)} %convolution_convert_fusion.6) | copy-start | bytes 9437188
  731.0 5.7 copy-start.52
  731.0 44.4 %collective-permute-start.7 = (bf16[256,1024]{1,0:T(8,128)(2,1)S(1)}, bf16[256,1024]{1,0:T(8,128)(2,1)S(1)}, u32[]{:S(2)}, u32[]{:S(2)}) collective-permute-start(bf16[256,1024]{1,0:T(8,128)(2,1)S(1)} %fusion.21), channel_id=1, source_target_pairs={{8,0},{16,8},{24,16},{9,1},{17,9},{25,17},{10,2},{18,10},{26,18},{... | collective-permute-start | bytes 1572872 | tf_op jit(solution)/shard_map/ppermute | solution.py:33
  734.0 204.3 %collective-permute-start.10 = (bf16[2,384,512]{2,1,0:T(8,128)(2,1)}, bf16[2,384,512]{2,1,0:T(8,128)(2,1)}, u32[]{:S(2)}, u32[]{:S(2)}) collective-permute-start(bf16[2,384,512]{2,1,0:T(8,128)(2,1)} %get-tuple-element.111), channel_id=1, source_target_pairs={{0,24},{8,16},{16,8},{24,0},{1,25},{9,17},{17,9},{25,1},{2,26},{10... | collective-permute-start | bytes 2359304 | tf_op jit(solution)/shard_map/ppermute | solution.py:27
  734.1 204.3 %collective-permute-start.9 = (bf16[2,384,512]{2,1,0:T(8,128)(2,1)}, bf16[2,384,512]{2,1,0:T(8,128)(2,1)}, u32[]{:S(2)}, u32[]{:S(2)}) collective-permute-start(bf16[2,384,512]{2,1,0:T(8,128)(2,1)} %get-tuple-element.112), channel_id=1, source_target_pairs={{0,8},{8,0},{16,24},{24,16},{1,9},{9,1},{17,25},{25,17},{2,10},{10... | collective-permute-start | bytes 2359304 | tf_op jit(solution)/shard_map/ppermute | solution.py:27
  736.8 38.7 %copy-start.11 = (f32[768,512]{1,0:T(8,128)S(1)}, f32[768,512]{1,0:T(8,128)}, u32[]{:S(2)}) copy-start(f32[768,512]{1,0:T(8,128)} %copy-done.10) | copy-start | bytes 4718596
  736.8 38.7 %copy-start.13 = (f32[768,512]{1,0:T(8,128)S(1)}, f32[768,512]{1,0:T(8,128)}, u32[]{:S(2)}) copy-start(f32[768,512]{1,0:T(8,128)} %copy-done.12) | copy-start | bytes 4718596
  742.1 33.6 %copy-start.22 = (bf16[1,256,1536]{2,1,0:T(8,128)(2,1)S(1)}, bf16[1,256,1536]{2,1,0:T(8,128)(2,1)}, u32[]{:S(2)}) copy-start(bf16[1,256,1536]{2,1,0:T(8,128)(2,1)} %param.18) | copy-start | bytes 2359300
  742.1 33.6 %copy-start.46 = (f32[1536]{0:T(1024)S(1)}, f32[1536]{0:T(1024)}, u32[]{:S(2)}) copy-start(f32[1536]{0:T(1024)} %get-tuple-element.96) | copy-start | bytes 18436
  742.1 33.6 %copy-start.53 = (f32[256]{0:T(256)S(1)}, f32[256]{0:T(256)}, u32[]{:S(2)}) copy-start(f32[256]{0:T(256)} %fusion.37) | copy-start | bytes 3076
  775.4 165.8 %collective-permute-start.8 = (bf16[2,384,512]{2,1,0:T(8,128)(2,1)}, bf16[2,384,512]{2,1,0:T(8,128)(2,1)}, u32[]{:S(2)}, u32[]{:S(2)}) collective-permute-start(bf16[2,384,512]{2,1,0:T(8,128)(2,1)} %get-tuple-element.113), channel_id=1, source_target_pairs={{0,16},{8,24},{16,0},{24,8},{1,17},{9,25},{17,1},{25,9},{2,18},{10... | collective-permute-start | bytes 2359304 | tf_op jit(solution)/shard_map/ppermute | solution.py:27
  775.6 8.2 copy-start.40
  782.4 160.8 %collective-permute-start.16 = (bf16[2,128,1536]{2,1,0:T(8,128)(2,1)}, bf16[2,128,1536]{2,1,0:T(8,128)(2,1)}, u32[]{:S(2)}, u32[]{:S(2)}) collective-permute-start(bf16[2,128,1536]{2,1,0:T(8,128)(2,1)} %get-tuple-element.103), channel_id=1, source_target_pairs={{0,24},{8,16},{16,8},{24,0},{1,25},{9,17},{17,9},{25,1},{2,26},{10... | collective-permute-start | bytes 2359304 | tf_op jit(solution)/shard_map/ppermute | solution.py:27
  783.8 6.8 copy-start.2
  795.8 140.8 %copy-start.29 = (bf16[2,1536,512]{2,1,0:T(8,128)(2,1)S(1)}, bf16[2,1536,512]{2,1,0:T(8,128)(2,1)}, u32[]{:S(2)}) copy-start(bf16[2,1536,512]{2,1,0:T(8,128)(2,1)} %convolution_convert_fusion.5) | copy-start | bytes 9437188
  936.6 7.4 copy-start.32
  936.6 7.4 copy-start.42
  936.8 22.4 %collective-permute-start.13 = (bf16[2,384,512]{2,1,0:T(8,128)(2,1)S(1)}, bf16[2,384,512]{2,1,0:T(8,128)(2,1)S(1)}, u32[]{:S(2)}, u32[]{:S(2)}) collective-permute-start(bf16[2,384,512]{2,1,0:T(8,128)(2,1)S(1)} %get-tuple-element.107), channel_id=1, source_target_pairs={{0,24},{8,16},{16,8},{24,0},{1,25},{9,17},{17,9},{25,1},{2,26},{10... | collective-permute-start | bytes 2359304 | tf_op jit(solution)/shard_map/ppermute | solution.py:27
  938.4 28.2 %collective-permute-start.12 = (bf16[2,384,512]{2,1,0:T(8,128)(2,1)S(1)}, bf16[2,384,512]{2,1,0:T(8,128)(2,1)S(1)}, u32[]{:S(2)}, u32[]{:S(2)}) collective-permute-start(bf16[2,384,512]{2,1,0:T(8,128)(2,1)S(1)} %get-tuple-element.108), channel_id=1, source_target_pairs={{0,8},{8,0},{16,24},{24,16},{1,9},{9,1},{17,25},{25,17},{2,10},{10... | collective-permute-start | bytes 2359304 | tf_op jit(solution)/shard_map/ppermute | solution.py:27
  938.4 54.5 %collective-permute-start.11 = (bf16[2,384,512]{2,1,0:T(8,128)(2,1)S(1)}, bf16[2,384,512]{2,1,0:T(8,128)(2,1)S(1)}, u32[]{:S(2)}, u32[]{:S(2)}) collective-permute-start(bf16[2,384,512]{2,1,0:T(8,128)(2,1)S(1)} %get-tuple-element.109), channel_id=1, source_target_pairs={{0,16},{8,24},{16,0},{24,8},{1,17},{9,25},{17,1},{25,9},{2,18},{10... | collective-permute-start | bytes 2359304 | tf_op jit(solution)/shard_map/ppermute | solution.py:27
  (21 other events, 48.9 us)

commit v3 on v2

--- a/solution.py
+++ b/solution.py
@@ -80,7 +80,7 @@
     def __init__(self, send_sems, recv_sems):
         self.send_sems, self.recv_sems, self.made = send_sems, recv_sems, []
 
-    def start(self, source, target, axis, partner):
+    def start(self, source, target, axis, partner, when=None):
         number = len(self.made)
         copy = pltpu.make_async_remote_copy(
             src_ref=source,
@@ -90,13 +90,19 @@
             device_id={axis: partner},
             device_id_type=MESH,
         )
-        copy.start()
-        self.made.append(copy)
+        if when is None:
+            copy.start()
+        else:
+            pl.when(when)(copy.start)
+        self.made.append((copy, when))
         return copy
 
     def finish(self):
-        for copy in self.made:
-            copy.wait_send()
+        for copy, when in self.made:
+            if when is None:
+                copy.wait_send()
+            else:
+                pl.when(when)(copy.wait_send)
 
 
 def greet(partners):
@@ -132,7 +138,7 @@
         places = list(outs)
     else:
         tokens = refs[count + 1]
-        normed_ref, query_ref, window_ref, held, send_sems, recv_sems, local_sems, key_sems = refs[2 * count + 3 :]
+        normed_ref, query_ref, window_ref, held, send_sems, recv_sems, local_sems = refs[2 * count + 3 :]
         places = [held] + list(outs[1:])
     seq, group = lax.axis_index("seq"), lax.axis_index("fsdp")
     own = [bit_of(group, bit) for bit in bits]
@@ -145,45 +151,60 @@
     side = lax.div(seq, half)
     low = [side * half, (1 - side) * half]
     orders = [list(range(far)), list(range(far))[::-1]]
-    stages = far + 2
-    waiting = [None] * count
+    hops = length - 1
+    stages = hops + far + 1
+    waiting = [[] for _ in range(count)]
+    right, left = lax.rem(seq + 1, length), lax.rem(seq + length - 1, length)
 
     def launch(t, stage):
-        if stage == 0:
-            local = pltpu.make_async_copy(shards[t], places[t].at[(seq, *own)], local_sems.at[t])
-            local.start()
-            made = [
-                copies.start(shards[t], places[t].at[(seq, *own)], "seq", flip_all(seq, k))
-                for k in range(1, length)
-            ]
-            return made, local
+        if stage < hops:
+            back_block = lax.rem(seq - stage + length, length)
+            next_block = lax.rem(seq + stage, length)
+            if stage == 0:
+                local = pltpu.make_async_copy(shards[t], places[t].at[(seq, *own)], local_sems.at[t])
+                local.start()
+            made = []
+            for block, target, sends, comes in (
+                (back_block, right, (seq >= stage) & (seq + 1 < length), seq > stage),
+                (next_block, left, (seq + stage < length) & (seq >= 1), seq + 1 + stage < length),
+            ):
+                view = places[t].at[(block, *own)]
+                source = shards[t] if stage == 0 else view
+                made.append((copies.start(source, view, "seq", target, sends).wait_recv, comes))
+            if stage == 0:
+                made.append((local.wait, None))
+            return made
         made = []
         for part in (0, 1):
             where = [pl.ds(low[part], half)] + list(own)
-            for done in orders[part][: stage - 1]:
+            for done in orders[part][: stage - hops]:
                 where[1 + done] = slice(None)
-            dim = orders[part][stage - 1] if stage <= far else far
+            dim = orders[part][stage - hops] if stage < hops + far else far
             view = places[t].at[tuple(where)]
-            made.append(copies.start(view, view, "fsdp", flip(group, bits[dim])))
-        return made, None
+            made.append((copies.start(view, view, "fsdp", flip(group, bits[dim])).wait_recv, None))
+        return made
+
+    def settle(made):
+        for wait, when in made:
+            if when is None:
+                wait()
+            else:
+                pl.when(when)(wait)
 
     def ship_expert():
-        held, depth = expert.shape[0] // PAIR, expert.shape[1]
+        held_experts, depth = expert.shape[0] // PAIR, expert.shape[1]
         rows = pl.ds(pl.multiple_of(seq * depth, depth), depth)
         parity = lax.rem(seq, PAIR)
         local = pltpu.make_async_copy(
-            expert.at[pl.ds(parity * held, held)], expert_full.at[:, rows], local_sems.at[count]
+            expert.at[pl.ds(parity * held_experts, held_experts)], expert_full.at[:, rows], local_sems.at[count]
         )
         local.start()
-        made = []
+        made = [(local.wait, None)]
         for k in range(1, length):
-            other = lax.rem(parity + k, PAIR)
-            made.append(
-                copies.start(
-                    expert.at[pl.ds(other * held, held)], expert_full.at[:, rows], "seq", flip_all(seq, k)
-                )
-            )
-        return made, local
+            mine = pl.ds(lax.rem(parity + k, PAIR) * held_experts, held_experts)
+            copy = copies.start(expert.at[mine], expert_full.at[:, rows], "seq", flip_all(seq, k))
+            made.append((copy.wait_recv, None))
+        return made
 
     def project():
         rows, width = normed_ref.shape
@@ -203,55 +224,53 @@
                 normed_ref[...], columns(query_width + start, 512), preferred_element_type=jnp.float32
             )
             window_ref[here, pl.ds(start, 512)] = tile.astype(window_ref.dtype)
-        sent = []
         for j in range(1, back + 1):
-            copy = pltpu.make_async_remote_copy(
-                src_ref=window_ref.at[here],
-                dst_ref=window_ref.at[pl.ds((back - j) * rows, rows)],
-                send_sem=key_sems.at[0, j - 1],
-                recv_sem=key_sems.at[1, j - 1],
-                device_id={"seq": lax.rem(seq + j, length)},
-                device_id_type=MESH,
-            )
-            pl.when(seq + j < length)(copy.start)
-            sent.append(copy)
 
             @pl.when(seq < j)
             def _(j=j):
                 window_ref[pl.ds((back - j) * rows, rows)] = jnp.zeros((rows, key_width), window_ref.dtype)
 
+        first = pass_keys(1)
         for start in range(0, query_width, 512):
             tile = jnp.dot(normed_ref[...], columns(start, 512), preferred_element_type=jnp.float32)
             query_ref[:, pl.ds(start, 512)] = tile.astype(query_ref.dtype)
         kept = pltpu.make_async_copy(held, outs[0], local_sems.at[0])
         kept.start()
-        return sent, kept
-
+        return first, kept
+
+    def pass_keys(j):
+        rows = normed_ref.shape[0]
+        source = window_ref.at[pl.ds((back - j + 1) * rows, rows)]
+        target = window_ref.at[pl.ds((back - j) * rows, rows)]
+        sends = (seq >= j - 1) & (seq + 1 < length)
+        return [(copies.start(source, target, "seq", right, sends).wait_recv, seq >= j)]
+
+    passing, passed = [], 0
     for step in range(count + stages):
-        if step == count:
+        if step == hops + 1:
             expert_waiting = ship_expert()
+        if passing:
+            settle(passing)
+            passing = []
+            if passed < back:
+                passed += 1
+                passing = pass_keys(passed)
         for t in range(count):
             stage = step - t
-            if 0 < stage <= stages and waiting[t]:
-                made, local = waiting[t]
-                for copy in made:
-                    copy.wait_recv()
-                if local is not None:
-                    local.wait()
-                waiting[t] = None
+            if 0 < stage <= stages:
+                settle(waiting[t])
             if 0 <= stage < stages:
                 waiting[t] = launch(t, stage)
         if step == stages and back is not None:
-            sent, kept = project()
-    made, local = expert_waiting
-    for copy in made:
-        copy.wait_recv()
-    local.wait()
+            passing, kept = project()
+            passed = 1
+    while passing:
+        settle(passing)
+        passed += 1
+        passing = pass_keys(passed) if passed <= back else []
+    settle(expert_waiting)
     copies.finish()
     if back is not None:
-        for j, copy in enumerate(sent, 1):
-            pl.when(seq >= j)(copy.wait_recv)
-            pl.when(seq + j < length)(copy.wait_send)
         kept.wait()
 
 
@@ -262,13 +281,13 @@
         bits.append(bit)
         bit //= 2
     count = len(shards)
-    number = count * (length - 1 + 2 * len(bits)) + length - 1
+    number = count * 2 * (length - 1 + len(bits)) + length - 1 + back
     size = sum(s.size * s.dtype.itemsize for s in shards) * length * groups
     experts, depth, wide = expert.shape
     lead = (length,) + (2,) * len(bits)
     rows, width = tokens.shape
     fused = shards[0].shape[0] % 16 == 0
-    extra_in, extra_out, extra_scratch, key_scratch = [], [], [], []
+    extra_in, extra_out, extra_scratch = [], [], []
     if fused:
         query_width = shards[0].shape[1] - key_width - 128
         extra_in = [tokens]
@@ -278,7 +297,6 @@
             jax.ShapeDtypeStruct(((back + 1) * rows, key_width), tokens.dtype),
         ]
         extra_scratch = [pltpu.VMEM(lead + shards[0].shape, shards[0].dtype)]
-        key_scratch = [pltpu.SemaphoreType.DMA((2, back))]
     results = pl.pallas_call(
         functools.partial(gather_dense_kernel, length, bits, count, back if fused else None),
         out_shape=[
@@ -296,8 +314,7 @@
             pltpu.SemaphoreType.DMA((number,)),
             pltpu.SemaphoreType.DMA((number,)),
             pltpu.SemaphoreType.DMA((count + 1,)),
-        ]
-        + key_scratch,
+        ],
         compiler_params=pltpu.CompilerParams(
             collective_id=0, has_side_effects=True, vmem_limit_bytes=60 * 2**20
         ),
@@ -838,17 +855,17 @@
     gathered = gather_dense(
         [
             jnp.concatenate([query_weight, key_weight, value_weight, gains], axis=1),
-            meta,
             output_weight,
             jnp.concatenate([shared_gate_weight, shared_up_weight], axis=1),
             shared_down_weight,
+            meta,
         ],
         expert_gate_weight,
         tokens[0],
         back,
         2 * key_width,
     )
-    qkv_full, meta, output_full, gate_up_full, down_full, expert_gate_full = gathered[:6]
+    qkv_full, output_full, gate_up_full, down_full, meta, expert_gate_full = gathered[:6]
     normed_one, query_rows, key_value_all = gathered[6:]
 
     def weight_grad(rows, grad_rows):

time: 1010 us -> 960 us (0.950)
  starting transfers between devices: 71.3 us -> 43.9 us
  waiting for transfers between devices: 121 us -> 95.4 us
    ppermute x15, starting transfers between devices: 68.5 us -> 41 us  [exchange(): return lax.ppermute(values, axis, [(i, i ^ bit) for i in range(count)])]
    ppermute x2, waiting for transfers between devices: 54.5 us -> 33.8 us  [shift(): return lax.ppermute(values, axis, pairs)]
  transfers between devices with their start and end apart: 17 -> 17, of which waited for: 6 -> 6; matrix products, arithmetic and copies ran while one was open for 8% -> 8% of each run, Pallas kernels for 25% -> 28%
where the time goes in v3:
time: 960 us; the launch traced here: 956 us
  Pallas kernels  632 us (66%)
  matrix products  108 us (11%)
  waiting for transfers between devices  95.4 us (10%)
  local copies, waits for them, and re-layouts  44.9 us (5%)
  starting transfers between devices  43.9 us (5%)
  other arithmetic  30.3 us (3%)
    pallas_call x2, Pallas kernels, gather_rows(): pl.pallas_call(functools.partial(gather_rows_kernel, dims, orders, held),...  163 us
    pallas_call x1, Pallas kernels, gather_dense(): pl.pallas_call(functools.partial(gather_dense_kernel, length, bits, count...  151 us
    pallas_call x2, Pallas kernels, scatter_rows(): pl.pallas_call(kernel, out_shape=jax.ShapeDtypeStruct((count, feat), jnp....  151 us
    pallas_call x1, Pallas kernels, scatter_dense(): pl.pallas_call(functools.partial(scatter_dense_kernel, length, bits, coun...  148 us
    ppermute x15, waiting for transfers between devices, exchange(): return lax.ppermute(values, axis, [(i, i ^ bit) for i in range(count)])  61.6 us
    dot_general x9, matrix products, batch_dot(): lax.dot_general(left, right, (((left_dim,), (right_dim,)), ((0,), (0,))),...  60.3 us
    dot_general x11, matrix products, dot(): lax.dot_general(left, right, (((left_dim,), (right_dim,)), ((), ())), pre...  47 us
    ppermute x15, starting transfers between devices, exchange(): return lax.ppermute(values, axis, [(i, i ^ bit) for i in range(count)])  41 us
  transfers between devices with their start and end apart: 17, of which 6 were waited for; matrix products, arithmetic and copies ran while one was open for 8% of the time, Pallas kernels for 28%

profile of v3, /device:TPU:0, one launch (start us, length us, event | category | flops | bytes accessed | tf_op | source)
XLA Modules:
  0.0 956.0 jit_solution(15819513885882875318)
XLA Ops:
  3.5 1.6 pad_maximum_fusion.7.refs_2_
  5.1 1.7 fusion.33.refs_0_
  6.8 150.7 %gather_dense.1 = (bf16[4,2,2,2,48,2688]{5,4,3,2,1,0:T(8,128)(2,1)}, bf16[4,2,2,2,48,1536]{5,4,3,2,1,0:T(8,128)(2,1)}, bf16[4,2,2,2,48,2048]{5,4,3,2,1,0:T(8,128...) custom-call(bf16[48,2688]{1,0:T(8,128)(2,1)} %fusion.33.refs_0_, ...), custom_call_target="tpu_custom_call" | custom-call | bytes 68812800 | tf_op jit(solution)/shard_map/gather_dense/pallas_call | solution.py:300
  157.5 2.8 constant_dynamic-slice_fusion.13
  160.2 1.5 collective-permute-start.2
  163.9 8.1 attend.1
  172.0 4.0 multiply_reduce_fusion.2
  176.3 1.7 copy-done.26
  179.3 2.4 collective-permute-start.5
  189.2 4.6 fusion.45
  196.0 110.3 %gather_rows.2 = bf16[2,2,2,2,2,64,1536]{6,5,4,3,2,1,0:T(8,128)(2,1)S(1)} custom-call(bf16[256,1536]{1,0:T(8,128)(2,1)S(1)} %multiply_convert_fusion.3.rows_ref, bf16[2,2,2,2,128,256]{5,4,3,2,1,0:T(8,128)(2,1)S(1)} %and_convert_fusion.pick_ref), custom_call_target="tpu_custom_call" | custom-call | flops 1610612736 | bytes 37748736 | tf_op jit(solution)/shard_map/gather_rows/pallas_call | solution.py:561
  306.3 2.6 copy-done.3
  310.6 1.9 broadcast_in_dim.155
  313.4 3.0 fusion.46
  316.4 3.4 fusion.47
  320.0 1.8 constant_dynamic-update-slice_fusion.5
  324.2 5.3 multiply_convert_fusion.2
  329.6 26.1 %collective-permute-done.4 = bf16[2,128,1536]{2,1,0:T(8,128)(2,1)S(1)} collective-permute-done((bf16[2,128,1536]{2,1,0:T(8,128)(2,1)S(1)}, bf16[2,128,1536]{2,1,0:T(8,128)(2,1)S(1)}, u32[]{:S(2)}, u32[]{:S(2)}) %collective-permute-start.4) | collective-permute-done | bytes 786464 | tf_op jit(solution)/shard_map/ppermute | solution.py:27
  355.7 2.1 constant_dynamic-update-slice_fusion.2
  358.7 2.1 constant_dynamic-update-slice_fusion
  360.7 5.9 multiply_convert_fusion
  366.7 61.5 %scatter_rows.2 = f32[256,1536]{1,0:T(8,128)S(1)} custom-call(bf16[2,2,2,2,2,64,1536]{6,5,4,3,2,1,0:T(8,128)(2,1)S(1)} %bitcast.112, bf16[2,2,2,2,128,256]{5,4,3,2,1,0:T(8,128)(2,1)S(1)} %and_convert_fusion.pick_ref), custom_call_target="tpu_custom_call" | custom-call | flops 1610612736 | bytes 37748736 | tf_op jit(solution)/shard_map/scatter_rows/pallas_call | solution.py:675
  428.2 1.8 fusion.26
  431.3 2.3 fusion.18
  433.6 2.7 convolution_convert_fusion.3
  436.3 52.7 %gather_rows.3 = bf16[2,2,2,2,2,64,1536]{6,5,4,3,2,1,0:T(8,128)(2,1)S(1)} custom-call(bf16[256,1536]{1,0:T(8,128)(2,1)S(1)} %get-tuple-element.98.rows_ref, bf16[2,2,2,2,128,256]{5,4,3,2,1,0:T(8,128)(2,1)S(1)} %and_convert_fusion.pick_ref), custom_call_target="tpu_custom_call" | custom-call | flops 1610612736 | bytes 37748736 | tf_op jit(solution)/shard_map/gather_rows/pallas_call | solution.py:561
  489.0 3.9 fusion
  492.8 8.5 convolution_convert_fusion.4
  501.4 11.1 %multiply_convert_fusion.1 = (bf16[2,1024,512]{2,1,0:T(8,128)(2,1)S(1)}, bf16[2,1024,512]{2,1,0:T(8,128)(2,1)S(1)}) fusion(f32[2,1024,512]{2,1,0:T(8,128)} %copy-done.62, f32[2,1024,512]{2,1,0:T(8,128)} %get-tuple-element.137, bf16[2,1024,1536]{2,1,0:T(8,128)(2,1)} %fusion, bf16[2,512,1536]{2,1,0:T(8,128)(2,1)} %constant_dynamic-update-slice_fusion), kind=kOutput, calls=%fused_computation.13 | convolution fusion | flops 3235905536 | bytes 22020096 | tf_op jit(solution)/shard_map/dot_general | solution.py:47
  512.5 4.9 convolution_convert_fusion.6
  517.4 6.4 fusion.48
  523.9 5.0 convolution_convert_fusion.5
  528.9 9.6 %add_convert_fusion = bf16[2,1024,1536]{2,1,0:T(8,128)(2,1)S(1)} fusion(f32[2,1024,1536]{2,1,0:T(8,128)} %fusion.48, bf16[2,1024,512]{2,1,0:T(8,128)(2,1)} %copy-done.36, bf16[2,1536,512]{2,1,0:T(8,128)(2,1)} %copy-done.19), kind=kOutput, calls=%fused_computation.2 | convolution fusion | flops 3227516928 | bytes 24117248 | tf_op jit(solution)/shard_map/dot_general | solution.py:47
  538.6 89.2 %scatter_rows.3 = f32[256,1536]{1,0:T(8,128)S(1)} custom-call(bf16[2,2,2,2,2,64,1536]{6,5,4,3,2,1,0:T(8,128)(2,1)S(1)} %bitcast.110, bf16[2,2,2,2,128,256]{5,4,3,2,1,0:T(8,128)(2,1)S(1)} %and_convert_fusion.pick_ref), custom_call_target="tpu_custom_call" | custom-call | flops 1610612736 | bytes 37748736 | tf_op jit(solution)/shard_map/scatter_rows/pallas_call | solution.py:675
  627.9 5.8 multiply_reduce_fusion
  633.8 1.5 fusion.8
  635.3 1.4 convolution_convert_fusion.7.grad
  637.4 11.6 %attend_back.1 = (bf16[256,1536]{1,0:T(8,128)(2,1)S(1)}, f32[2,768,512]{2,1,0:T(8,128)S(1)}) custom-call(bf16[256,1536]{1,0:T(8,128)(2,1)S(1)} %copy-done.7, bf16[768,1024]{1,0:T(8,128)(2,1)S(1)} %copy-done.6, bf16[768,1024]{1,0:T(8,128)(2,1)S(1)} %copy-done.6, s32[256,1]{1,0:T(8,128)S(1)} %copy.86.seg_rows, s32[1,768]{1,0:T(1,128)S(1)} %broadcast_in_dim.149.seg_keys, ...), custom_call_target="tpu_custom_call" | custom-call | flops 3019898880 | bytes 6291456 | tf_op jit(solution)/shard_map/attend_back/pallas_call | solution.py:793
  649.5 1.6 collective-permute-start.6
  652.4 1.8 constant_dynamic-slice_fusion.1
  655.5 3.8 collective-permute-start.14
  659.3 4.5 convolution_convert_fusion.1
  663.8 3.2 collective-permute-done.6
  668.5 1.7 constant_dynamic-slice_fusion.9
  670.3 5.2 collective-permute-start.10
  675.6 5.2 convolution_convert_fusion.2
  680.8 30.5 %collective-permute-done.7 = bf16[256,1024]{1,0:T(8,128)(2,1)S(1)} collective-permute-done((bf16[256,1024]{1,0:T(8,128)(2,1)S(1)}, bf16[256,1024]{1,0:T(8,128)(2,1)S(1)}, u32[]{:S(2)}, u32[]{:S(2)}) %collective-permute-start.7) | collective-permute-done | bytes 524320 | tf_op jit(solution)/shard_map/ppermute | solution.py:33
  711.4 3.8 collective-permute-start.8
  715.4 6.7 fusion.14
  722.1 16.5 %collective-permute-start.16 = (bf16[2,128,1536]{2,1,0:T(8,128)(2,1)}, bf16[2,128,1536]{2,1,0:T(8,128)(2,1)}, u32[]{:S(2)}, u32[]{:S(2)}) collective-permute-start(bf16[2,128,1536]{2,1,0:T(8,128)(2,1)} %get-tuple-element.103), channel_id=1, source_target_pairs={{0,24},{8,16},{16,8},{24,0},{1,25},{9,17},{17,9},{25,1},{2,26},{10... | collective-permute-start | bytes 2359304 | tf_op jit(solution)/shard_map/ppermute | solution.py:27
  738.6 6.7 convolution_convert_fusion
  745.5 2.8 copy-done
  748.3 2.3 copy-done.1
  750.6 148.0 %scatter_dense.1 = (f32[48,2048]{1,0:T(8,128)S(1)}, f32[48,2560]{1,0:T(8,128)S(1)}, f32[48,1536]{1,0:T(8,128)S(1)}, f32[32,1536]{1,0:T(8,128)S(1)}, f32[8,128]{1,0:T(8,128)S(1)}) custom-call(bf16[4,2,2,2,48,2048]{5,4,3,2,1,0:T(8,128)(2,1)S(1)} %bitcast.108, bf16[4,2,2,2,48,2560]{5,4,3,2,1,0:T(8,128)(2,1)} %bitcast.120, ...), custom_call_target="tpu_custom_call" | custom-call | bytes 66453504 | tf_op jit(solution)/shard_map/scatter_dense/pallas_call | solution.py:450
  898.9 1.5 collective-permute-start.13
  900.4 2.9 collective-permute-start.11
  906.0 1.8 convert_add_fusion.1
  907.9 2.1 bitcast_select_fusion
  910.0 2.2 convert_add_fusion.5
  912.8 1.6 fusion.10
  914.4 4.2 collective-permute-done.13
  918.6 5.7 collective-permute-done.12
  924.3 25.5 %collective-permute-done.11 = bf16[2,384,512]{2,1,0:T(8,128)(2,1)S(1)} collective-permute-done((bf16[2,384,512]{2,1,0:T(8,128)(2,1)S(1)}, bf16[2,384,512]{2,1,0:T(8,128)(2,1)S(1)}, u32[]{:S(2)}, u32[]{:S(2)}) %collective-permute-start.11) | collective-permute-done | bytes 786464 | tf_op jit(solution)/shard_map/ppermute | solution.py:27
  950.3 4.0 bitcast_select_fusion.1
  (218 shorter events, 34.3 us)
Async XLA Ops:
  6.8 154.9 %copy-start.56 = (s32[1,1024]{1,0:T(1,128)S(1)}, s32[1,1024]{1,0:T(1,128)}, u32[]{:S(2)}) copy-start(s32[1,1024]{1,0:T(1,128)} %param.21) | copy-start | bytes 12292
  157.5 6.4 copy-start.5
  157.5 6.4 copy-start.7
  160.2 159.6 %collective-permute-start.2 = (bf16[2,384,512]{2,1,0:T(8,128)(2,1)}, bf16[2,384,512]{2,1,0:T(8,128)(2,1)}, u32[]{:S(2)}, u32[]{:S(2)}) collective-permute-start(bf16[2,384,512]{2,1,0:T(8,128)(2,1)} %get-tuple-element.123), channel_id=1, source_target_pairs={{0,24},{8,16},{16,8},{24,0},{1,25},{9,17},{17,9},{25,1},{2,26},{10... | collective-permute-start | bytes 2359304 | tf_op jit(solution)/shard_map/ppermute | solution.py:27
  161.7 158.3 %collective-permute-start = (bf16[2,384,512]{2,1,0:T(8,128)(2,1)}, bf16[2,384,512]{2,1,0:T(8,128)(2,1)}, u32[]{:S(2)}, u32[]{:S(2)}) collective-permute-start(bf16[2,384,512]{2,1,0:T(8,128)(2,1)} %get-tuple-element.123), channel_id=1, source_target_pairs={{0,8},{8,0},{16,24},{24,16},{1,9},{9,1},{17,25},{25,17},{2,10},{10... | collective-permute-start | bytes 2359304 | tf_op jit(solution)/shard_map/ppermute | solution.py:27
  163.3 8.7 copy-start.20
  172.0 4.0 copy-start.8
  176.0 3.3 copy-start.14
  176.1 7.7 copy-start.21
  178.0 8.6 copy-start.58
  179.3 150.3 %collective-permute-start.5 = (bf16[2,128,1536]{2,1,0:T(8,128)(2,1)}, bf16[2,128,1536]{2,1,0:T(8,128)(2,1)}, u32[]{:S(2)}, u32[]{:S(2)}) collective-permute-start(bf16[2,128,1536]{2,1,0:T(8,128)(2,1)} %get-tuple-element.121), channel_id=1, source_target_pairs={{0,24},{8,16},{16,8},{24,0},{1,25},{9,17},{17,9},{25,1},{2,26},{10... | collective-permute-start | bytes 2359304 | tf_op jit(solution)/shard_map/ppermute | solution.py:27
  181.7 174.0 %collective-permute-start.3 = (bf16[2,128,1536]{2,1,0:T(8,128)(2,1)}, bf16[2,128,1536]{2,1,0:T(8,128)(2,1)}, u32[]{:S(2)}, u32[]{:S(2)}) collective-permute-start(bf16[2,128,1536]{2,1,0:T(8,128)(2,1)} %get-tuple-element.121), channel_id=1, source_target_pairs={{0,8},{8,0},{16,24},{24,16},{1,9},{9,1},{17,25},{25,17},{2,10},{10... | collective-permute-start | bytes 2359304 | tf_op jit(solution)/shard_map/ppermute | solution.py:27
  182.8 137.1 %collective-permute-start.1 = (bf16[2,384,512]{2,1,0:T(8,128)(2,1)}, bf16[2,384,512]{2,1,0:T(8,128)(2,1)}, u32[]{:S(2)}, u32[]{:S(2)}) collective-permute-start(bf16[2,384,512]{2,1,0:T(8,128)(2,1)} %get-tuple-element.122), channel_id=1, source_target_pairs={{0,16},{8,24},{16,0},{24,8},{1,17},{9,25},{17,1},{25,9},{2,18},{10... | collective-permute-start | bytes 2359304 | tf_op jit(solution)/shard_map/ppermute | solution.py:27
  308.9 7.4 slice-start
  309.1 3.3 copy-start.27
  310.5 5.8 slice-start.1
  316.4 3.4 copy-start.43
  319.8 9.7 %copy-start.62 = (f32[2,1024,512]{2,1,0:T(8,128)}, f32[2,1024,512]{2,1,0:T(8,128)S(1)}, u32[]{:S(2)}) copy-start(f32[2,1024,512]{2,1,0:T(8,128)S(1)} %fusion.47) | copy-start | bytes 12582916
  319.9 35.8 %collective-permute-start.4 = (bf16[2,128,1536]{2,1,0:T(8,128)(2,1)S(1)}, bf16[2,128,1536]{2,1,0:T(8,128)(2,1)S(1)}, u32[]{:S(2)}, u32[]{:S(2)}) collective-permute-start(bf16[2,128,1536]{2,1,0:T(8,128)(2,1)S(1)} %copy-done.43), channel_id=1, source_target_pairs={{0,16},{8,24},{16,0},{24,8},{1,17},{9,25},{17,1},{25,9},{2,18},{10... | collective-permute-start | bytes 2359304 | tf_op jit(solution)/shard_map/ppermute | solution.py:27
  324.2 5.4 copy-start.19
  329.5 37.1 %copy-start.63 = (bf16[2,1024,512]{2,1,0:T(8,128)(2,1)}, bf16[2,1024,512]{2,1,0:T(8,128)(2,1)S(1)}, u32[]{:S(2)}) copy-start(bf16[2,1024,512]{2,1,0:T(8,128)(2,1)S(1)} %get-tuple-element.136) | copy-start | bytes 6291460
  329.5 31.2 %copy-start.47 = (f32[2,1024]{1,0:T(2,128)S(1)}, f32[2,1024]{1,0:T(2,128)}, u32[]{:S(2)}) copy-start(f32[2,1024]{1,0:T(2,128)} %mul.265) | copy-start | bytes 24580
  366.7 61.5 %copy-start.15 = (f32[256,1536]{1,0:T(8,128)S(1)}, f32[256,1536]{1,0:T(8,128)}, u32[]{:S(2)}) copy-start(f32[256,1536]{1,0:T(8,128)} %copy-done.14) | copy-start | bytes 4718596
  366.7 61.5 %copy-start.34 = (bf16[1,256,1536]{2,1,0:T(8,128)(2,1)S(1)}, bf16[1,256,1536]{2,1,0:T(8,128)(2,1)}, u32[]{:S(2)}) copy-start(bf16[1,256,1536]{2,1,0:T(8,128)(2,1)} %param.19) | copy-start | bytes 2359300
  366.7 61.5 %copy-start.50 = (f32[1,256]{1,0:T(1,128)S(1)}, f32[1,256]{1,0:T(1,128)}, u32[]{:S(2)}) copy-start(f32[1,256]{1,0:T(1,128)} %convert_element_type.184) | copy-start | bytes 3076
  512.5 11.4 %copy-start.36 = (bf16[2,1024,512]{2,1,0:T(8,128)(2,1)}, bf16[2,1024,512]{2,1,0:T(8,128)(2,1)S(1)}, u32[]{:S(2)}) copy-start(bf16[2,1024,512]{2,1,0:T(8,128)(2,1)S(1)} %get-tuple-element.100) | copy-start | bytes 6291460
  512.5 5.0 copy-start.61
  538.5 89.3 %copy-start.16 = (f32[256,1536]{1,0:T(8,128)S(1)}, f32[256,1536]{1,0:T(8,128)}, u32[]{:S(2)}) copy-start(f32[256,1536]{1,0:T(8,128)} %copy-done.14) | copy-start | bytes 4718596
  538.5 89.3 %copy-start.44 = (bf16[256,1024]{1,0:T(8,128)(2,1)S(1)}, bf16[256,1024]{1,0:T(8,128)(2,1)}, u32[]{:S(2)}) copy-start(bf16[256,1024]{1,0:T(8,128)(2,1)} %get-tuple-element.116) | copy-start | bytes 1572868
  538.6 89.3 %copy-start.45 = (bf16[256,1024]{1,0:T(8,128)(2,1)S(1)}, bf16[256,1024]{1,0:T(8,128)(2,1)}, u32[]{:S(2)}) copy-start(bf16[256,1024]{1,0:T(8,128)(2,1)} %get-tuple-element.117) | copy-start | bytes 1572868
  538.6 89.3 %copy-start.49 = (f32[256]{0:T(256)S(1)}, f32[256]{0:T(256)}, u32[]{:S(2)}) copy-start(f32[256]{0:T(256)} %copy-done.48) | copy-start | bytes 3076
  538.6 96.7 %slice-start.2 = ((s8[4718592]{0:T(1024)(128)(4,1)}), s8[4194304]{0:T(1024)(128)(4,1)S(1)}, s32[]{:S(2)}) async-start(s8[4718592]{0:T(1024)(128)(4,1)} %bitcast.140), calls=%async_computation.2 | async-start | bytes 8388608
  627.8 5.9 copy-start.55
  627.8 5.9 copy-start.25
  627.9 5.9 copy-start.35
  627.9 5.9 copy-start.51
  627.9 7.4 slice-start.3
  649.0 66.3 %copy-start.4 = (bf16[256,1536]{1,0:T(8,128)(2,1)}, bf16[256,1536]{1,0:T(8,128)(2,1)S(1)}, u32[]{:S(2)}) copy-start(bf16[256,1536]{1,0:T(8,128)(2,1)S(1)} %get-tuple-element.71) | copy-start | bytes 2359300
  649.4 17.7 %copy-start.10 = (f32[768,512]{1,0:T(8,128)}, f32[768,512]{1,0:T(8,128)S(1)}, u32[]{:S(2)}) copy-start(f32[768,512]{1,0:T(8,128)S(1)} %get-tuple-element.114) | copy-start | bytes 4718596
  649.4 17.7 %copy-start.12 = (f32[768,512]{1,0:T(8,128)}, f32[768,512]{1,0:T(8,128)S(1)}, u32[]{:S(2)}) copy-start(f32[768,512]{1,0:T(8,128)S(1)} %get-tuple-element.115) | copy-start | bytes 4718596
  649.5 17.6 %collective-permute-start.6 = (bf16[256,1024]{1,0:T(8,128)(2,1)S(1)}, bf16[256,1024]{1,0:T(8,128)(2,1)S(1)}, u32[]{:S(2)}, u32[]{:S(2)}) collective-permute-start(bf16[256,1024]{1,0:T(8,128)(2,1)S(1)} %fusion.23), channel_id=1, source_target_pairs={{8,0},{16,8},{24,16},{9,1},{17,9},{25,17},{10,2},{18,10},{26,18},{... | collective-permute-start | bytes 1572872 | tf_op jit(solution)/shard_map/ppermute | solution.py:33
  654.2 67.9 %collective-permute-start.15 = (bf16[2,128,1536]{2,1,0:T(8,128)(2,1)}, bf16[2,128,1536]{2,1,0:T(8,128)(2,1)S(1)}, u32[]{:S(2)}, u32[]{:S(2)}) collective-permute-start(bf16[2,128,1536]{2,1,0:T(8,128)(2,1)} %get-tuple-element.104), channel_id=1, source_target_pairs={{0,8},{8,0},{16,24},{24,16},{1,9},{9,1},{17,25},{25,17},{2,10},{10... | collective-permute-start | bytes 2359304 | tf_op jit(solution)/shard_map/ppermute | solution.py:27
  655.5 243.4 %collective-permute-start.14 = (bf16[2,128,1536]{2,1,0:T(8,128)(2,1)}, bf16[2,128,1536]{2,1,0:T(8,128)(2,1)}, u32[]{:S(2)}, u32[]{:S(2)}) collective-permute-start(bf16[2,128,1536]{2,1,0:T(8,128)(2,1)} %get-tuple-element.105), channel_id=1, source_target_pairs={{0,16},{8,24},{16,0},{24,8},{1,17},{9,25},{17,1},{25,9},{2,18},{10... | collective-permute-start | bytes 2359304 | tf_op jit(solution)/shard_map/ppermute | solution.py:27
  663.8 4.7 copy-start.30
  667.2 8.3 copy-start.52
  667.2 44.1 %collective-permute-start.7 = (bf16[256,1024]{1,0:T(8,128)(2,1)S(1)}, bf16[256,1024]{1,0:T(8,128)(2,1)S(1)}, u32[]{:S(2)}, u32[]{:S(2)}) collective-permute-start(bf16[256,1024]{1,0:T(8,128)(2,1)S(1)} %fusion.21), channel_id=1, source_target_pairs={{8,0},{16,8},{24,16},{9,1},{17,9},{25,17},{10,2},{18,10},{26,18},{... | collective-permute-start | bytes 1572872 | tf_op jit(solution)/shard_map/ppermute | solution.py:33
  670.3 230.1 %collective-permute-start.10 = (bf16[2,384,512]{2,1,0:T(8,128)(2,1)}, bf16[2,384,512]{2,1,0:T(8,128)(2,1)}, u32[]{:S(2)}, u32[]{:S(2)}) collective-permute-start(bf16[2,384,512]{2,1,0:T(8,128)(2,1)} %get-tuple-element.111), channel_id=1, source_target_pairs={{0,24},{8,16},{16,8},{24,0},{1,25},{9,17},{17,9},{25,1},{2,26},{10... | collective-permute-start | bytes 2359304 | tf_op jit(solution)/shard_map/ppermute | solution.py:27
  675.5 224.9 %collective-permute-start.9 = (bf16[2,384,512]{2,1,0:T(8,128)(2,1)}, bf16[2,384,512]{2,1,0:T(8,128)(2,1)}, u32[]{:S(2)}, u32[]{:S(2)}) collective-permute-start(bf16[2,384,512]{2,1,0:T(8,128)(2,1)} %get-tuple-element.112), channel_id=1, source_target_pairs={{0,8},{8,0},{16,24},{24,16},{1,9},{9,1},{17,25},{25,17},{2,10},{10... | collective-permute-start | bytes 2359304 | tf_op jit(solution)/shard_map/ppermute | solution.py:27
  675.6 39.6 %copy-start.11 = (f32[768,512]{1,0:T(8,128)S(1)}, f32[768,512]{1,0:T(8,128)}, u32[]{:S(2)}) copy-start(f32[768,512]{1,0:T(8,128)} %copy-done.10) | copy-start | bytes 4718596
  675.6 39.6 %copy-start.13 = (f32[768,512]{1,0:T(8,128)S(1)}, f32[768,512]{1,0:T(8,128)}, u32[]{:S(2)}) copy-start(f32[768,512]{1,0:T(8,128)} %copy-done.12) | copy-start | bytes 4718596
  680.8 34.5 %copy-start.22 = (bf16[1,256,1536]{2,1,0:T(8,128)(2,1)S(1)}, bf16[1,256,1536]{2,1,0:T(8,128)(2,1)}, u32[]{:S(2)}) copy-start(bf16[1,256,1536]{2,1,0:T(8,128)(2,1)} %param.18) | copy-start | bytes 2359300
  680.8 34.5 %copy-start.46 = (f32[1536]{0:T(1024)S(1)}, f32[1536]{0:T(1024)}, u32[]{:S(2)}) copy-start(f32[1536]{0:T(1024)} %get-tuple-element.96) | copy-start | bytes 18436
  680.8 34.5 %copy-start.53 = (f32[256]{0:T(256)S(1)}, f32[256]{0:T(256)}, u32[]{:S(2)}) copy-start(f32[256]{0:T(256)} %fusion.37) | copy-start | bytes 3076
  711.4 192.0 %collective-permute-start.8 = (bf16[2,384,512]{2,1,0:T(8,128)(2,1)}, bf16[2,384,512]{2,1,0:T(8,128)(2,1)}, u32[]{:S(2)}, u32[]{:S(2)}) collective-permute-start(bf16[2,384,512]{2,1,0:T(8,128)(2,1)} %get-tuple-element.113), channel_id=1, source_target_pairs={{0,16},{8,24},{16,0},{24,8},{1,17},{9,25},{17,1},{25,9},{2,18},{10... | collective-permute-start | bytes 2359304 | tf_op jit(solution)/shard_map/ppermute | solution.py:27
  715.3 23.3 %copy-start.40 = (bf16[256,1536]{1,0:T(8,128)(2,1)S(1)}, bf16[256,1536]{1,0:T(8,128)(2,1)}, u32[]{:S(2)}) copy-start(bf16[256,1536]{1,0:T(8,128)(2,1)} %get-tuple-element.73) | copy-start | bytes 2359300
  722.1 16.5 %copy-start.41 = (bf16[2,128,1536]{2,1,0:T(8,128)(2,1)}, bf16[2,128,1536]{2,1,0:T(8,128)(2,1)S(1)}, u32[]{:S(2)}) copy-start(bf16[2,128,1536]{2,1,0:T(8,128)(2,1)S(1)} %collective-permute-done.15) | copy-start | bytes 2359300
  722.1 183.2 %collective-permute-start.16 = (bf16[2,128,1536]{2,1,0:T(8,128)(2,1)}, bf16[2,128,1536]{2,1,0:T(8,128)(2,1)}, u32[]{:S(2)}, u32[]{:S(2)}) collective-permute-start(bf16[2,128,1536]{2,1,0:T(8,128)(2,1)} %get-tuple-element.103), channel_id=1, source_target_pairs={{0,24},{8,16},{16,8},{24,0},{1,25},{9,17},{17,9},{25,1},{2,26},{10... | collective-permute-start | bytes 2359304 | tf_op jit(solution)/shard_map/ppermute | solution.py:27
  738.6 6.8 copy-start.2
  750.6 148.0 %copy-start.29 = (bf16[2,1536,512]{2,1,0:T(8,128)(2,1)S(1)}, bf16[2,1536,512]{2,1,0:T(8,128)(2,1)}, u32[]{:S(2)}) copy-start(bf16[2,1536,512]{2,1,0:T(8,128)(2,1)} %convolution_convert_fusion.5) | copy-start | bytes 9437188
  898.6 7.4 copy-start.32
  898.6 7.4 copy-start.42
  898.9 19.7 %collective-permute-start.13 = (bf16[2,384,512]{2,1,0:T(8,128)(2,1)S(1)}, bf16[2,384,512]{2,1,0:T(8,128)(2,1)S(1)}, u32[]{:S(2)}, u32[]{:S(2)}) collective-permute-start(bf16[2,384,512]{2,1,0:T(8,128)(2,1)S(1)} %get-tuple-element.107), channel_id=1, source_target_pairs={{0,24},{8,16},{16,8},{24,0},{1,25},{9,17},{17,9},{25,1},{2,26},{10... | collective-permute-start | bytes 2359304 | tf_op jit(solution)/shard_map/ppermute | solution.py:27
  900.4 23.9 %collective-permute-start.12 = (bf16[2,384,512]{2,1,0:T(8,128)(2,1)S(1)}, bf16[2,384,512]{2,1,0:T(8,128)(2,1)S(1)}, u32[]{:S(2)}, u32[]{:S(2)}) collective-permute-start(bf16[2,384,512]{2,1,0:T(8,128)(2,1)S(1)} %get-tuple-element.108), channel_id=1, source_target_pairs={{0,8},{8,0},{16,24},{24,16},{1,9},{9,1},{17,25},{25,17},{2,10},{10... | collective-permute-start | bytes 2359304 | tf_op jit(solution)/shard_map/ppermute | solution.py:27
  900.4 49.4 %collective-permute-start.11 = (bf16[2,384,512]{2,1,0:T(8,128)(2,1)S(1)}, bf16[2,384,512]{2,1,0:T(8,128)(2,1)S(1)}, u32[]{:S(2)}, u32[]{:S(2)}) collective-permute-start(bf16[2,384,512]{2,1,0:T(8,128)(2,1)S(1)} %get-tuple-element.109), channel_id=1, source_target_pairs={{0,16},{8,24},{16,0},{24,8},{1,17},{9,25},{17,1},{25,9},{2,18},{10... | collective-permute-start | bytes 2359304 | tf_op jit(solution)/shard_map/ppermute | solution.py:27
  (21 other events, 50.7 us)

commit v4 on v3

--- a/solution.py
+++ b/solution.py
@@ -466,6 +466,212 @@
     )(*[g.reshape((length,) + (2,) * len(bits) + g.shape[1:]) for g in grads])
 
 
+def sum_dense_kernel(length, bits, cuts, plan, keys_at, back, *refs):
+    count = len(cuts)
+    weights = count - 1
+    act_count = 1 + max(a for group in plan for a, _ in group)
+    grad_count = 1 + max(g for group in plan for _, g in group if g is not None)
+    acts, grads = refs[:act_count], refs[act_count : act_count + grad_count]
+    ready, window, *refs = refs[act_count + grad_count :]
+    number = sum(len(cut) for cut in cuts)
+    flat_outs, keys_out, refs = list(refs[:number]), refs[number], refs[number + 1 :]
+    outs = [[flat_outs.pop(0) for _ in cut] for cut in cuts]
+    far = len(bits) - 1
+    per = 3 + far
+    scratch = refs[: per * count]
+    keys_sum, keys_sent, keys_came, send_sems, recv_sems = refs[per * count :]
+    seq, group = lax.axis_index("seq"), lax.axis_index("fsdp")
+    own = [bit_of(group, bit) for bit in bits]
+    partners = [("seq", flip_all(seq, k)) for k in range(1, length)]
+    partners += [("fsdp", flip(group, bit)) for bit in bits]
+    greet(partners)
+    copies = Copies(send_sems, recv_sems)
+    half = length // 2
+    side = lax.div(seq, half)
+    low = [side * half, (1 - side) * half]
+    orders = [list(range(far))[::-1], list(range(far))]
+    stages = far + 2
+    everything = (slice(None),) * (1 + far)
+    rows, key_width = keys_sum.shape[0], window.shape[2]
+    left = lax.rem(seq + length - 1, length)
+
+    def buffers(t):
+        held = scratch[per * t : per * (t + 1)]
+        return held[0], held[1], held[2 : 2 + far], held[2 + far]
+
+    def key_piece(b, part):
+        return window[part, pl.ds(b * rows, rows)]
+
+    def send_keys(j):
+        copy = copies.start(keys_sent.at[j], keys_came.at[j], "seq", left, seq >= 1)
+        return copy
+
+    def advance_keys(j, copy):
+        for part in (0, 1):
+            keys_sum[:, pl.ds(part * key_width, key_width)] = key_piece(j, part)
+
+        @pl.when(seq + 1 < length)
+        def _():
+            copy.wait_recv()
+            keys_sum[...] = keys_sum[...] + keys_came[j - 1].astype(jnp.float32)
+
+        if j < back:
+            keys_sent[j] = keys_sum[...].astype(keys_sent.dtype)
+            return send_keys(j)
+        keys_out[...] = keys_sum[...].astype(keys_out.dtype)
+        return None
+
+    def produce(t):
+        held = buffers(t)[0]
+        if t == weights:
+            held[...] = ready[...]
+            return
+        block = held.shape[-2]
+
+        def body(z, carry):
+            start = 0
+            for a, g in plan[t]:
+                depth = acts[a].shape[0] // length
+                left_rows = acts[a][pl.ds(pl.multiple_of(z * depth, depth), depth)]
+                source = keys_out if g is None else grads[g]
+                for c in range(0, source.shape[1], 512):
+                    tile = jnp.dot(left_rows, source[:, c : c + 512], preferred_element_type=jnp.float32)
+                    tile = tile.astype(held.dtype).reshape((2,) * (far + 1) + (block, 512))
+                    held[(z, *(slice(None),) * (far + 2), pl.ds(start, 512))] = tile
+                    start += 512
+            return carry
+
+        lax.fori_loop(0, length, body, 0)
+
+    def add(held, came, lead, fixed, inner_of):
+        start, size = lead
+        free = [d for d in range(far) if d not in fixed]
+
+        def body(i, carry):
+            z = lax.div(i, 2 ** len(free))
+            where, inner = [own[d] for d in range(far)], []
+            for k, d in enumerate(free):
+                where[d] = lax.rem(lax.div(i, 2 ** (len(free) - 1 - k)), 2)
+                inner.append(where[d])
+            place = (start + z, *where, own[far])
+            total = held[place].astype(jnp.float32) + came[inner_of(start + z, z, inner)].astype(jnp.float32)
+            held[place] = total.astype(held.dtype)
+            return carry
+
+        lax.fori_loop(0, size * 2 ** len(free), body, 0)
+
+    def launch(t, stage):
+        held, came_core, came_far, came_seq = buffers(t)
+        if stage == 0:
+            produce(t)
+            return [copies.start(held.at[(*everything, 1 - own[far])], came_core, "fsdp", flip(group, bits[far]))]
+        made = []
+        if stage <= far:
+            for part in (0, 1):
+                order = orders[part]
+                if stage == 1:
+                    add(held, came_core, (low[part], half), [], lambda z, at, inner: (z, *inner))
+                else:
+                    came = came_far[stage - 2].at[part]
+                    add(held, came, (low[part], half), order[: stage - 1], lambda z, at, inner: (at, *inner))
+                dim = order[stage - 1]
+                where = [slice(None)] * far
+                for d in order[: stage - 1]:
+                    where[d] = own[d]
+                where[dim] = 1 - own[dim]
+                source = held.at[(pl.ds(low[part], half), *where, own[far])]
+                made.append(
+                    copies.start(source, came_far[stage - 1].at[part], "fsdp", flip(group, bits[dim]))
+                )
+            return made
+        for part in (0, 1):
+            add(held, came_far[far - 1].at[part], (low[part], half), orders[part], lambda z, at, inner: (at,))
+        for k in range(1, length):
+            other = flip_all(seq, k)
+            made.append(copies.start(held.at[(other, *own)], came_seq.at[k - 1], "seq", other))
+        return made
+
+    def close(t):
+        held, _, _, came_seq = buffers(t)
+        total = held[(seq, *own)].astype(jnp.float32)
+        for k in range(1, length):
+            total = total + came_seq[k - 1].astype(jnp.float32)
+        start = 0
+        for out, size in zip(outs[t], cuts[t]):
+            out[...] = total[:, start : start + size]
+            start += size
+
+    for part in (0, 1):
+        keys_sent[0, :, pl.ds(part * key_width, key_width)] = key_piece(0, part).astype(keys_sent.dtype)
+    flying = send_keys(0)
+    waiting = [[] for _ in range(count)]
+    for step in range(count + stages - 1):
+        for t in range(count):
+            stage = step - t
+            if 0 < stage < stages:
+                for copy in waiting[t]:
+                    copy.wait_recv()
+            if stage == 0 and t == keys_at:
+                advance_keys(back, flying)
+            if 0 <= stage < stages:
+                waiting[t] = launch(t, stage)
+        if 1 <= step < back:
+            flying = advance_keys(step, flying)
+    for t in range(count):
+        for copy in waiting[t]:
+            copy.wait_recv()
+        close(t)
+    copies.finish()
+
+
+def sum_dense(acts, grads, ready, window, cuts, plan, collective_id):
+    length, groups = lax.axis_size("seq"), lax.axis_size("fsdp")
+    bits, bit = [], groups // 2
+    while bit >= 1:
+        bits.append(bit)
+        bit //= 2
+    far = len(bits) - 1
+    devices = length * groups
+    rows = grads[0].shape[0]
+    back = window.shape[1] // rows - 1
+    key_width = 2 * window.shape[2]
+    blocks = [
+        ((acts[group[0][0]].shape[0] // devices, sum(cut)), grads[0].dtype) for group, cut in zip(plan, cuts)
+    ]
+    keys_at = [any(g is None for _, g in group) for group in plan].index(True)
+    blocks.append((ready.shape[1:], ready.dtype))
+    count = len(blocks)
+    number = count * (1 + 2 * far + length - 1) + back
+    scratch = []
+    for block, dtype in blocks:
+        scratch.append(pltpu.VMEM((length,) + (2,) * (far + 1) + block, dtype))
+        scratch.append(pltpu.VMEM((length,) + (2,) * far + block, dtype))
+        scratch += [pltpu.VMEM((2, length // 2) + (2,) * (far - 1 - s) + block, dtype) for s in range(far)]
+        scratch.append(pltpu.VMEM((length - 1,) + block, dtype))
+    scratch.append(pltpu.VMEM((rows, key_width), jnp.float32))
+    scratch += [pltpu.VMEM((back, rows, key_width), grads[0].dtype)] * 2
+    elements = sum(math.prod(block) for block, _ in blocks) * devices
+    return pl.pallas_call(
+        functools.partial(sum_dense_kernel, length, bits, cuts, plan, keys_at, back),
+        out_shape=[
+            jax.ShapeDtypeStruct((block[0], size), jnp.float32)
+            for (block, _), cut in zip(blocks, cuts)
+            for size in cut
+        ]
+        + [jax.ShapeDtypeStruct((rows, key_width), grads[0].dtype)],
+        in_specs=[pl.BlockSpec(memory_space=pltpu.VMEM)] * (len(acts) + len(grads) + 2),
+        out_specs=[pl.BlockSpec(memory_space=pltpu.VMEM)] * (sum(len(cut) for cut in cuts) + 1),
+        scratch_shapes=scratch + [pltpu.SemaphoreType.DMA((number,))] * 2,
+        compiler_params=pltpu.CompilerParams(
+            collective_id=collective_id, has_side_effects=True, vmem_limit_bytes=67 * 10**6
+        ),
+        cost_estimate=pl.CostEstimate(
+            flops=2 * elements * rows, bytes_accessed=4 * elements, transcendentals=0
+        ),
+        name="sum_dense",
+    )(*acts, *grads, ready.reshape((length,) + (2,) * len(bits) + ready.shape[1:]), window)
+
+
 def row_dims():
     groups = lax.axis_size("fsdp")
     dims, bit = [("seq", 1)], groups // 2
@@ -839,7 +1045,7 @@
     length, groups = lax.axis_size("seq"), lax.axis_size("fsdp")
     seq_index, group_index = lax.axis_index("seq"), lax.axis_index("fsdp")
     devices = length * groups
-    tok_rows = tokens.shape[1]
+    tok_rows, feat_width = tokens.shape[1], tokens.shape[2]
     seq_len = segment_ids.shape[1]
     score_scale = 1.0 / math.sqrt(HEAD)
     key_width = KV_HEADS * HEAD
@@ -999,30 +1205,49 @@
     grad_query, grad_key_value = attend_back(
         query_rows, key_value_all, seg_rows, seg_line, log_total, grad_attended, score_scale
     )
-    grad_key_value = jnp.concatenate([grad_key_value[0], grad_key_value[1]], axis=1)
-    total = grad_key_value[:tok_rows]
-    for step in range(1, back + 1):
-        came = shift(total.astype(BF16), "seq", -1)
-        total = came.astype(F32) + grad_key_value[step * tok_rows : (step + 1) * tok_rows]
-    grad_qkv = jnp.concatenate([grad_query, total.astype(BF16)], axis=1)
-    expert_up_own = expert_grad(slot_rows, grad_up_rows, [total])
+    expert_up_own = expert_grad(slot_rows, grad_up_rows, [])
+    gain_grads = jnp.pad(grad_gain_two.reshape(devices, 1, -1), ((0, 0), (0, 7), (0, 0)))
+    gain_rows = gain_grads.shape[2]
+    gain_grads = jnp.pad(gain_grads, ((0, 0), (0, 0), (0, lanes - gain_rows)))
+    if gain_rows % 16 == 0:
+        sums = sum_dense(
+            [normed_two.T, attended.T, shared_hidden.T, normed_one.T],
+            [grad_gate_up, grad_mixed_low, grad_low, grad_query],
+            gain_grads,
+            grad_key_value,
+            ((shared_width, shared_width), (query_width, feat_width), (key_width, key_width), (feat_width,), (lanes,)),
+            (((0, 0),), ((3, 3), (1, 1)), ((3, None),), ((2, 2),)),
+            5,
+        )
+        gate_up_blocks, query_block, grad_output_block = sums[:2], sums[2], sums[3]
+        qkv_blocks = [query_block, sums[4], sums[5]]
+        grad_down_block, grad_gain_block = sums[6:8]
+        grad_qkv = jnp.concatenate([grad_query, sums[8]], axis=1)
+    else:
+        grad_key_value = jnp.concatenate([grad_key_value[0], grad_key_value[1]], axis=1)
+        total = grad_key_value[:tok_rows]
+        for step in range(1, back + 1):
+            came = shift(total.astype(BF16), "seq", -1)
+            total = came.astype(F32) + grad_key_value[step * tok_rows : (step + 1) * tok_rows]
+        grad_qkv = jnp.concatenate([grad_query, total.astype(BF16)], axis=1)
+        dense_grads = [
+            weight_grad(normed_two, grad_gate_up),
+            weight_grad(attended, grad_mixed_low),
+            weight_grad(shared_hidden, grad_low),
+            weight_grad(normed_one, grad_qkv),
+            gain_grads,
+        ]
+        sums = scatter_dense(dense_grads, 5)
+        gate_up_blocks, grad_output_block, grad_down_block, qkv_blocks, grad_gain_block = sums
+        gate_up_blocks = jnp.split(gate_up_blocks, [shared_width], axis=1)
+        qkv_blocks = jnp.split(qkv_blocks, [query_width, query_width + key_width], axis=1)
     grad_normed_one = dot(grad_qkv, qkv_full, 1, 1)
-    _, pull_one = jax.vjp(rms_norm, x_float, gain_one)
-    grad_x_norm, grad_gain_one = pull_one(grad_normed_one)
-    grad_tokens = grad_mixed + grad_x_norm
-
-    gain_grads = jnp.stack([grad_gain_one, grad_gain_two]).reshape(2, devices, -1).swapaxes(0, 1)
-    gain_rows = gain_grads.shape[2]
-    gain_grads = jnp.pad(gain_grads, ((0, 0), (0, 6), (0, lanes - gain_rows)))
-    dense_grads = [
-        weight_grad(normed_two, grad_gate_up),
-        weight_grad(normed_one, grad_qkv),
-        weight_grad(attended, grad_mixed_low),
-        weight_grad(shared_hidden, grad_low),
-        gain_grads,
-    ]
-    sums = scatter_dense(dense_grads, 5)
-    grad_gate_up_block, grad_qkv_block, grad_output_block, grad_down_block, grad_gain_block = sums
+    _, pull_one = jax.vjp(lambda values: rms_norm(values, gain_one), x_float)
+    grad_tokens = grad_mixed + pull_one(grad_normed_one)[0]
+    grad_gain_one = sum(
+        jnp.sum(weight.astype(F32) * grad, axis=1)
+        for weight, grad in zip((query_weight, key_weight, value_weight), qkv_blocks)
+    ) / norm1_gain.astype(F32)
     last = [grad_gain_block]
     grad_expert_down = expert_sum(expert_down_own, last)
     grad_expert_gate = expert_sum(expert_gate_own, last)
@@ -1030,14 +1255,11 @@
     return (
         block_output[None],
         grad_tokens[None],
+        grad_gain_one,
+        *qkv_blocks,
+        grad_output_block,
         grad_gain_block[0, :gain_rows],
-        grad_qkv_block[:, :query_width],
-        grad_qkv_block[:, query_width : query_width + key_width],
-        grad_qkv_block[:, query_width + key_width :],
-        grad_output_block,
-        grad_gain_block[1, :gain_rows],
-        grad_gate_up_block[:, :shared_width],
-        grad_gate_up_block[:, shared_width:],
+        *gate_up_blocks,
         grad_down_block,
         grad_expert_gate,
         grad_expert_up,

time: 960 us -> 945 us (0.984)
  waiting for transfers between devices: 95.4 us -> 122 us
  starting transfers between devices: 43.9 us -> 18.8 us
  matrix products: 108 us -> 96.1 us
  Pallas kernels: 632 us -> 621 us
    ppermute x15, waiting for transfers between devices: 61.6 us -> 122 us  [exchange(): return lax.ppermute(values, axis, [(i, i ^ bit) for i in range(count)])]
    ppermute x2 -> x0, waiting for transfers between devices: 33.8 us -> none  [shift(): return lax.ppermute(values, axis, pairs)]
    ppermute x15, starting transfers between devices: 41 us -> 18.8 us  [exchange(): return lax.ppermute(values, axis, [(i, i ^ bit) for i in range(count)])]
    pallas_call x1, Pallas kernels: 148 us -> 129 us  [sum_dense(): pl.pallas_call(functools.partial(sum_dense_kernel, length, bits, cuts, pl...]
    dot_general x11 -> x7, matrix products: 47 us -> 30.6 us  [dot(): lax.dot_general(left, right, (((left_dim,), (right_dim,)), ((), ())), pre...]
  transfers between devices with their start and end apart: 17 -> 15, of which waited for: 6 -> 3; matrix products, arithmetic and copies ran while one was open for 8% -> 8% of each run, Pallas kernels for 28% -> 37%
where the time goes in v4:
time: 945 us; the launch traced here: 941 us
  Pallas kernels  621 us (66%)
  waiting for transfers between devices  122 us (13%)
  matrix products  96.1 us (10%)
  local copies, waits for them, and re-layouts  45.3 us (5%)
  other arithmetic  35.6 us (4%)
  starting transfers between devices  18.8 us (2%)
    pallas_call x2, Pallas kernels, gather_rows(): pl.pallas_call(functools.partial(gather_rows_kernel, dims, orders, held),...  171 us
    pallas_call x2, Pallas kernels, scatter_rows(): pl.pallas_call(kernel, out_shape=jax.ShapeDtypeStruct((count, feat), jnp....  151 us
    pallas_call x1, Pallas kernels, gather_dense(): pl.pallas_call(functools.partial(gather_dense_kernel, length, bits, count...  151 us
    pallas_call x1, Pallas kernels, sum_dense(): pl.pallas_call(functools.partial(sum_dense_kernel, length, bits, cuts, pl...  129 us
    ppermute x15, waiting for transfers between devices, exchange(): return lax.ppermute(values, axis, [(i, i ^ bit) for i in range(count)])  122 us
    dot_general x9, matrix products, batch_dot(): lax.dot_general(left, right, (((left_dim,), (right_dim,)), ((0,), (0,))),...  65.3 us
    dot_general x7, matrix products, dot(): lax.dot_general(left, right, (((left_dim,), (right_dim,)), ((), ())), pre...  30.6 us
  transfers between devices with their start and end apart: 15, of which 3 were waited for; matrix products, arithmetic and copies ran while one was open for 8% of the time, Pallas kernels for 37%

profile of v4, /device:TPU:0, one launch (start us, length us, event | category | flops | bytes accessed | tf_op | source)
XLA Modules:
  0.0 940.9 jit_solution(6734721234750490892)
XLA Ops:
  4.4 1.6 pad_maximum_fusion.1.refs_2_
  6.0 1.7 fusion.29.refs_0_
  7.7 150.7 %gather_dense.1 = (bf16[4,2,2,2,48,2688]{5,4,3,2,1,0:T(8,128)(2,1)}, bf16[4,2,2,2,48,1536]{5,4,3,2,1,0:T(8,128)(2,1)}, bf16[4,2,2,2,48,2048]{5,4,3,2,1,0:T(8,128...) custom-call(bf16[48,2688]{1,0:T(8,128)(2,1)} %fusion.29.refs_0_, ...), custom_call_target="tpu_custom_call" | custom-call | bytes 68812800 | tf_op jit(solution)/shard_map/gather_dense/pallas_call | solution.py:300
  159.8 1.4 copy-done.3
  162.3 8.1 attend.1
  170.4 4.9 multiply_reduce_fusion.2
  175.3 1.6 multiply_convert_fusion.3.rows_ref
  176.9 2.8 constant_dynamic-slice_fusion.10
  179.7 1.5 collective-permute-start.5
  181.2 1.2 constant_dynamic-slice_fusion.13
  182.4 2.4 collective-permute-start.2
  187.2 1.2 copy.115
  188.4 1.6 fusion.73
  191.1 2.3 copy.116
  193.4 1.2 copy.117.refs_0_
  194.5 4.6 fusion.38
  199.1 1.3 copy-done.22
  201.8 4.7 fusion.39
  207.3 118.5 %gather_rows.2 = bf16[2,2,2,2,2,64,1536]{6,5,4,3,2,1,0:T(8,128)(2,1)S(1)} custom-call(bf16[256,1536]{1,0:T(8,128)(2,1)S(1)} %multiply_convert_fusion.3.rows_ref, bf16[2,2,2,2,128,256]{5,4,3,2,1,0:T(8,128)(2,1)S(1)} %and_convert_fusion.pick_ref), custom_call_target="tpu_custom_call" | custom-call | flops 1610612736 | bytes 37748736 | tf_op jit(solution)/shard_map/gather_rows/pallas_call | solution.py:767
  325.8 2.7 copy-done
  328.7 1.4 dynamic-slice_dynamic-update-slice_fusion.1
  330.3 1.7 copy-done.1
  332.0 5.4 fusion.40
  337.5 1.8 constant_dynamic-update-slice_fusion.5
  339.3 1.2 constant_dynamic-update-slice_fusion.4
  340.5 1.2 constant_dynamic-update-slice_fusion.3
  341.8 5.5 multiply_convert_fusion.2
  347.3 26.0 %collective-permute-done.4 = bf16[2,128,1536]{2,1,0:T(8,128)(2,1)S(1)} collective-permute-done((bf16[2,128,1536]{2,1,0:T(8,128)(2,1)S(1)}, bf16[2,128,1536]{2,1,0:T(8,128)(2,1)S(1)}, u32[]{:S(2)}, u32[]{:S(2)}) %collective-permute-start.4) | collective-permute-done | bytes 786464 | tf_op jit(solution)/shard_map/ppermute | solution.py:27
  373.3 1.2 constant_dynamic-update-slice_fusion.2
  374.5 1.2 constant_dynamic-update-slice_fusion
  375.7 3.6 multiply_convert_fusion
  379.4 61.5 %scatter_rows.2 = f32[256,1536]{1,0:T(8,128)S(1)} custom-call(bf16[2,2,2,2,2,64,1536]{6,5,4,3,2,1,0:T(8,128)(2,1)S(1)} %bitcast.99, bf16[2,2,2,2,128,256]{5,4,3,2,1,0:T(8,128)(2,1)S(1)} %and_convert_fusion.pick_ref), custom_call_target="tpu_custom_call" | custom-call | flops 1610612736 | bytes 37748736 | tf_op jit(solution)/shard_map/scatter_rows/pallas_call | solution.py:881
  440.9 3.4 fusion.24
  444.3 2.1 fusion.22
  446.4 52.6 %gather_rows.3 = bf16[2,2,2,2,2,64,1536]{6,5,4,3,2,1,0:T(8,128)(2,1)S(1)} custom-call(bf16[256,1536]{1,0:T(8,128)(2,1)S(1)} %get-tuple-element.106.rows_ref.refs_6_, bf16[2,2,2,2,128,256]{5,4,3,2,1,0:T(8,128)(2,1)S(1)} %and_convert_fusion.pick_ref), custom_call_target="tpu_custom_call" | custom-call | flops 1610612736 | bytes 37748736 | tf_op jit(solution)/shard_map/gather_rows/pallas_call | solution.py:767
  499.1 3.9 fusion
  502.9 6.9 convolution_convert_fusion
  509.8 13.0 %multiply_convert_fusion.1 = (bf16[2,1024,512]{2,1,0:T(8,128)(2,1)}, bf16[2,1024,512]{2,1,0:T(8,128)(2,1)}) fusion(f32[2,1024,512]{2,1,0:T(8,128)} %copy-done.47, f32[2,1024,512]{2,1,0:T(8,128)} %get-tuple-element.138, bf16[2,1024,1536]{2,1,0:T(8,128)(2,1)} %fusion, bf16[2,512,1536]{2,1,0:T(8,128)(2,1)} %copy-done.18), kind=kOutput, calls=%fused_computation.10 | convolution fusion | flops 3235905536 | bytes 22020096 | tf_op jit(solution)/shard_map/dot_general | solution.py:47
  522.8 5.5 convolution_convert_fusion.2
  528.3 10.5 %fusion.41 = f32[2,1024,1536]{2,1,0:T(8,128)} fusion(bf16[2,1024,512]{2,1,0:T(8,128)(2,1)} %get-tuple-element.109, bf16[2,1536,512]{2,1,0:T(8,128)(2,1)} %get-tuple-element.64), kind=kOutput, calls=%fused_computation.129 | convolution fusion | flops 3221225472 | bytes 17825792 | tf_op jit(solution)/shard_map/dot_general | solution.py:47
  538.8 1.8 constant_dynamic-slice_fusion.1
  540.6 4.0 collective-permute-start.14
  545.2 5.3 convolution_convert_fusion.1
  550.5 1.8 constant_dynamic-slice_fusion.5
  552.4 1.8 constant_dynamic-slice_fusion.9
  554.2 3.8 collective-permute-start.11
  558.0 9.6 %add_convert_fusion = bf16[2,1024,1536]{2,1,0:T(8,128)(2,1)S(1)} fusion(f32[2,1024,1536]{2,1,0:T(8,128)} %fusion.41, bf16[2,1024,512]{2,1,0:T(8,128)(2,1)} %get-tuple-element.108, bf16[2,1536,512]{2,1,0:T(8,128)(2,1)} %copy-done.10), kind=kOutput, calls=%fused_computation.2 | convolution fusion | flops 3227516928 | bytes 24117248 | tf_op jit(solution)/shard_map/dot_general | solution.py:47
  567.6 89.6 %scatter_rows.3 = f32[256,1536]{1,0:T(8,128)S(1)} custom-call(bf16[2,2,2,2,2,64,1536]{6,5,4,3,2,1,0:T(8,128)(2,1)S(1)} %bitcast.98, bf16[2,2,2,2,128,256]{5,4,3,2,1,0:T(8,128)(2,1)S(1)} %and_convert_fusion.pick_ref), custom_call_target="tpu_custom_call" | custom-call | flops 1610612736 | bytes 37748736 | tf_op jit(solution)/shard_map/scatter_rows/pallas_call | solution.py:881
  658.4 5.7 multiply_reduce_fusion
  664.1 3.4 fusion.35
  667.6 2.3 convolution_convert_fusion.3.grad
  671.8 11.5 %attend_back.1 = (bf16[256,1536]{1,0:T(8,128)(2,1)S(1)}, f32[2,768,512]{2,1,0:T(8,128)S(1)}) custom-call(bf16[256,1536]{1,0:T(8,128)(2,1)S(1)} %copy-done.6, bf16[768,1024]{1,0:T(8,128)(2,1)S(1)} %copy-done.4, bf16[768,1024]{1,0:T(8,128)(2,1)S(1)} %copy-done.4, s32[256,1]{1,0:T(8,128)S(1)} %copy.106.seg_rows, s32[1,768]{1,0:T(1,128)S(1)} %broadcast_in_dim.149.seg_keys, ...), custom_call_target="tpu_custom_call" | custom-call | flops 3019898880 | bytes 6291456 | tf_op jit(solution)/shard_map/attend_back/pallas_call | solution.py:999
  683.3 1.7 copy-done.8
  685.9 128.6 %sum_dense.1 = (f32[48,1024]{1,0:T(8,128)}, f32[48,1024]{1,0:T(8,128)}, f32[48,1536]{1,0:T(8,128)}, f32[48,1536]{1,0:T(8,128)}, f32[48,512]{1,0:T(8,128)}, /*ind...) custom-call(bf16[1536,256]{1,0:T(8,128)(2,1)} %copy.117.refs_0_, ...), custom_call_target="tpu_custom_call" | custom-call | flops 5653921792 | bytes 44171264 | tf_op jit(solution)/shard_map/sum_dense/pallas_call | solution.py:654
  814.6 6.2 fusion.14
  821.2 1.2 slice_bitcast_fusion
  822.4 2.9 collective-permute-start.8
  827.4 1.5 fusion.13
  829.0 48.6 %collective-permute-done.9 = bf16[2,384,512]{2,1,0:T(8,128)(2,1)S(1)} collective-permute-done((bf16[2,384,512]{2,1,0:T(8,128)(2,1)S(1)}, bf16[2,384,512]{2,1,0:T(8,128)(2,1)S(1)}, u32[]{:S(2)}, u32[]{:S(2)}) %collective-permute-start.9) | collective-permute-done | bytes 786464 | tf_op jit(solution)/shard_map/ppermute | solution.py:27
  877.6 47.7 %collective-permute-done.6 = bf16[2,384,512]{2,1,0:T(8,128)(2,1)S(1)} collective-permute-done((bf16[2,384,512]{2,1,0:T(8,128)(2,1)S(1)}, bf16[2,384,512]{2,1,0:T(8,128)(2,1)S(1)}, u32[]{:S(2)}, u32[]{:S(2)}) %collective-permute-start.6) | collective-permute-done | bytes 786464 | tf_op jit(solution)/shard_map/ppermute | solution.py:27
  925.3 2.1 convert_add_fusion.1
  927.4 2.1 bitcast_select_fusion
  929.5 1.9 convert_add_fusion.3
  931.9 4.0 bitcast_select_fusion.1
  (178 shorter events, 24.6 us)
Async XLA Ops:
  159.4 10.9 %copy-start.16 = (bf16[1,256,1536]{2,1,0:T(8,128)(2,1)S(1)}, bf16[1,256,1536]{2,1,0:T(8,128)(2,1)}, u32[]{:S(2)}) copy-start(bf16[1,256,1536]{2,1,0:T(8,128)(2,1)} %param.18) | copy-start | bytes 2359300
  159.7 1.4 copy-start.3
  176.9 4.3 copy-start.13
  176.9 9.9 %copy-start.43 = (f32[4,2,2,2,16,256]{5,4,3,2,1,0:T(8,128)S(1)}, f32[4,2,2,2,16,256]{5,4,3,2,1,0:T(8,128)}, u32[]{:S(2)}) copy-start(f32[4,2,2,2,16,256]{5,4,3,2,1,0:T(8,128)} %get-tuple-element.63) | copy-start | bytes 1572868
  179.7 167.6 %collective-permute-start.5 = (bf16[2,128,1536]{2,1,0:T(8,128)(2,1)}, bf16[2,128,1536]{2,1,0:T(8,128)(2,1)}, u32[]{:S(2)}, u32[]{:S(2)}) collective-permute-start(bf16[2,128,1536]{2,1,0:T(8,128)(2,1)} %get-tuple-element.126), channel_id=1, source_target_pairs={{0,24},{8,16},{16,8},{24,0},{1,25},{9,17},{17,9},{25,1},{2,26},{10... | collective-permute-start | bytes 2359304 | tf_op jit(solution)/shard_map/ppermute | solution.py:27
  181.2 192.1 %collective-permute-start.3 = (bf16[2,128,1536]{2,1,0:T(8,128)(2,1)}, bf16[2,128,1536]{2,1,0:T(8,128)(2,1)}, u32[]{:S(2)}, u32[]{:S(2)}) collective-permute-start(bf16[2,128,1536]{2,1,0:T(8,128)(2,1)} %get-tuple-element.126), channel_id=1, source_target_pairs={{0,8},{8,0},{16,24},{24,16},{1,9},{9,1},{17,25},{25,17},{2,10},{10... | collective-permute-start | bytes 2359304 | tf_op jit(solution)/shard_map/ppermute | solution.py:27
  182.4 155.0 %collective-permute-start.2 = (bf16[2,384,512]{2,1,0:T(8,128)(2,1)}, bf16[2,384,512]{2,1,0:T(8,128)(2,1)}, u32[]{:S(2)}, u32[]{:S(2)}) collective-permute-start(bf16[2,384,512]{2,1,0:T(8,128)(2,1)} %get-tuple-element.128), channel_id=1, source_target_pairs={{0,24},{8,16},{16,8},{24,0},{1,25},{9,17},{17,9},{25,1},{2,26},{10... | collective-permute-start | bytes 2359304 | tf_op jit(solution)/shard_map/ppermute | solution.py:27
  184.8 152.7 %collective-permute-start = (bf16[2,384,512]{2,1,0:T(8,128)(2,1)}, bf16[2,384,512]{2,1,0:T(8,128)(2,1)}, u32[]{:S(2)}, u32[]{:S(2)}) collective-permute-start(bf16[2,384,512]{2,1,0:T(8,128)(2,1)} %get-tuple-element.128), channel_id=1, source_target_pairs={{0,8},{8,0},{16,24},{24,16},{1,9},{9,1},{17,25},{25,17},{2,10},{10... | collective-permute-start | bytes 2359304 | tf_op jit(solution)/shard_map/ppermute | solution.py:27
  185.9 151.6 %collective-permute-start.1 = (bf16[2,384,512]{2,1,0:T(8,128)(2,1)}, bf16[2,384,512]{2,1,0:T(8,128)(2,1)}, u32[]{:S(2)}, u32[]{:S(2)}) collective-permute-start(bf16[2,384,512]{2,1,0:T(8,128)(2,1)} %get-tuple-element.127), channel_id=1, source_target_pairs={{0,16},{8,24},{16,0},{24,8},{1,17},{9,25},{17,1},{25,9},{2,18},{10... | collective-permute-start | bytes 2359304 | tf_op jit(solution)/shard_map/ppermute | solution.py:27
  186.8 3.3 copy-start.44
  199.1 1.3 copy-start.22
  325.8 2.7 copy-start
  328.5 1.8 copy-start.14
  328.7 3.3 copy-start.1
  332.0 5.4 copy-start.27
  337.4 9.9 %copy-start.47 = (f32[2,1024,512]{2,1,0:T(8,128)}, f32[2,1024,512]{2,1,0:T(8,128)S(1)}, u32[]{:S(2)}) copy-start(f32[2,1024,512]{2,1,0:T(8,128)S(1)} %fusion.40) | copy-start | bytes 12582916
  337.4 35.8 %collective-permute-start.4 = (bf16[2,128,1536]{2,1,0:T(8,128)(2,1)S(1)}, bf16[2,128,1536]{2,1,0:T(8,128)(2,1)S(1)}, u32[]{:S(2)}, u32[]{:S(2)}) collective-permute-start(bf16[2,128,1536]{2,1,0:T(8,128)(2,1)S(1)} %copy-done.27), channel_id=1, source_target_pairs={{0,16},{8,24},{16,0},{24,8},{1,17},{9,25},{17,1},{25,9},{2,18},{10... | collective-permute-start | bytes 2359304 | tf_op jit(solution)/shard_map/ppermute | solution.py:27
  341.7 5.5 copy-start.10
  347.3 32.1 %copy-start.48 = (bf16[2,1024,512]{2,1,0:T(8,128)(2,1)}, bf16[2,1024,512]{2,1,0:T(8,128)(2,1)S(1)}, u32[]{:S(2)}) copy-start(bf16[2,1024,512]{2,1,0:T(8,128)(2,1)S(1)} %get-tuple-element.137) | copy-start | bytes 6291460
  375.7 3.7 copy-start.18
  379.4 61.5 %copy-start.15 = (bf16[1,256,1536]{2,1,0:T(8,128)(2,1)S(1)}, bf16[1,256,1536]{2,1,0:T(8,128)(2,1)}, u32[]{:S(2)}) copy-start(bf16[1,256,1536]{2,1,0:T(8,128)(2,1)} %param.19) | copy-start | bytes 2359300
  379.4 61.5 %copy-start.24 = (f32[256,1536]{1,0:T(8,128)S(1)}, f32[256,1536]{1,0:T(8,128)}, u32[]{:S(2)}) copy-start(f32[256,1536]{1,0:T(8,128)} %fusion.39) | copy-start | bytes 4718596
  440.9 3.4 copy-start.23
  440.9 3.4 copy-start.46
  444.3 2.1 copy-start.2
  446.4 210.9 %copy-start.33 = (bf16[256,1024]{1,0:T(8,128)(2,1)}, bf16[256,1024]{1,0:T(8,128)(2,1)S(1)}, u32[]{:S(2)}) copy-start(bf16[256,1024]{1,0:T(8,128)(2,1)S(1)} %get-tuple-element.122) | copy-start | bytes 1572868
  540.6 281.8 %collective-permute-start.14 = (bf16[2,128,1536]{2,1,0:T(8,128)(2,1)}, bf16[2,128,1536]{2,1,0:T(8,128)(2,1)}, u32[]{:S(2)}, u32[]{:S(2)}) collective-permute-start(bf16[2,128,1536]{2,1,0:T(8,128)(2,1)} %get-tuple-element.111), channel_id=1, source_target_pairs={{0,24},{8,16},{16,8},{24,0},{1,25},{9,17},{17,9},{25,1},{2,26},{10... | collective-permute-start | bytes 2359304 | tf_op jit(solution)/shard_map/ppermute | solution.py:27
  544.7 277.8 %collective-permute-start.13 = (bf16[2,128,1536]{2,1,0:T(8,128)(2,1)}, bf16[2,128,1536]{2,1,0:T(8,128)(2,1)}, u32[]{:S(2)}, u32[]{:S(2)}) collective-permute-start(bf16[2,128,1536]{2,1,0:T(8,128)(2,1)} %get-tuple-element.112), channel_id=1, source_target_pairs={{0,8},{8,0},{16,24},{24,16},{1,9},{9,1},{17,25},{25,17},{2,10},{10... | collective-permute-start | bytes 2359304 | tf_op jit(solution)/shard_map/ppermute | solution.py:27
  544.7 280.7 %collective-permute-start.12 = (bf16[2,128,1536]{2,1,0:T(8,128)(2,1)}, bf16[2,128,1536]{2,1,0:T(8,128)(2,1)}, u32[]{:S(2)}, u32[]{:S(2)}) collective-permute-start(bf16[2,128,1536]{2,1,0:T(8,128)(2,1)} %get-tuple-element.113), channel_id=1, source_target_pairs={{0,16},{8,24},{16,0},{24,8},{1,17},{9,25},{17,1},{25,9},{2,18},{10... | collective-permute-start | bytes 2359304 | tf_op jit(solution)/shard_map/ppermute | solution.py:27
  554.2 271.8 %collective-permute-start.11 = (bf16[2,384,512]{2,1,0:T(8,128)(2,1)}, bf16[2,384,512]{2,1,0:T(8,128)(2,1)}, u32[]{:S(2)}, u32[]{:S(2)}) collective-permute-start(bf16[2,384,512]{2,1,0:T(8,128)(2,1)} %get-tuple-element.115), channel_id=1, source_target_pairs={{0,24},{8,16},{16,8},{24,0},{1,25},{9,17},{17,9},{25,1},{2,26},{10... | collective-permute-start | bytes 2359304 | tf_op jit(solution)/shard_map/ppermute | solution.py:27
  558.0 271.0 %collective-permute-start.10 = (bf16[2,384,512]{2,1,0:T(8,128)(2,1)}, bf16[2,384,512]{2,1,0:T(8,128)(2,1)}, u32[]{:S(2)}, u32[]{:S(2)}) collective-permute-start(bf16[2,384,512]{2,1,0:T(8,128)(2,1)} %get-tuple-element.116), channel_id=1, source_target_pairs={{0,8},{8,0},{16,24},{24,16},{1,9},{9,1},{17,25},{25,17},{2,10},{10... | collective-permute-start | bytes 2359304 | tf_op jit(solution)/shard_map/ppermute | solution.py:27
  567.6 89.7 %copy-start.34 = (bf16[256,1024]{1,0:T(8,128)(2,1)S(1)}, bf16[256,1024]{1,0:T(8,128)(2,1)}, u32[]{:S(2)}) copy-start(bf16[256,1024]{1,0:T(8,128)(2,1)} %get-tuple-element.123) | copy-start | bytes 1572868
  567.6 99.9 %slice-start = ((s8[4718592]{0:T(1024)(128)(4,1)}), s8[4194304]{0:T(1024)(128)(4,1)S(1)}, s32[]{:S(2)}) async-start(s8[4718592]{0:T(1024)(128)(4,1)} %bitcast.125), calls=%async_computation | async-start | bytes 8388608
  658.3 5.8 copy-start.12
  658.3 9.2 slice-start.1
  667.5 2.4 copy-start.26
  667.5 3.1 copy-start.4
  667.6 3.1 copy-start.6
  670.7 1.1 copy-start.7
  683.3 1.7 copy-start.8
  814.5 6.4 copy-start.35
  814.5 6.4 copy-start.36
  814.5 6.4 copy-start.41
  814.5 6.4 copy-start.42
  814.5 6.5 copy-start.25
  814.6 6.5 copy-start.32
  814.6 7.9 copy-start.30
  814.6 7.9 copy-start.31
  814.6 10.8 %copy-start.29 = (bf16[2,384,512]{2,1,0:T(8,128)(2,1)S(1)}, bf16[2,384,512]{2,1,0:T(8,128)(2,1)}, u32[]{:S(2)}) copy-start(bf16[2,384,512]{2,1,0:T(8,128)(2,1)} %get-tuple-element.120) | copy-start | bytes 2359300
  814.6 11.3 %copy-start.28 = (bf16[2,384,512]{2,1,0:T(8,128)(2,1)S(1)}, bf16[2,384,512]{2,1,0:T(8,128)(2,1)}, u32[]{:S(2)}) copy-start(bf16[2,384,512]{2,1,0:T(8,128)(2,1)} %get-tuple-element.121) | copy-start | bytes 2359300
  814.6 12.3 %copy-start.45 = (bf16[48]{0:T(256)(128)(2,1)S(1)}, bf16[48]{0:T(256)(128)(2,1)}, u32[]{:S(2)}) copy-start(bf16[48]{0:T(256)(128)(2,1)} %param.24) | copy-start | bytes 292
  814.6 12.8 %copy-start.11 = (f32[256,1536]{1,0:T(8,128)S(1)}, f32[256,1536]{1,0:T(8,128)}, u32[]{:S(2)}) copy-start(f32[256,1536]{1,0:T(8,128)} %get-tuple-element.105) | copy-start | bytes 4718596
  814.6 12.8 %copy-start.17 = (bf16[1,256,1536]{2,1,0:T(8,128)(2,1)S(1)}, bf16[1,256,1536]{2,1,0:T(8,128)(2,1)}, u32[]{:S(2)}) copy-start(bf16[1,256,1536]{2,1,0:T(8,128)(2,1)} %param.18) | copy-start | bytes 2359300
  822.4 55.2 %collective-permute-start.9 = (bf16[2,384,512]{2,1,0:T(8,128)(2,1)S(1)}, bf16[2,384,512]{2,1,0:T(8,128)(2,1)S(1)}, u32[]{:S(2)}, u32[]{:S(2)}) collective-permute-start(bf16[2,384,512]{2,1,0:T(8,128)(2,1)S(1)} %copy-done.30), channel_id=1, source_target_pairs={{0,16},{8,24},{16,0},{24,8},{1,17},{9,25},{17,1},{25,9},{2,18},{10... | collective-permute-start | bytes 2359304 | tf_op jit(solution)/shard_map/ppermute | solution.py:27
  822.4 55.1 %collective-permute-start.8 = (bf16[2,384,512]{2,1,0:T(8,128)(2,1)S(1)}, bf16[2,384,512]{2,1,0:T(8,128)(2,1)S(1)}, u32[]{:S(2)}, u32[]{:S(2)}) collective-permute-start(bf16[2,384,512]{2,1,0:T(8,128)(2,1)S(1)} %copy-done.31), channel_id=1, source_target_pairs={{0,24},{8,16},{16,8},{24,0},{1,25},{9,17},{17,9},{25,1},{2,26},{10... | collective-permute-start | bytes 2359304 | tf_op jit(solution)/shard_map/ppermute | solution.py:27
  825.4 52.2 %collective-permute-start.7 = (bf16[2,384,512]{2,1,0:T(8,128)(2,1)S(1)}, bf16[2,384,512]{2,1,0:T(8,128)(2,1)S(1)}, u32[]{:S(2)}, u32[]{:S(2)}) collective-permute-start(bf16[2,384,512]{2,1,0:T(8,128)(2,1)S(1)} %copy-done.29), channel_id=1, source_target_pairs={{0,8},{8,0},{16,24},{24,16},{1,9},{9,1},{17,25},{25,17},{2,10},{10... | collective-permute-start | bytes 2359304 | tf_op jit(solution)/shard_map/ppermute | solution.py:27
  825.9 99.3 %collective-permute-start.6 = (bf16[2,384,512]{2,1,0:T(8,128)(2,1)S(1)}, bf16[2,384,512]{2,1,0:T(8,128)(2,1)S(1)}, u32[]{:S(2)}, u32[]{:S(2)}) collective-permute-start(bf16[2,384,512]{2,1,0:T(8,128)(2,1)S(1)} %copy-done.28), channel_id=1, source_target_pairs={{0,16},{8,24},{16,0},{24,8},{1,17},{9,25},{17,1},{25,9},{2,18},{10... | collective-permute-start | bytes 2359304 | tf_op jit(solution)/shard_map/ppermute | solution.py:27
  827.4 97.8 %copy-start.19 = (bf16[2,128,1536]{2,1,0:T(8,128)(2,1)S(1)}, bf16[2,128,1536]{2,1,0:T(8,128)(2,1)}, u32[]{:S(2)}) copy-start(bf16[2,128,1536]{2,1,0:T(8,128)(2,1)} %get-tuple-element.94) | copy-start | bytes 2359300
  927.3 2.1 copy-start.21
  929.5 1.9 copy-start.20
  931.9 6.0 copy-start.37
  931.9 6.7 copy-start.40
  931.9 7.4 copy-start.39
  931.9 8.1 copy-start.38
  (2 other events, 2.1 us)

commit v5 on v4

--- a/solution.py
+++ b/solution.py
@@ -246,24 +246,23 @@
         return [(copies.start(source, target, "seq", right, sends).wait_recv, seq >= j)]
 
     passing, passed = [], 0
-    for step in range(count + stages):
-        if step == hops + 1:
-            expert_waiting = ship_expert()
-        if passing:
-            settle(passing)
-            passing = []
-            if passed < back:
-                passed += 1
-                passing = pass_keys(passed)
+    starts = [(t + 1) // 2 for t in range(count)]
+    for step in range(starts[-1] + stages + 1):
         for t in range(count):
-            stage = step - t
+            stage = step - starts[t]
             if 0 < stage <= stages:
                 settle(waiting[t])
             if 0 <= stage < stages:
                 waiting[t] = launch(t, stage)
+        if step == starts[-1] + hops - 1:
+            expert_waiting = ship_expert()
         if step == stages and back is not None:
             passing, kept = project()
             passed = 1
+        elif passing and passed < back and step == stages + 2 * passed:
+            settle(passing)
+            passed += 1
+            passing = pass_keys(passed)
     while passing:
         settle(passing)
         passed += 1
@@ -605,9 +604,10 @@
         keys_sent[0, :, pl.ds(part * key_width, key_width)] = key_piece(0, part).astype(keys_sent.dtype)
     flying = send_keys(0)
     waiting = [[] for _ in range(count)]
-    for step in range(count + stages - 1):
+    starts = [min(t, count - 2) for t in range(count)]
+    for step in range(starts[-1] + stages):
         for t in range(count):
-            stage = step - t
+            stage = step - starts[t]
             if 0 < stage < stages:
                 for copy in waiting[t]:
                     copy.wait_recv()
@@ -615,8 +615,9 @@
                 advance_keys(back, flying)
             if 0 <= stage < stages:
                 waiting[t] = launch(t, stage)
-        if 1 <= step < back:
-            flying = advance_keys(step, flying)
+        hop = step - starts[keys_at] + back
+        if 1 <= hop < back:
+            flying = advance_keys(hop, flying)
     for t in range(count):
         for copy in waiting[t]:
             copy.wait_recv()
@@ -1215,13 +1216,13 @@
             [grad_gate_up, grad_mixed_low, grad_low, grad_query],
             gain_grads,
             grad_key_value,
-            ((shared_width, shared_width), (query_width, feat_width), (key_width, key_width), (feat_width,), (lanes,)),
-            (((0, 0),), ((3, 3), (1, 1)), ((3, None),), ((2, 2),)),
+            ((shared_width, shared_width), (query_width, feat_width), (feat_width,), (key_width, key_width), (lanes,)),
+            (((0, 0),), ((3, 3), (1, 1)), ((2, 2),), ((3, None),)),
             5,
         )
         gate_up_blocks, query_block, grad_output_block = sums[:2], sums[2], sums[3]
-        qkv_blocks = [query_block, sums[4], sums[5]]
-        grad_down_block, grad_gain_block = sums[6:8]
+        qkv_blocks = [query_block, sums[5], sums[6]]
+        grad_down_block, grad_gain_block = sums[4], sums[7]
         grad_qkv = jnp.concatenate([grad_query, sums[8]], axis=1)
     else:
         grad_key_value = jnp.concatenate([grad_key_value[0], grad_key_value[1]], axis=1)

time: 945 us -> 943 us (level)
  no operation moved by 1% of the time
where the time goes in v5:
time: 943 us; the launch traced here: 939 us
  Pallas kernels  614 us (65%)
  waiting for transfers between devices  120 us (13%)
  matrix products  96.1 us (10%)
  local copies, waits for them, and re-layouts  45.3 us (5%)
  other arithmetic  35.6 us (4%)
  starting transfers between devices  25.6 us (3%)
    pallas_call x2, Pallas kernels, gather_rows(): pl.pallas_call(functools.partial(gather_rows_kernel, dims, orders, held),...  171 us
    pallas_call x2, Pallas kernels, scatter_rows(): pl.pallas_call(kernel, out_shape=jax.ShapeDtypeStruct((count, feat), jnp....  152 us
    pallas_call x1, Pallas kernels, gather_dense(): pl.pallas_call(functools.partial(gather_dense_kernel, length, bits, count...  143 us
    pallas_call x1, Pallas kernels, sum_dense(): pl.pallas_call(functools.partial(sum_dense_kernel, length, bits, cuts, pl...  128 us
    ppermute x15, waiting for transfers between devices, exchange(): return lax.ppermute(values, axis, [(i, i ^ bit) for i in range(count)])  120 us
    dot_general x9, matrix products, batch_dot(): lax.dot_general(left, right, (((left_dim,), (right_dim,)), ((0,), (0,))),...  65.3 us
    dot_general x7, matrix products, dot(): lax.dot_general(left, right, (((left_dim,), (right_dim,)), ((), ())), pre...  30.6 us
    ppermute x15, starting transfers between devices, exchange(): return lax.ppermute(values, axis, [(i, i ^ bit) for i in range(count)])  25.6 us
  transfers between devices with their start and end apart: 15, of which 3 were waited for; matrix products, arithmetic and copies ran while one was open for 8% of the time, Pallas kernels for 37%

profile of v5, /device:TPU:0, one launch (start us, length us, event | category | flops | bytes accessed | tf_op | source)
XLA Modules:
  0.0 938.8 jit_solution(61775292307878159)
XLA Ops:
  4.4 1.6 pad_maximum_fusion.1.refs_2_
  6.0 1.7 fusion.29.refs_0_
  7.7 143.1 %gather_dense.1 = (bf16[4,2,2,2,48,2688]{5,4,3,2,1,0:T(8,128)(2,1)}, bf16[4,2,2,2,48,1536]{5,4,3,2,1,0:T(8,128)(2,1)}, bf16[4,2,2,2,48,2048]{5,4,3,2,1,0:T(8,128...) custom-call(bf16[48,2688]{1,0:T(8,128)(2,1)} %fusion.29.refs_0_, ...), custom_call_target="tpu_custom_call" | custom-call | bytes 68812800 | tf_op jit(solution)/shard_map/gather_dense/pallas_call | solution.py:299
  152.2 1.4 copy-done.3
  154.7 8.1 attend.1
  162.8 4.9 multiply_reduce_fusion.2
  167.7 1.6 multiply_convert_fusion.3.rows_ref
  169.4 2.8 constant_dynamic-slice_fusion.10
  172.2 7.3 collective-permute-start.5
  179.5 1.5 collective-permute-start.3
  180.9 1.2 constant_dynamic-slice_fusion.13
  183.1 3.5 collective-permute-start.1
  187.0 1.2 copy.115
  188.2 1.6 fusion.73
  190.8 2.3 copy.116
  194.3 4.6 fusion.38
  198.9 1.3 copy-done.22
  201.5 4.7 fusion.39
  207.0 117.5 %gather_rows.2 = bf16[2,2,2,2,2,64,1536]{6,5,4,3,2,1,0:T(8,128)(2,1)S(1)} custom-call(bf16[256,1536]{1,0:T(8,128)(2,1)S(1)} %multiply_convert_fusion.3.rows_ref, bf16[2,2,2,2,128,256]{5,4,3,2,1,0:T(8,128)(2,1)S(1)} %and_convert_fusion.pick_ref), custom_call_target="tpu_custom_call" | custom-call | flops 1610612736 | bytes 37748736 | tf_op jit(solution)/shard_map/gather_rows/pallas_call | solution.py:768
  324.6 2.7 copy-done
  327.5 1.4 dynamic-slice_dynamic-update-slice_fusion.1
  329.1 1.7 copy-done.1
  330.8 5.4 fusion.40
  336.3 1.8 constant_dynamic-update-slice_fusion.5
  338.1 1.2 constant_dynamic-update-slice_fusion.4
  339.3 1.2 constant_dynamic-update-slice_fusion.3
  340.5 5.5 multiply_convert_fusion.2
  346.1 26.8 %collective-permute-done.4 = bf16[2,128,1536]{2,1,0:T(8,128)(2,1)S(1)} collective-permute-done((bf16[2,128,1536]{2,1,0:T(8,128)(2,1)S(1)}, bf16[2,128,1536]{2,1,0:T(8,128)(2,1)S(1)}, u32[]{:S(2)}, u32[]{:S(2)}) %collective-permute-start.4) | collective-permute-done | bytes 786464 | tf_op jit(solution)/shard_map/ppermute | solution.py:27
  372.8 1.2 constant_dynamic-update-slice_fusion.2
  374.1 1.2 constant_dynamic-update-slice_fusion
  375.3 3.6 multiply_convert_fusion
  379.0 62.2 %scatter_rows.2 = f32[256,1536]{1,0:T(8,128)S(1)} custom-call(bf16[2,2,2,2,2,64,1536]{6,5,4,3,2,1,0:T(8,128)(2,1)S(1)} %bitcast.99, bf16[2,2,2,2,128,256]{5,4,3,2,1,0:T(8,128)(2,1)S(1)} %and_convert_fusion.pick_ref), custom_call_target="tpu_custom_call" | custom-call | flops 1610612736 | bytes 37748736 | tf_op jit(solution)/shard_map/scatter_rows/pallas_call | solution.py:882
  441.2 3.4 fusion.24
  444.6 2.1 fusion.22
  446.7 53.3 %gather_rows.3 = bf16[2,2,2,2,2,64,1536]{6,5,4,3,2,1,0:T(8,128)(2,1)S(1)} custom-call(bf16[256,1536]{1,0:T(8,128)(2,1)S(1)} %get-tuple-element.106.rows_ref.refs_6_, bf16[2,2,2,2,128,256]{5,4,3,2,1,0:T(8,128)(2,1)S(1)} %and_convert_fusion.pick_ref), custom_call_target="tpu_custom_call" | custom-call | flops 1610612736 | bytes 37748736 | tf_op jit(solution)/shard_map/gather_rows/pallas_call | solution.py:768
  500.0 3.9 fusion
  503.9 6.9 convolution_convert_fusion
  510.8 13.0 %multiply_convert_fusion.1 = (bf16[2,1024,512]{2,1,0:T(8,128)(2,1)}, bf16[2,1024,512]{2,1,0:T(8,128)(2,1)}) fusion(f32[2,1024,512]{2,1,0:T(8,128)} %copy-done.47, f32[2,1024,512]{2,1,0:T(8,128)} %get-tuple-element.138, bf16[2,1024,1536]{2,1,0:T(8,128)(2,1)} %fusion, bf16[2,512,1536]{2,1,0:T(8,128)(2,1)} %copy-done.18), kind=kOutput, calls=%fused_computation.10 | convolution fusion | flops 3235905536 | bytes 22020096 | tf_op jit(solution)/shard_map/dot_general | solution.py:47
  523.8 5.5 convolution_convert_fusion.2
  529.3 10.5 %fusion.41 = f32[2,1024,1536]{2,1,0:T(8,128)} fusion(bf16[2,1024,512]{2,1,0:T(8,128)(2,1)} %get-tuple-element.109, bf16[2,1536,512]{2,1,0:T(8,128)(2,1)} %get-tuple-element.64), kind=kOutput, calls=%fused_computation.129 | convolution fusion | flops 3221225472 | bytes 17825792 | tf_op jit(solution)/shard_map/dot_general | solution.py:47
  539.8 1.8 constant_dynamic-slice_fusion.1
  543.4 2.6 collective-permute-start.12
  546.0 5.3 convolution_convert_fusion.1
  551.3 1.8 constant_dynamic-slice_fusion.5
  553.1 1.8 constant_dynamic-slice_fusion.9
  556.0 9.6 %add_convert_fusion = bf16[2,1024,1536]{2,1,0:T(8,128)(2,1)S(1)} fusion(f32[2,1024,1536]{2,1,0:T(8,128)} %fusion.41, bf16[2,1024,512]{2,1,0:T(8,128)(2,1)} %get-tuple-element.108, bf16[2,1536,512]{2,1,0:T(8,128)(2,1)} %copy-done.10), kind=kOutput, calls=%fused_computation.2 | convolution fusion | flops 3227516928 | bytes 24117248 | tf_op jit(solution)/shard_map/dot_general | solution.py:47
  565.7 90.2 %scatter_rows.3 = f32[256,1536]{1,0:T(8,128)S(1)} custom-call(bf16[2,2,2,2,2,64,1536]{6,5,4,3,2,1,0:T(8,128)(2,1)S(1)} %bitcast.98, bf16[2,2,2,2,128,256]{5,4,3,2,1,0:T(8,128)(2,1)S(1)} %and_convert_fusion.pick_ref), custom_call_target="tpu_custom_call" | custom-call | flops 1610612736 | bytes 37748736 | tf_op jit(solution)/shard_map/scatter_rows/pallas_call | solution.py:882
  657.0 5.8 multiply_reduce_fusion
  662.7 3.4 fusion.35
  666.2 2.3 convolution_convert_fusion.3.grad
  670.4 11.5 %attend_back.1 = (bf16[256,1536]{1,0:T(8,128)(2,1)S(1)}, f32[2,768,512]{2,1,0:T(8,128)S(1)}) custom-call(bf16[256,1536]{1,0:T(8,128)(2,1)S(1)} %copy-done.6, bf16[768,1024]{1,0:T(8,128)(2,1)S(1)} %copy-done.4, bf16[768,1024]{1,0:T(8,128)(2,1)S(1)} %copy-done.4, s32[256,1]{1,0:T(8,128)S(1)} %copy.106.seg_rows, s32[1,768]{1,0:T(1,128)S(1)} %broadcast_in_dim.149.seg_keys, ...), custom_call_target="tpu_custom_call" | custom-call | flops 3019898880 | bytes 6291456 | tf_op jit(solution)/shard_map/attend_back/pallas_call | solution.py:1000
  681.9 1.7 copy-done.8
  684.5 128.0 %sum_dense.1 = (f32[48,1024]{1,0:T(8,128)}, f32[48,1024]{1,0:T(8,128)}, f32[48,1536]{1,0:T(8,128)}, f32[48,1536]{1,0:T(8,128)}, f32[32,1536]{1,0:T(8,128)}, /*in...) custom-call(bf16[1536,256]{1,0:T(8,128)(2,1)} %copy.117.refs_0_, ...), custom_call_target="tpu_custom_call" | custom-call | flops 5653921792 | bytes 44171264 | tf_op jit(solution)/shard_map/sum_dense/pallas_call | solution.py:655
  812.7 6.2 fusion.14
  819.2 1.2 slice_bitcast_fusion
  820.4 2.5 collective-permute-start.9
  824.5 2.9 collective-permute-start.6
  827.9 1.5 fusion.13
  829.4 46.6 %collective-permute-done.9 = bf16[2,384,512]{2,1,0:T(8,128)(2,1)S(1)} collective-permute-done((bf16[2,384,512]{2,1,0:T(8,128)(2,1)S(1)}, bf16[2,384,512]{2,1,0:T(8,128)(2,1)S(1)}, u32[]{:S(2)}, u32[]{:S(2)}) %collective-permute-start.9) | collective-permute-done | bytes 786464 | tf_op jit(solution)/shard_map/ppermute | solution.py:27
  876.0 47.1 %collective-permute-done.6 = bf16[2,384,512]{2,1,0:T(8,128)(2,1)S(1)} collective-permute-done((bf16[2,384,512]{2,1,0:T(8,128)(2,1)S(1)}, bf16[2,384,512]{2,1,0:T(8,128)(2,1)S(1)}, u32[]{:S(2)}, u32[]{:S(2)}) %collective-permute-start.6) | collective-permute-done | bytes 786464 | tf_op jit(solution)/shard_map/ppermute | solution.py:27
  923.1 2.1 convert_add_fusion.1
  925.2 2.1 bitcast_select_fusion
  927.3 1.9 convert_add_fusion.3
  929.8 4.0 bitcast_select_fusion.1
  (178 shorter events, 27.0 us)
Async XLA Ops:
  151.9 10.9 %copy-start.16 = (bf16[1,256,1536]{2,1,0:T(8,128)(2,1)S(1)}, bf16[1,256,1536]{2,1,0:T(8,128)(2,1)}, u32[]{:S(2)}) copy-start(bf16[1,256,1536]{2,1,0:T(8,128)(2,1)} %param.18) | copy-start | bytes 2359300
  152.2 1.4 copy-start.3
  169.3 11.6 %copy-start.13 = (bf16[4,384,512]{2,1,0:T(8,128)(2,1)S(1)}, bf16[4,384,512]{2,1,0:T(8,128)(2,1)}, u32[]{:S(2)}) copy-start(bf16[4,384,512]{2,1,0:T(8,128)(2,1)} %param.34) | copy-start | bytes 4718596
  169.4 17.2 %copy-start.43 = (f32[4,2,2,2,16,256]{5,4,3,2,1,0:T(8,128)S(1)}, f32[4,2,2,2,16,256]{5,4,3,2,1,0:T(8,128)}, u32[]{:S(2)}) copy-start(f32[4,2,2,2,16,256]{5,4,3,2,1,0:T(8,128)} %get-tuple-element.63) | copy-start | bytes 1572868
  172.2 173.9 %collective-permute-start.5 = (bf16[2,128,1536]{2,1,0:T(8,128)(2,1)}, bf16[2,128,1536]{2,1,0:T(8,128)(2,1)}, u32[]{:S(2)}, u32[]{:S(2)}) collective-permute-start(bf16[2,128,1536]{2,1,0:T(8,128)(2,1)} %get-tuple-element.126), channel_id=1, source_target_pairs={{0,24},{8,16},{16,8},{24,0},{1,25},{9,17},{17,9},{25,1},{2,26},{10... | collective-permute-start | bytes 2359304 | tf_op jit(solution)/shard_map/ppermute | solution.py:27
  179.5 193.4 %collective-permute-start.3 = (bf16[2,128,1536]{2,1,0:T(8,128)(2,1)}, bf16[2,128,1536]{2,1,0:T(8,128)(2,1)}, u32[]{:S(2)}, u32[]{:S(2)}) collective-permute-start(bf16[2,128,1536]{2,1,0:T(8,128)(2,1)} %get-tuple-element.126), channel_id=1, source_target_pairs={{0,8},{8,0},{16,24},{24,16},{1,9},{9,1},{17,25},{25,17},{2,10},{10... | collective-permute-start | bytes 2359304 | tf_op jit(solution)/shard_map/ppermute | solution.py:27
  182.2 154.0 %collective-permute-start.2 = (bf16[2,384,512]{2,1,0:T(8,128)(2,1)}, bf16[2,384,512]{2,1,0:T(8,128)(2,1)}, u32[]{:S(2)}, u32[]{:S(2)}) collective-permute-start(bf16[2,384,512]{2,1,0:T(8,128)(2,1)} %get-tuple-element.128), channel_id=1, source_target_pairs={{0,24},{8,16},{16,8},{24,0},{1,25},{9,17},{17,9},{25,1},{2,26},{10... | collective-permute-start | bytes 2359304 | tf_op jit(solution)/shard_map/ppermute | solution.py:27
  183.1 153.2 %collective-permute-start = (bf16[2,384,512]{2,1,0:T(8,128)(2,1)}, bf16[2,384,512]{2,1,0:T(8,128)(2,1)}, u32[]{:S(2)}, u32[]{:S(2)}) collective-permute-start(bf16[2,384,512]{2,1,0:T(8,128)(2,1)} %get-tuple-element.128), channel_id=1, source_target_pairs={{0,8},{8,0},{16,24},{24,16},{1,9},{9,1},{17,25},{25,17},{2,10},{10... | collective-permute-start | bytes 2359304 | tf_op jit(solution)/shard_map/ppermute | solution.py:27
  183.1 153.2 %collective-permute-start.1 = (bf16[2,384,512]{2,1,0:T(8,128)(2,1)}, bf16[2,384,512]{2,1,0:T(8,128)(2,1)}, u32[]{:S(2)}, u32[]{:S(2)}) collective-permute-start(bf16[2,384,512]{2,1,0:T(8,128)(2,1)} %get-tuple-element.127), channel_id=1, source_target_pairs={{0,16},{8,24},{16,0},{24,8},{1,17},{9,25},{17,1},{25,9},{2,18},{10... | collective-permute-start | bytes 2359304 | tf_op jit(solution)/shard_map/ppermute | solution.py:27
  186.6 3.3 copy-start.44
  198.9 1.3 copy-start.22
  324.5 2.7 copy-start
  327.3 1.8 copy-start.14
  327.5 3.3 copy-start.1
  330.8 5.4 copy-start.27
  336.2 9.9 %copy-start.47 = (f32[2,1024,512]{2,1,0:T(8,128)}, f32[2,1024,512]{2,1,0:T(8,128)S(1)}, u32[]{:S(2)}) copy-start(f32[2,1024,512]{2,1,0:T(8,128)S(1)} %fusion.40) | copy-start | bytes 12582916
  336.2 36.6 %collective-permute-start.4 = (bf16[2,128,1536]{2,1,0:T(8,128)(2,1)S(1)}, bf16[2,128,1536]{2,1,0:T(8,128)(2,1)S(1)}, u32[]{:S(2)}, u32[]{:S(2)}) collective-permute-start(bf16[2,128,1536]{2,1,0:T(8,128)(2,1)S(1)} %copy-done.27), channel_id=1, source_target_pairs={{0,16},{8,24},{16,0},{24,8},{1,17},{9,25},{17,1},{25,9},{2,18},{10... | collective-permute-start | bytes 2359304 | tf_op jit(solution)/shard_map/ppermute | solution.py:27
  340.5 5.5 copy-start.10
  346.1 32.9 %copy-start.48 = (bf16[2,1024,512]{2,1,0:T(8,128)(2,1)}, bf16[2,1024,512]{2,1,0:T(8,128)(2,1)S(1)}, u32[]{:S(2)}) copy-start(bf16[2,1024,512]{2,1,0:T(8,128)(2,1)S(1)} %get-tuple-element.137) | copy-start | bytes 6291460
  375.3 3.7 copy-start.18
  379.0 62.2 %copy-start.15 = (bf16[1,256,1536]{2,1,0:T(8,128)(2,1)S(1)}, bf16[1,256,1536]{2,1,0:T(8,128)(2,1)}, u32[]{:S(2)}) copy-start(bf16[1,256,1536]{2,1,0:T(8,128)(2,1)} %param.19) | copy-start | bytes 2359300
  379.0 62.2 %copy-start.24 = (f32[256,1536]{1,0:T(8,128)S(1)}, f32[256,1536]{1,0:T(8,128)}, u32[]{:S(2)}) copy-start(f32[256,1536]{1,0:T(8,128)} %fusion.39) | copy-start | bytes 4718596
  441.2 3.4 copy-start.23
  441.2 3.4 copy-start.46
  444.6 2.1 copy-start.2
  446.7 209.2 %copy-start.33 = (bf16[256,1024]{1,0:T(8,128)(2,1)}, bf16[256,1024]{1,0:T(8,128)(2,1)S(1)}, u32[]{:S(2)}) copy-start(bf16[256,1024]{1,0:T(8,128)(2,1)S(1)} %get-tuple-element.122) | copy-start | bytes 1572868
  541.6 278.9 %collective-permute-start.14 = (bf16[2,128,1536]{2,1,0:T(8,128)(2,1)}, bf16[2,128,1536]{2,1,0:T(8,128)(2,1)}, u32[]{:S(2)}, u32[]{:S(2)}) collective-permute-start(bf16[2,128,1536]{2,1,0:T(8,128)(2,1)} %get-tuple-element.111), channel_id=1, source_target_pairs={{0,24},{8,16},{16,8},{24,0},{1,25},{9,17},{17,9},{25,1},{2,26},{10... | collective-permute-start | bytes 2359304 | tf_op jit(solution)/shard_map/ppermute | solution.py:27
  542.7 280.3 %collective-permute-start.13 = (bf16[2,128,1536]{2,1,0:T(8,128)(2,1)}, bf16[2,128,1536]{2,1,0:T(8,128)(2,1)}, u32[]{:S(2)}, u32[]{:S(2)}) collective-permute-start(bf16[2,128,1536]{2,1,0:T(8,128)(2,1)} %get-tuple-element.112), channel_id=1, source_target_pairs={{0,8},{8,0},{16,24},{24,16},{1,9},{9,1},{17,25},{25,17},{2,10},{10... | collective-permute-start | bytes 2359304 | tf_op jit(solution)/shard_map/ppermute | solution.py:27
  543.4 280.5 %collective-permute-start.12 = (bf16[2,128,1536]{2,1,0:T(8,128)(2,1)}, bf16[2,128,1536]{2,1,0:T(8,128)(2,1)}, u32[]{:S(2)}, u32[]{:S(2)}) collective-permute-start(bf16[2,128,1536]{2,1,0:T(8,128)(2,1)} %get-tuple-element.113), channel_id=1, source_target_pairs={{0,16},{8,24},{16,0},{24,8},{1,17},{9,25},{17,1},{25,9},{2,18},{10... | collective-permute-start | bytes 2359304 | tf_op jit(solution)/shard_map/ppermute | solution.py:27
  554.9 269.6 %collective-permute-start.11 = (bf16[2,384,512]{2,1,0:T(8,128)(2,1)}, bf16[2,384,512]{2,1,0:T(8,128)(2,1)}, u32[]{:S(2)}, u32[]{:S(2)}) collective-permute-start(bf16[2,384,512]{2,1,0:T(8,128)(2,1)} %get-tuple-element.115), channel_id=1, source_target_pairs={{0,24},{8,16},{16,8},{24,0},{1,25},{9,17},{17,9},{25,1},{2,26},{10... | collective-permute-start | bytes 2359304 | tf_op jit(solution)/shard_map/ppermute | solution.py:27
  556.0 273.4 %collective-permute-start.10 = (bf16[2,384,512]{2,1,0:T(8,128)(2,1)}, bf16[2,384,512]{2,1,0:T(8,128)(2,1)}, u32[]{:S(2)}, u32[]{:S(2)}) collective-permute-start(bf16[2,384,512]{2,1,0:T(8,128)(2,1)} %get-tuple-element.116), channel_id=1, source_target_pairs={{0,8},{8,0},{16,24},{24,16},{1,9},{9,1},{17,25},{25,17},{2,10},{10... | collective-permute-start | bytes 2359304 | tf_op jit(solution)/shard_map/ppermute | solution.py:27
  565.6 90.2 %copy-start.34 = (bf16[256,1024]{1,0:T(8,128)(2,1)S(1)}, bf16[256,1024]{1,0:T(8,128)(2,1)}, u32[]{:S(2)}) copy-start(bf16[256,1024]{1,0:T(8,128)(2,1)} %get-tuple-element.123) | copy-start | bytes 1572868
  565.7 100.5 %slice-start = ((s8[4718592]{0:T(1024)(128)(4,1)}), s8[4194304]{0:T(1024)(128)(4,1)S(1)}, s32[]{:S(2)}) async-start(s8[4718592]{0:T(1024)(128)(4,1)} %bitcast.125), calls=%async_computation | async-start | bytes 8388608
  657.0 5.8 copy-start.12
  657.0 9.2 slice-start.1
  666.1 2.4 copy-start.26
  666.2 3.1 copy-start.4
  666.2 3.1 copy-start.6
  669.3 1.1 copy-start.7
  681.9 1.7 copy-start.8
  812.5 6.4 copy-start.35
  812.5 6.4 copy-start.36
  812.5 6.4 copy-start.41
  812.6 6.4 copy-start.42
  812.6 6.5 copy-start.25
  812.6 6.5 copy-start.32
  812.6 7.9 copy-start.30
  812.6 10.4 %copy-start.31 = (bf16[2,384,512]{2,1,0:T(8,128)(2,1)S(1)}, bf16[2,384,512]{2,1,0:T(8,128)(2,1)}, u32[]{:S(2)}) copy-start(bf16[2,384,512]{2,1,0:T(8,128)(2,1)} %get-tuple-element.119) | copy-start | bytes 2359300
  812.6 11.3 %copy-start.29 = (bf16[2,384,512]{2,1,0:T(8,128)(2,1)S(1)}, bf16[2,384,512]{2,1,0:T(8,128)(2,1)}, u32[]{:S(2)}) copy-start(bf16[2,384,512]{2,1,0:T(8,128)(2,1)} %get-tuple-element.120) | copy-start | bytes 2359300
  812.6 11.9 %copy-start.28 = (bf16[2,384,512]{2,1,0:T(8,128)(2,1)S(1)}, bf16[2,384,512]{2,1,0:T(8,128)(2,1)}, u32[]{:S(2)}) copy-start(bf16[2,384,512]{2,1,0:T(8,128)(2,1)} %get-tuple-element.121) | copy-start | bytes 2359300
  812.6 14.8 %copy-start.45 = (bf16[48]{0:T(256)(128)(2,1)S(1)}, bf16[48]{0:T(256)(128)(2,1)}, u32[]{:S(2)}) copy-start(bf16[48]{0:T(256)(128)(2,1)} %param.24) | copy-start | bytes 292
  812.6 15.3 %copy-start.11 = (f32[256,1536]{1,0:T(8,128)S(1)}, f32[256,1536]{1,0:T(8,128)}, u32[]{:S(2)}) copy-start(f32[256,1536]{1,0:T(8,128)} %get-tuple-element.105) | copy-start | bytes 4718596
  812.7 15.3 %copy-start.17 = (bf16[1,256,1536]{2,1,0:T(8,128)(2,1)S(1)}, bf16[1,256,1536]{2,1,0:T(8,128)(2,1)}, u32[]{:S(2)}) copy-start(bf16[1,256,1536]{2,1,0:T(8,128)(2,1)} %param.18) | copy-start | bytes 2359300
  820.4 55.6 %collective-permute-start.9 = (bf16[2,384,512]{2,1,0:T(8,128)(2,1)S(1)}, bf16[2,384,512]{2,1,0:T(8,128)(2,1)S(1)}, u32[]{:S(2)}, u32[]{:S(2)}) collective-permute-start(bf16[2,384,512]{2,1,0:T(8,128)(2,1)S(1)} %copy-done.30), channel_id=1, source_target_pairs={{0,16},{8,24},{16,0},{24,8},{1,17},{9,25},{17,1},{25,9},{2,18},{10... | collective-permute-start | bytes 2359304 | tf_op jit(solution)/shard_map/ppermute | solution.py:27
  823.0 53.1 %collective-permute-start.8 = (bf16[2,384,512]{2,1,0:T(8,128)(2,1)S(1)}, bf16[2,384,512]{2,1,0:T(8,128)(2,1)S(1)}, u32[]{:S(2)}, u32[]{:S(2)}) collective-permute-start(bf16[2,384,512]{2,1,0:T(8,128)(2,1)S(1)} %copy-done.31), channel_id=1, source_target_pairs={{0,24},{8,16},{16,8},{24,0},{1,25},{9,17},{17,9},{25,1},{2,26},{10... | collective-permute-start | bytes 2359304 | tf_op jit(solution)/shard_map/ppermute | solution.py:27
  823.9 52.1 %collective-permute-start.7 = (bf16[2,384,512]{2,1,0:T(8,128)(2,1)S(1)}, bf16[2,384,512]{2,1,0:T(8,128)(2,1)S(1)}, u32[]{:S(2)}, u32[]{:S(2)}) collective-permute-start(bf16[2,384,512]{2,1,0:T(8,128)(2,1)S(1)} %copy-done.29), channel_id=1, source_target_pairs={{0,8},{8,0},{16,24},{24,16},{1,9},{9,1},{17,25},{25,17},{2,10},{10... | collective-permute-start | bytes 2359304 | tf_op jit(solution)/shard_map/ppermute | solution.py:27
  824.5 98.6 %collective-permute-start.6 = (bf16[2,384,512]{2,1,0:T(8,128)(2,1)S(1)}, bf16[2,384,512]{2,1,0:T(8,128)(2,1)S(1)}, u32[]{:S(2)}, u32[]{:S(2)}) collective-permute-start(bf16[2,384,512]{2,1,0:T(8,128)(2,1)S(1)} %copy-done.28), channel_id=1, source_target_pairs={{0,16},{8,24},{16,0},{24,8},{1,17},{9,25},{17,1},{25,9},{2,18},{10... | collective-permute-start | bytes 2359304 | tf_op jit(solution)/shard_map/ppermute | solution.py:27
  827.9 95.2 %copy-start.19 = (bf16[2,128,1536]{2,1,0:T(8,128)(2,1)S(1)}, bf16[2,128,1536]{2,1,0:T(8,128)(2,1)}, u32[]{:S(2)}) copy-start(bf16[2,128,1536]{2,1,0:T(8,128)(2,1)} %get-tuple-element.94) | copy-start | bytes 2359300
  925.2 2.1 copy-start.21
  927.3 1.9 copy-start.20
  929.7 6.0 copy-start.37
  929.7 6.7 copy-start.40
  929.7 7.4 copy-start.39
  929.7 8.1 copy-start.38
  (2 other events, 2.1 us)

commit v6 on v5

--- a/solution.py
+++ b/solution.py
@@ -788,7 +788,7 @@
 
 
 def scatter_rows_kernel(
-    dims, orders, held, slots_ref, pick_ref, out_ref, mine, other, came_core, came_far, send_sems, recv_sems
+    dims, orders, held, base, slots_ref, pick_ref, out_ref, mine, other, came_core, came_far, send_sems, recv_sems
 ):
     own, partner = row_places(dims)
     greet(partner)
@@ -853,13 +853,13 @@
             )
     for piece in range(pieces):
         flying[piece].wait_recv()
-        out_ref[:, pl.ds(piece * width, width)] = mine[(piece, *own[:far])].astype(jnp.float32) + came_far[far - 1][piece].astype(
-            jnp.float32
-        )
+        columns = pl.ds(piece * width, width)
+        total = mine[(piece, *own[:far])].astype(jnp.float32) + came_far[far - 1][piece].astype(jnp.float32)
+        out_ref[:, columns] = total if base is None else base[:, columns] + total
     copies.finish()
 
 
-def scatter_rows(slots, pick_low, held, collective_id, light):
+def scatter_rows(slots, pick_low, held, collective_id, light, base=None):
     dims = row_dims()
     far = len(dims) - 1
     orders = row_orders(far, light)
@@ -873,16 +873,20 @@
     scratch = [pltpu.VMEM((len(orders),) + (2,) * far + (count, width), slots.dtype)] * 3
     scratch += [pltpu.VMEM((len(orders),) + (2,) * (far - 1 - s) + (count, width), slots.dtype) for s in range(far)]
 
-    def kernel(slots_ref, pick_ref, out_ref, mine, other, came_core, *rest):
+    extra = [] if base is None else [base]
+
+    def kernel(slots_ref, pick_ref, *refs):
+        base_ref, refs = (None, refs) if base is None else (refs[0], refs[1:])
+        out_ref, mine, other, came_core, *rest = refs
         came_far, sems = rest[:far], rest[far:]
         scatter_rows_kernel(
-            dims, orders, held, slots_ref, pick_ref, out_ref, mine, other, came_core, came_far, *sems
+            dims, orders, held, base_ref, slots_ref, pick_ref, out_ref, mine, other, came_core, came_far, *sems
         )
 
     return pl.pallas_call(
         kernel,
         out_shape=jax.ShapeDtypeStruct((count, feat), jnp.float32),
-        in_specs=[pl.BlockSpec(memory_space=pltpu.VMEM)] * 2,
+        in_specs=[pl.BlockSpec(memory_space=pltpu.VMEM)] * (2 + len(extra)),
         out_specs=pl.BlockSpec(memory_space=pltpu.VMEM),
         scratch_shapes=scratch + [pltpu.SemaphoreType.DMA((number,)), pltpu.SemaphoreType.DMA((number,))],
         compiler_params=pltpu.CompilerParams(
@@ -896,7 +900,7 @@
             transcendentals=0,
         ),
         name="scatter_rows",
-    )(slots.reshape((held,) + lead + (capacity, feat)), pick_low.reshape(lead + pick_low.shape[1:]))
+    )(slots.reshape((held,) + lead + (capacity, feat)), pick_low.reshape(lead + pick_low.shape[1:]), *extra)
 
 
 def allowed_keys(seg_rows_ref, seg_keys_ref, back_rows):
@@ -1192,11 +1196,12 @@
     grad_input = (
         batch_dot(grad_gate_rows, expert_gate_full, 2, 2) + batch_dot(grad_up_rows, expert_up_full, 2, 2)
     ).astype(BF16)
-    grad_routed = scatter_rows(grad_input, chosen_low, num_held, 4, True)
     grad_shidden = dot(grad_low, down_full, 1, 1)
     grad_sgate_rows, grad_sup_rows = swiglu_backward(shared_gate, shared_up, grad_shidden)
     grad_gate_up = jnp.concatenate([grad_sgate_rows, grad_sup_rows], axis=1)
-    grad_normed_two = dot(grad_gate_up, gate_up_full, 1, 1) + grad_routed
+    grad_shared = dot(grad_gate_up, gate_up_full, 1, 1)
+    grad_routed = scatter_rows(grad_input, chosen_low, num_held, 4, True, grad_shared)
+    grad_normed_two = grad_routed
     _, pull_two = jax.vjp(rms_norm, mixed_rows, gain_two)
     grad_mixed_norm, grad_gain_two = pull_two(grad_normed_two)
     grad_mixed = grad_out + grad_mixed_norm

time: 943 us -> 942 us (level)
    unnamed x111 -> x113, local copies, waits for them, and re-layouts: 17.9 us -> 20.4 us
where the time goes in v6:
time: 942 us; the launch traced here: 938 us
  Pallas kernels  614 us (65%)
  waiting for transfers between devices  120 us (13%)
  matrix products  91.6 us (10%)
  local copies, waits for them, and re-layouts  46.4 us (5%)
  other arithmetic  38 us (4%)
  starting transfers between devices  25.5 us (3%)
    pallas_call x2, Pallas kernels, gather_rows(): pl.pallas_call(functools.partial(gather_rows_kernel, dims, orders, held),...  171 us
    pallas_call x2, Pallas kernels, scatter_rows(): pl.pallas_call(kernel, out_shape=jax.ShapeDtypeStruct((count, feat), jnp....  152 us
    pallas_call x1, Pallas kernels, gather_dense(): pl.pallas_call(functools.partial(gather_dense_kernel, length, bits, count...  143 us
    pallas_call x1, Pallas kernels, sum_dense(): pl.pallas_call(functools.partial(sum_dense_kernel, length, bits, cuts, pl...  128 us
    ppermute x15, waiting for transfers between devices, exchange(): return lax.ppermute(values, axis, [(i, i ^ bit) for i in range(count)])  120 us
    dot_general x9, matrix products, batch_dot(): lax.dot_general(left, right, (((left_dim,), (right_dim,)), ((0,), (0,))),...  65.4 us
    dot_general x7, matrix products, dot(): lax.dot_general(left, right, (((left_dim,), (right_dim,)), ((), ())), pre...  26 us
    ppermute x15, starting transfers between devices, exchange(): return lax.ppermute(values, axis, [(i, i ^ bit) for i in range(count)])  25.5 us
  transfers between devices with their start and end apart: 15, of which 3 were waited for; matrix products, arithmetic and copies ran while one was open for 8% of the time, Pallas kernels for 37%

profile of v6, /device:TPU:0, one launch (start us, length us, event | category | flops | bytes accessed | tf_op | source)
XLA Modules:
  0.0 938.2 jit_solution(6451545398222092999)
XLA Ops:
  4.4 1.6 pad_maximum_fusion.1.refs_2_
  6.0 1.7 fusion.29.refs_0_
  7.7 143.2 %gather_dense.1 = (bf16[4,2,2,2,48,2688]{5,4,3,2,1,0:T(8,128)(2,1)}, bf16[4,2,2,2,48,1536]{5,4,3,2,1,0:T(8,128)(2,1)}, bf16[4,2,2,2,48,2048]{5,4,3,2,1,0:T(8,128...) custom-call(bf16[48,2688]{1,0:T(8,128)(2,1)} %fusion.29.refs_0_, ...), custom_call_target="tpu_custom_call" | custom-call | bytes 68812800 | tf_op jit(solution)/shard_map/gather_dense/pallas_call | solution.py:299
  152.3 1.4 copy-done.3
  154.8 8.1 attend.1
  162.9 5.1 multiply_reduce_fusion.2
  168.0 1.6 multiply_convert_fusion.3.rows_ref
  169.6 2.8 constant_dynamic-slice_fusion.10
  172.4 7.3 collective-permute-start.5
  179.7 1.5 collective-permute-start.3
  181.2 1.2 constant_dynamic-slice_fusion.13
  183.3 3.5 collective-permute-start.1
  187.2 1.2 copy.115
  188.4 1.6 fusion.74
  191.1 2.3 copy.116
  194.5 4.6 fusion.39
  199.1 1.3 copy-done.23
  201.8 4.7 fusion.40
  207.3 117.5 %gather_rows.2 = bf16[2,2,2,2,2,64,1536]{6,5,4,3,2,1,0:T(8,128)(2,1)S(1)} custom-call(bf16[256,1536]{1,0:T(8,128)(2,1)S(1)} %multiply_convert_fusion.3.rows_ref, bf16[2,2,2,2,128,256]{5,4,3,2,1,0:T(8,128)(2,1)S(1)} %and_convert_fusion.pick_ref), custom_call_target="tpu_custom_call" | custom-call | flops 1610612736 | bytes 37748736 | tf_op jit(solution)/shard_map/gather_rows/pallas_call | solution.py:768
  324.8 2.7 copy-done
  327.7 1.2 copy-done.14
  329.4 2.4 copy-done.1
  331.8 5.4 fusion.41
  337.3 1.8 constant_dynamic-update-slice_fusion.5
  339.1 1.2 constant_dynamic-update-slice_fusion.4
  340.3 1.2 constant_dynamic-update-slice_fusion.3
  341.5 5.7 multiply_convert_fusion.2
  347.2 26.6 %collective-permute-done.4 = bf16[2,128,1536]{2,1,0:T(8,128)(2,1)S(1)} collective-permute-done((bf16[2,128,1536]{2,1,0:T(8,128)(2,1)S(1)}, bf16[2,128,1536]{2,1,0:T(8,128)(2,1)S(1)}, u32[]{:S(2)}, u32[]{:S(2)}) %collective-permute-start.4) | collective-permute-done | bytes 786464 | tf_op jit(solution)/shard_map/ppermute | solution.py:27
  375.1 1.2 constant_dynamic-update-slice_fusion
  376.3 3.6 multiply_convert_fusion
  380.0 62.2 %scatter_rows.2 = f32[256,1536]{1,0:T(8,128)S(1)} custom-call(bf16[2,2,2,2,2,64,1536]{6,5,4,3,2,1,0:T(8,128)(2,1)S(1)} %bitcast.99, bf16[2,2,2,2,128,256]{5,4,3,2,1,0:T(8,128)(2,1)S(1)} %and_convert_fusion.pick_ref), custom_call_target="tpu_custom_call" | custom-call | flops 1610612736 | bytes 37748736 | tf_op jit(solution)/shard_map/scatter_rows/pallas_call | solution.py:886
  442.2 3.3 fusion.24
  445.5 1.3 fusion.22
  447.4 1.8 fusion.35.refs_0_
  450.3 53.3 %gather_rows.3 = bf16[2,2,2,2,2,64,1536]{6,5,4,3,2,1,0:T(8,128)(2,1)S(1)} custom-call(bf16[256,1536]{1,0:T(8,128)(2,1)S(1)} %get-tuple-element.106.rows_ref.refs_6_, bf16[2,2,2,2,128,256]{5,4,3,2,1,0:T(8,128)(2,1)S(1)} %and_convert_fusion.pick_ref), custom_call_target="tpu_custom_call" | custom-call | flops 1610612736 | bytes 37748736 | tf_op jit(solution)/shard_map/gather_rows/pallas_call | solution.py:768
  503.7 3.9 fusion
  507.6 6.9 convolution_convert_fusion
  514.5 12.9 %multiply_convert_fusion.1 = (bf16[2,1024,512]{2,1,0:T(8,128)(2,1)}, bf16[2,1024,512]{2,1,0:T(8,128)(2,1)}) fusion(f32[2,1024,512]{2,1,0:T(8,128)} %copy-done.46, f32[2,1024,512]{2,1,0:T(8,128)} %get-tuple-element.138, bf16[2,1024,1536]{2,1,0:T(8,128)(2,1)} %fusion, bf16[2,512,1536]{2,1,0:T(8,128)(2,1)} %copy-done.19), kind=kOutput, calls=%fused_computation.10 | convolution fusion | flops 3235905536 | bytes 22020096 | tf_op jit(solution)/shard_map/dot_general | solution.py:47
  527.4 5.5 convolution_convert_fusion.2
  532.9 10.5 %fusion.42 = f32[2,1024,1536]{2,1,0:T(8,128)} fusion(bf16[2,1024,512]{2,1,0:T(8,128)(2,1)} %get-tuple-element.109, bf16[2,1536,512]{2,1,0:T(8,128)(2,1)} %get-tuple-element.64), kind=kOutput, calls=%fused_computation.129 | convolution fusion | flops 3221225472 | bytes 17825792 | tf_op jit(solution)/shard_map/dot_general | solution.py:47
  543.4 1.7 constant_dynamic-slice_fusion.1
  546.9 2.6 collective-permute-start.12
  549.5 5.3 convolution_convert_fusion.1
  554.9 1.8 constant_dynamic-slice_fusion.5
  556.7 1.7 constant_dynamic-slice_fusion.9
  559.5 9.6 %add_convert_fusion = bf16[2,1024,1536]{2,1,0:T(8,128)(2,1)S(1)} fusion(f32[2,1024,1536]{2,1,0:T(8,128)} %fusion.42, bf16[2,1024,512]{2,1,0:T(8,128)(2,1)} %get-tuple-element.108, bf16[2,1536,512]{2,1,0:T(8,128)(2,1)} %copy-done.10), kind=kOutput, calls=%fused_computation.2 | convolution fusion | flops 3227516928 | bytes 24117248 | tf_op jit(solution)/shard_map/dot_general | solution.py:47
  569.2 90.3 %scatter_rows.3 = f32[256,1536]{1,0:T(8,128)S(1)} custom-call(bf16[2,2,2,2,2,64,1536]{6,5,4,3,2,1,0:T(8,128)(2,1)S(1)} %bitcast.98, bf16[2,2,2,2,128,256]{5,4,3,2,1,0:T(8,128)(2,1)S(1)} %and_convert_fusion.pick_ref, f32[256,1536]{1,0:T(8,128)S(1)} %fusion.35.refs_0_), custom_call_target="tpu_custom_call" | custom-call | flops 1610612736 | bytes 37748736 | tf_op jit(solution)/shard_map/scatter_rows/pallas_call | solution.py:886
  659.5 2.0 multiply_reduce_fusion
  661.6 3.7 fusion.36
  665.3 2.3 convolution_convert_fusion.3.grad
  669.5 11.7 %attend_back.1 = (bf16[256,1536]{1,0:T(8,128)(2,1)S(1)}, f32[2,768,512]{2,1,0:T(8,128)S(1)}) custom-call(bf16[256,1536]{1,0:T(8,128)(2,1)S(1)} %copy-done.6, bf16[768,1024]{1,0:T(8,128)(2,1)S(1)} %copy-done.4, bf16[768,1024]{1,0:T(8,128)(2,1)S(1)} %copy-done.4, s32[256,1]{1,0:T(8,128)S(1)} %copy.106.seg_rows, s32[1,768]{1,0:T(1,128)S(1)} %broadcast_in_dim.149.seg_keys, ...), custom_call_target="tpu_custom_call" | custom-call | flops 3019898880 | bytes 6291456 | tf_op jit(solution)/shard_map/attend_back/pallas_call | solution.py:1004
  681.2 1.7 copy-done.8
  683.8 128.3 %sum_dense.1 = (f32[48,1024]{1,0:T(8,128)}, f32[48,1024]{1,0:T(8,128)}, f32[48,1536]{1,0:T(8,128)}, f32[48,1536]{1,0:T(8,128)}, f32[32,1536]{1,0:T(8,128)}, /*in...) custom-call(bf16[1536,256]{1,0:T(8,128)(2,1)} %copy.117.refs_0_, ...), custom_call_target="tpu_custom_call" | custom-call | flops 5653921792 | bytes 44171264 | tf_op jit(solution)/shard_map/sum_dense/pallas_call | solution.py:655
  812.2 6.2 fusion.14
  818.8 1.2 slice_bitcast_fusion
  820.0 2.4 collective-permute-start.9
  823.9 2.9 collective-permute-start.6
  827.3 1.5 fusion.13
  828.9 46.6 %collective-permute-done.9 = bf16[2,384,512]{2,1,0:T(8,128)(2,1)S(1)} collective-permute-done((bf16[2,384,512]{2,1,0:T(8,128)(2,1)S(1)}, bf16[2,384,512]{2,1,0:T(8,128)(2,1)S(1)}, u32[]{:S(2)}, u32[]{:S(2)}) %collective-permute-start.9) | collective-permute-done | bytes 786464 | tf_op jit(solution)/shard_map/ppermute | solution.py:27
  875.5 47.1 %collective-permute-done.6 = bf16[2,384,512]{2,1,0:T(8,128)(2,1)S(1)} collective-permute-done((bf16[2,384,512]{2,1,0:T(8,128)(2,1)S(1)}, bf16[2,384,512]{2,1,0:T(8,128)(2,1)S(1)}, u32[]{:S(2)}, u32[]{:S(2)}) %collective-permute-start.6) | collective-permute-done | bytes 786464 | tf_op jit(solution)/shard_map/ppermute | solution.py:27
  922.6 2.1 convert_add_fusion.1
  924.6 2.1 bitcast_select_fusion
  926.7 1.9 convert_add_fusion.3
  929.2 4.0 bitcast_select_fusion.1
  (182 shorter events, 28.9 us)
Async XLA Ops:
  152.3 1.4 copy-start.3
  169.6 11.6 %copy-start.13 = (bf16[4,384,512]{2,1,0:T(8,128)(2,1)S(1)}, bf16[4,384,512]{2,1,0:T(8,128)(2,1)}, u32[]{:S(2)}) copy-start(bf16[4,384,512]{2,1,0:T(8,128)(2,1)} %param.34) | copy-start | bytes 4718596
  169.6 17.2 %copy-start.42 = (f32[4,2,2,2,16,256]{5,4,3,2,1,0:T(8,128)S(1)}, f32[4,2,2,2,16,256]{5,4,3,2,1,0:T(8,128)}, u32[]{:S(2)}) copy-start(f32[4,2,2,2,16,256]{5,4,3,2,1,0:T(8,128)} %get-tuple-element.63) | copy-start | bytes 1572868
  172.4 174.8 %collective-permute-start.5 = (bf16[2,128,1536]{2,1,0:T(8,128)(2,1)}, bf16[2,128,1536]{2,1,0:T(8,128)(2,1)}, u32[]{:S(2)}, u32[]{:S(2)}) collective-permute-start(bf16[2,128,1536]{2,1,0:T(8,128)(2,1)} %get-tuple-element.126), channel_id=1, source_target_pairs={{0,24},{8,16},{16,8},{24,0},{1,25},{9,17},{17,9},{25,1},{2,26},{10... | collective-permute-start | bytes 2359304 | tf_op jit(solution)/shard_map/ppermute | solution.py:27
  179.7 194.1 %collective-permute-start.3 = (bf16[2,128,1536]{2,1,0:T(8,128)(2,1)}, bf16[2,128,1536]{2,1,0:T(8,128)(2,1)}, u32[]{:S(2)}, u32[]{:S(2)}) collective-permute-start(bf16[2,128,1536]{2,1,0:T(8,128)(2,1)} %get-tuple-element.126), channel_id=1, source_target_pairs={{0,8},{8,0},{16,24},{24,16},{1,9},{9,1},{17,25},{25,17},{2,10},{10... | collective-permute-start | bytes 2359304 | tf_op jit(solution)/shard_map/ppermute | solution.py:27
  182.4 7.8 copy-start.43
  182.4 154.8 %collective-permute-start.2 = (bf16[2,384,512]{2,1,0:T(8,128)(2,1)}, bf16[2,384,512]{2,1,0:T(8,128)(2,1)}, u32[]{:S(2)}, u32[]{:S(2)}) collective-permute-start(bf16[2,384,512]{2,1,0:T(8,128)(2,1)} %get-tuple-element.128), channel_id=1, source_target_pairs={{0,24},{8,16},{16,8},{24,0},{1,25},{9,17},{17,9},{25,1},{2,26},{10... | collective-permute-start | bytes 2359304 | tf_op jit(solution)/shard_map/ppermute | solution.py:27
  183.3 154.0 %collective-permute-start = (bf16[2,384,512]{2,1,0:T(8,128)(2,1)}, bf16[2,384,512]{2,1,0:T(8,128)(2,1)}, u32[]{:S(2)}, u32[]{:S(2)}) collective-permute-start(bf16[2,384,512]{2,1,0:T(8,128)(2,1)} %get-tuple-element.128), channel_id=1, source_target_pairs={{0,8},{8,0},{16,24},{24,16},{1,9},{9,1},{17,25},{25,17},{2,10},{10... | collective-permute-start | bytes 2359304 | tf_op jit(solution)/shard_map/ppermute | solution.py:27
  183.3 153.9 %collective-permute-start.1 = (bf16[2,384,512]{2,1,0:T(8,128)(2,1)}, bf16[2,384,512]{2,1,0:T(8,128)(2,1)}, u32[]{:S(2)}, u32[]{:S(2)}) collective-permute-start(bf16[2,384,512]{2,1,0:T(8,128)(2,1)} %get-tuple-element.127), channel_id=1, source_target_pairs={{0,16},{8,24},{16,0},{24,8},{1,17},{9,25},{17,1},{25,9},{2,18},{10... | collective-permute-start | bytes 2359304 | tf_op jit(solution)/shard_map/ppermute | solution.py:27
  199.1 1.3 copy-start.23
  324.8 2.7 copy-start
  327.5 1.4 copy-start.14
  327.5 1.9 copy-start.15
  328.9 2.9 copy-start.1
  331.8 5.4 copy-start.28
  337.1 10.0 %copy-start.46 = (f32[2,1024,512]{2,1,0:T(8,128)}, f32[2,1024,512]{2,1,0:T(8,128)S(1)}, u32[]{:S(2)}) copy-start(f32[2,1024,512]{2,1,0:T(8,128)S(1)} %fusion.41) | copy-start | bytes 12582916
  337.2 36.6 %collective-permute-start.4 = (bf16[2,128,1536]{2,1,0:T(8,128)(2,1)S(1)}, bf16[2,128,1536]{2,1,0:T(8,128)(2,1)S(1)}, u32[]{:S(2)}, u32[]{:S(2)}) collective-permute-start(bf16[2,128,1536]{2,1,0:T(8,128)(2,1)S(1)} %copy-done.28), channel_id=1, source_target_pairs={{0,16},{8,24},{16,0},{24,8},{1,17},{9,25},{17,1},{25,9},{2,18},{10... | collective-permute-start | bytes 2359304 | tf_op jit(solution)/shard_map/ppermute | solution.py:27
  341.5 5.7 copy-start.10
  347.2 32.7 %copy-start.47 = (bf16[2,1024,512]{2,1,0:T(8,128)(2,1)}, bf16[2,1024,512]{2,1,0:T(8,128)(2,1)S(1)}, u32[]{:S(2)}) copy-start(bf16[2,1024,512]{2,1,0:T(8,128)(2,1)S(1)} %get-tuple-element.137) | copy-start | bytes 6291460
  376.3 3.7 copy-start.19
  379.9 62.2 %copy-start.16 = (bf16[1,256,1536]{2,1,0:T(8,128)(2,1)S(1)}, bf16[1,256,1536]{2,1,0:T(8,128)(2,1)}, u32[]{:S(2)}) copy-start(bf16[1,256,1536]{2,1,0:T(8,128)(2,1)} %param.19) | copy-start | bytes 2359300
  379.9 62.2 %copy-start.25 = (f32[256,1536]{1,0:T(8,128)S(1)}, f32[256,1536]{1,0:T(8,128)}, u32[]{:S(2)}) copy-start(f32[256,1536]{1,0:T(8,128)} %fusion.40) | copy-start | bytes 4718596
  379.9 65.6 %copy-start.45 = (bf16[4,2,2,2,32,1536]{5,4,3,2,1,0:T(8,128)(2,1)S(1)}, bf16[4,2,2,2,32,1536]{5,4,3,2,1,0:T(8,128)(2,1)}, u32[]{:S(2)}) copy-start(bf16[4,2,2,2,32,1536]{5,4,3,2,1,0:T(8,128)(2,1)} %get-tuple-element.62) | copy-start | bytes 9437188
  442.2 3.4 copy-start.24
  442.2 4.7 slice-start
  445.5 4.8 copy-start.2
  445.5 1.9 slice-start.1
  545.1 274.8 %collective-permute-start.14 = (bf16[2,128,1536]{2,1,0:T(8,128)(2,1)}, bf16[2,128,1536]{2,1,0:T(8,128)(2,1)}, u32[]{:S(2)}, u32[]{:S(2)}) collective-permute-start(bf16[2,128,1536]{2,1,0:T(8,128)(2,1)} %get-tuple-element.111), channel_id=1, source_target_pairs={{0,24},{8,16},{16,8},{24,0},{1,25},{9,17},{17,9},{25,1},{2,26},{10... | collective-permute-start | bytes 2359304 | tf_op jit(solution)/shard_map/ppermute | solution.py:27
  546.3 276.1 %collective-permute-start.13 = (bf16[2,128,1536]{2,1,0:T(8,128)(2,1)}, bf16[2,128,1536]{2,1,0:T(8,128)(2,1)}, u32[]{:S(2)}, u32[]{:S(2)}) collective-permute-start(bf16[2,128,1536]{2,1,0:T(8,128)(2,1)} %get-tuple-element.112), channel_id=1, source_target_pairs={{0,8},{8,0},{16,24},{24,16},{1,9},{9,1},{17,25},{25,17},{2,10},{10... | collective-permute-start | bytes 2359304 | tf_op jit(solution)/shard_map/ppermute | solution.py:27
  546.9 276.4 %collective-permute-start.12 = (bf16[2,128,1536]{2,1,0:T(8,128)(2,1)}, bf16[2,128,1536]{2,1,0:T(8,128)(2,1)}, u32[]{:S(2)}, u32[]{:S(2)}) collective-permute-start(bf16[2,128,1536]{2,1,0:T(8,128)(2,1)} %get-tuple-element.113), channel_id=1, source_target_pairs={{0,16},{8,24},{16,0},{24,8},{1,17},{9,25},{17,1},{25,9},{2,18},{10... | collective-permute-start | bytes 2359304 | tf_op jit(solution)/shard_map/ppermute | solution.py:27
  558.4 265.5 %collective-permute-start.11 = (bf16[2,384,512]{2,1,0:T(8,128)(2,1)}, bf16[2,384,512]{2,1,0:T(8,128)(2,1)}, u32[]{:S(2)}, u32[]{:S(2)}) collective-permute-start(bf16[2,384,512]{2,1,0:T(8,128)(2,1)} %get-tuple-element.115), channel_id=1, source_target_pairs={{0,24},{8,16},{16,8},{24,0},{1,25},{9,17},{17,9},{25,1},{2,26},{10... | collective-permute-start | bytes 2359304 | tf_op jit(solution)/shard_map/ppermute | solution.py:27
  559.5 269.3 %collective-permute-start.10 = (bf16[2,384,512]{2,1,0:T(8,128)(2,1)}, bf16[2,384,512]{2,1,0:T(8,128)(2,1)}, u32[]{:S(2)}, u32[]{:S(2)}) collective-permute-start(bf16[2,384,512]{2,1,0:T(8,128)(2,1)} %get-tuple-element.116), channel_id=1, source_target_pairs={{0,8},{8,0},{16,24},{24,16},{1,9},{9,1},{17,25},{25,17},{2,10},{10... | collective-permute-start | bytes 2359304 | tf_op jit(solution)/shard_map/ppermute | solution.py:27
  569.2 96.1 %slice-start.2 = ((s8[4718592]{0:T(1024)(128)(4,1)}), s8[524288]{0:T(1024)(128)(4,1)S(1)}, s32[]{:S(2)}) async-start(s8[4718592]{0:T(1024)(128)(4,1)} %bitcast.127), calls=%async_computation.2 | async-start | bytes 1048576
  659.5 2.1 copy-start.12
  659.5 2.1 copy-start.17
  659.5 5.8 slice-start.3
  665.3 2.3 copy-start.27
  665.3 3.1 copy-start.4
  665.3 3.1 copy-start.6
  681.2 1.7 copy-start.8
  812.1 6.4 copy-start.34
  812.1 6.4 copy-start.35
  812.1 6.4 copy-start.40
  812.1 6.4 copy-start.41
  812.1 6.5 copy-start.26
  812.1 6.5 copy-start.33
  812.1 7.9 copy-start.31
  812.1 10.3 %copy-start.32 = (bf16[2,384,512]{2,1,0:T(8,128)(2,1)S(1)}, bf16[2,384,512]{2,1,0:T(8,128)(2,1)}, u32[]{:S(2)}) copy-start(bf16[2,384,512]{2,1,0:T(8,128)(2,1)} %get-tuple-element.119) | copy-start | bytes 2359300
  812.2 11.2 %copy-start.30 = (bf16[2,384,512]{2,1,0:T(8,128)(2,1)S(1)}, bf16[2,384,512]{2,1,0:T(8,128)(2,1)}, u32[]{:S(2)}) copy-start(bf16[2,384,512]{2,1,0:T(8,128)(2,1)} %get-tuple-element.120) | copy-start | bytes 2359300
  812.2 11.8 %copy-start.29 = (bf16[2,384,512]{2,1,0:T(8,128)(2,1)S(1)}, bf16[2,384,512]{2,1,0:T(8,128)(2,1)}, u32[]{:S(2)}) copy-start(bf16[2,384,512]{2,1,0:T(8,128)(2,1)} %get-tuple-element.121) | copy-start | bytes 2359300
  812.2 14.6 %copy-start.44 = (bf16[48]{0:T(256)(128)(2,1)S(1)}, bf16[48]{0:T(256)(128)(2,1)}, u32[]{:S(2)}) copy-start(bf16[48]{0:T(256)(128)(2,1)} %param.24) | copy-start | bytes 292
  812.2 15.2 %copy-start.11 = (f32[256,1536]{1,0:T(8,128)S(1)}, f32[256,1536]{1,0:T(8,128)}, u32[]{:S(2)}) copy-start(f32[256,1536]{1,0:T(8,128)} %get-tuple-element.105) | copy-start | bytes 4718596
  812.2 15.1 %copy-start.18 = (bf16[1,256,1536]{2,1,0:T(8,128)(2,1)S(1)}, bf16[1,256,1536]{2,1,0:T(8,128)(2,1)}, u32[]{:S(2)}) copy-start(bf16[1,256,1536]{2,1,0:T(8,128)(2,1)} %param.18) | copy-start | bytes 2359300
  818.4 104.1 %copy-start.20 = (bf16[2,128,1536]{2,1,0:T(8,128)(2,1)S(1)}, bf16[2,128,1536]{2,1,0:T(8,128)(2,1)}, u32[]{:S(2)}) copy-start(bf16[2,128,1536]{2,1,0:T(8,128)(2,1)} %get-tuple-element.94) | copy-start | bytes 2359300
  820.0 55.5 %collective-permute-start.9 = (bf16[2,384,512]{2,1,0:T(8,128)(2,1)S(1)}, bf16[2,384,512]{2,1,0:T(8,128)(2,1)S(1)}, u32[]{:S(2)}, u32[]{:S(2)}) collective-permute-start(bf16[2,384,512]{2,1,0:T(8,128)(2,1)S(1)} %copy-done.31), channel_id=1, source_target_pairs={{0,16},{8,24},{16,0},{24,8},{1,17},{9,25},{17,1},{25,9},{2,18},{10... | collective-permute-start | bytes 2359304 | tf_op jit(solution)/shard_map/ppermute | solution.py:27
  822.4 53.1 %collective-permute-start.8 = (bf16[2,384,512]{2,1,0:T(8,128)(2,1)S(1)}, bf16[2,384,512]{2,1,0:T(8,128)(2,1)S(1)}, u32[]{:S(2)}, u32[]{:S(2)}) collective-permute-start(bf16[2,384,512]{2,1,0:T(8,128)(2,1)S(1)} %copy-done.32), channel_id=1, source_target_pairs={{0,24},{8,16},{16,8},{24,0},{1,25},{9,17},{17,9},{25,1},{2,26},{10... | collective-permute-start | bytes 2359304 | tf_op jit(solution)/shard_map/ppermute | solution.py:27
  823.4 52.1 %collective-permute-start.7 = (bf16[2,384,512]{2,1,0:T(8,128)(2,1)S(1)}, bf16[2,384,512]{2,1,0:T(8,128)(2,1)S(1)}, u32[]{:S(2)}, u32[]{:S(2)}) collective-permute-start(bf16[2,384,512]{2,1,0:T(8,128)(2,1)S(1)} %copy-done.30), channel_id=1, source_target_pairs={{0,8},{8,0},{16,24},{24,16},{1,9},{9,1},{17,25},{25,17},{2,10},{10... | collective-permute-start | bytes 2359304 | tf_op jit(solution)/shard_map/ppermute | solution.py:27
  823.9 98.6 %collective-permute-start.6 = (bf16[2,384,512]{2,1,0:T(8,128)(2,1)S(1)}, bf16[2,384,512]{2,1,0:T(8,128)(2,1)S(1)}, u32[]{:S(2)}, u32[]{:S(2)}) collective-permute-start(bf16[2,384,512]{2,1,0:T(8,128)(2,1)S(1)} %copy-done.29), channel_id=1, source_target_pairs={{0,16},{8,24},{16,0},{24,8},{1,17},{9,25},{17,1},{25,9},{2,18},{10... | collective-permute-start | bytes 2359304 | tf_op jit(solution)/shard_map/ppermute | solution.py:27
  924.6 2.1 copy-start.22
  926.7 1.9 copy-start.21
  929.2 6.0 copy-start.36
  929.2 6.7 copy-start.39
  929.2 7.4 copy-start.38
  929.2 8.1 copy-start.37
  (3 other events, 3.1 us)
